TPU v7x, 32 devices: a whole 2x2x4 slice. The times are simulated.
32 devices in a mesh: section: 2 (over core), shard: 2 (over x), replica: 8 (over z, y).
Axes of the slice: x: 2, y: 2, z: 4, core: 2. Of those that a mesh axis runs over, the one named last changes fastest.
Arguments:
- inputs: bfloat16 [32, 512, 1024], P(('shard', 'replica')), may hold values from -6 to 6
- cotangent: bfloat16 [32, 512, 1024], P(('shard', 'replica')), may hold values from -6 to 6
- lengths: int32 [32], replicated, may hold values from 128 to 512, as said below
- permutation: int32 [32], replicated, may hold values from 0 to 31, as said below
- query_weight: bfloat16 [2, 1024, 1024], P('section', 'shard'), may hold values from -0.1875 to 0.1875
- query_bias: bfloat16 [2, 1024], P('section', 'shard'), may hold values from -3 to 3
- key_weight: bfloat16 [2, 1024, 1024], P('section', 'shard'), may hold values from -0.1875 to 0.1875
- value_weight: bfloat16 [2, 1024, 1024], P('section', 'shard'), may hold values from -0.1875 to 0.1875
- value_bias: bfloat16 [2, 1024], P('section', 'shard'), may hold values from -3 to 3
- output_weight: bfloat16 [2, 1024, 1024], P('section', 'shard'), may hold values from -3 to 3
- output_bias: bfloat16 [2, 1024], P('section', 'shard'), may hold values from -3 to 3
- first_gain: bfloat16 [2, 1024], P('section', 'shard'), may hold values from 0.5 to 1.5
- first_bias: bfloat16 [2, 1024], P('section', 'shard'), may hold values from -3 to 3
- inner_weight: bfloat16 [2, 1024, 4096], P('section', 'shard'), may hold values from -0.1875 to 0.1875
- inner_bias: bfloat16 [2, 4096], P('section', 'shard'), may hold values from -3 to 3
- outer_weight: bfloat16 [2, 4096, 1024], P('section', 'shard'), may hold values from -0.09375 to 0.09375
- outer_bias: bfloat16 [2, 1024], P('section', 'shard'), may hold values from -3 to 3
- second_gain: bfloat16 [2, 1024], P('section', 'shard'), may hold values from 0.5 to 1.5
- second_bias: bfloat16 [2, 1024], P('section', 'shard'), may hold values from -3 to 3
Outputs:
- activations: bfloat16 [2, 32, 512, 1024], P('section', ('shard', 'replica'))
- input_grads: bfloat16 [2, 32, 512, 1024], P('section', ('shard', 'replica'))
- grad_query_weight: float32 [2, 1024, 1024], P('section', 'shard')
- grad_query_bias: float32 [2, 1024], P('section', 'shard')
- grad_key_weight: float32 [2, 1024, 1024], P('section', 'shard')
- grad_value_weight: float32 [2, 1024, 1024], P('section', 'shard')
- grad_value_bias: float32 [2, 1024], P('section', 'shard')
- grad_output_weight: float32 [2, 1024, 1024], P('section', 'shard')
- grad_output_bias: float32 [2, 1024], P('section', 'shard')
- grad_first_gain: float32 [2, 1024], P('section', 'shard')
- grad_first_bias: float32 [2, 1024], P('section', 'shard')
- grad_inner_weight: float32 [2, 1024, 4096], P('section', 'shard')
- grad_inner_bias: float32 [2, 4096], P('section', 'shard')
- grad_outer_weight: float32 [2, 4096, 1024], P('section', 'shard')
- grad_outer_bias: float32 [2, 1024], P('section', 'shard')
- grad_second_gain: float32 [2, 1024], P('section', 'shard')
- grad_second_bias: float32 [2, 1024], P('section', 'shard')
Inputs may be any that keep to these rules, and one draw needn't show every extreme that they name: `lengths`: live tokens of each sequence; slots from it up to 512 are padding; some sequence has exactly 512. `permutation`: each of 0 to 31 once.
All inputs are finite; a program needn't handle non-finite values.
Results may differ from a plain program's by a relative error of at most 0.029.
Values may be sent and summed in bfloat16 or wider, within the bound.
A program may use at most 448 MiB of HBM per device.

v0:
```python
from functools import partial

import jax
import jax.numpy as jnp
from jax import lax
from jax.sharding import PartitionSpec as P

HEAD_DIM = 64
MICRO = 2


EPSILON = 1e-12
MASKED = -1000000000.0


def passed_along(value, axis, by):
    size = lax.axis_size(axis)
    pairs = [(i, i + by) for i in range(size) if 0 <= i + by < size]
    return lax.ppermute(value, axis, pairs)


def normalize(values, scaling, offset):
    average = jnp.mean(values, axis=-1, keepdims=True)
    centred = values - average
    variance = jnp.mean(centred * centred, axis=-1, keepdims=True)
    return centred * lax.rsqrt(variance + EPSILON) * scaling + offset


def dense(left_side, right_side):
    return jnp.dot(left_side, right_side, preferred_element_type=jnp.float32)


def dense_left(left_side, right_side):
    return jnp.einsum("ra,rb->ab", left_side, right_side, preferred_element_type=jnp.float32)


def dense_right(left_side, right_side):
    return jnp.einsum("rb,ab->ra", left_side, right_side, preferred_element_type=jnp.float32)


def column_sum(values):
    return jnp.sum(values, axis=0, dtype=jnp.float32)


def live_keys(lengths_in, slot_count):
    return jnp.arange(slot_count)[None, :] < lengths_in[:, None]


def choose_rows(targets, carry, pieces):
    count = pieces[0].shape[0]
    hit = jnp.logical_and(targets >= 0, targets < count)
    position = jnp.clip(targets, 0, count - 1)
    return tuple(
        (
            jnp.where(hit[:, None, None], jnp.take(piece, position, axis=0), kept)
            for piece, kept in zip(pieces, carry)
        )
    )


def score_block(queries, key_rows, live):
    scores = jnp.einsum("sqhd,skhd->shqk", queries, key_rows, preferred_element_type=jnp.float32)
    scores = scores * HEAD_DIM ** (-0.5)
    return jnp.where(live[:, None, None, :], scores, MASKED)


def forward_part(row_block, lengths_in, params):
    (
        query_weight,
        query_bias,
        key_weight,
        value_weight,
        value_bias,
        output_weight,
        output_bias,
        first_gain,
        first_bias,
        inner_weight,
        inner_bias,
        outer_weight,
        outer_bias,
        second_gain,
        second_bias,
    ) = params
    sequences, slot_count, model_width = row_block.shape
    head_count = model_width // HEAD_DIM
    split_heads = (sequences, slot_count, head_count, HEAD_DIM)
    flat_rows = row_block.reshape(sequences * slot_count, model_width)
    queries = (
        (dense(flat_rows, query_weight) + query_bias).astype(jnp.bfloat16).reshape(split_heads)
    )
    key_rows = dense(flat_rows, key_weight).astype(jnp.bfloat16).reshape(split_heads)
    values = (dense(flat_rows, value_weight) + value_bias).astype(jnp.bfloat16).reshape(split_heads)
    live = live_keys(lengths_in, slot_count)
    scores = score_block(queries, key_rows, live)
    highest = jnp.max(scores, axis=-1, keepdims=True)
    exponent = jnp.exp(scores - highest)
    totals = jnp.sum(exponent, axis=-1, keepdims=True)
    attention_weights = (exponent / totals).astype(jnp.bfloat16)
    log_total = highest + jnp.log(totals)
    context = jnp.einsum(
        "shqk,skhd->sqhd", attention_weights, values, preferred_element_type=jnp.float32
    )
    context = context.astype(jnp.bfloat16).reshape(sequences * slot_count, model_width)
    first_sum = flat_rows.astype(jnp.float32) + (dense(context, output_weight) + output_bias)
    middle = normalize(first_sum, first_gain.astype(jnp.float32), first_bias.astype(jnp.float32))
    middle_low = middle.astype(jnp.bfloat16)
    inner = dense(middle_low, inner_weight) + inner_bias
    activated = jax.nn.gelu(inner, approximate=False).astype(jnp.bfloat16)
    second_sum = middle + (dense(activated, outer_weight) + outer_bias)
    row_mask = live.reshape(-1, 1).astype(jnp.float32)
    normed = normalize(second_sum, second_gain.astype(jnp.float32), second_bias.astype(jnp.float32))
    result = (normed * row_mask).astype(jnp.bfloat16).reshape(row_block.shape)
    stored = (
        queries,
        key_rows,
        values,
        log_total,
        context,
        first_sum,
        middle_low,
        inner,
        second_sum,
    )
    return (result, stored)


def empty_forward(row_block, lengths_in, params):
    sequences, slot_count, model_width = row_block.shape
    head_count = model_width // HEAD_DIM
    hidden_width = params[9].shape[1]
    flat_count = sequences * slot_count
    split_heads = (sequences, slot_count, head_count, HEAD_DIM)
    stored = (
        jnp.zeros(split_heads, jnp.bfloat16),
        jnp.zeros(split_heads, jnp.bfloat16),
        jnp.zeros(split_heads, jnp.bfloat16),
        jnp.zeros((sequences, head_count, slot_count, 1), jnp.float32),
        jnp.zeros((flat_count, model_width), jnp.bfloat16),
        jnp.zeros((flat_count, model_width), jnp.float32),
        jnp.zeros((flat_count, model_width), jnp.bfloat16),
        jnp.zeros((flat_count, hidden_width), jnp.float32),
        jnp.zeros((flat_count, model_width), jnp.float32),
    )
    return (jnp.zeros(row_block.shape, jnp.bfloat16), stored)


def backward_part(grad_block, row_block, lengths_in, params, stored):
    (
        query_weight,
        query_bias,
        key_weight,
        value_weight,
        value_bias,
        output_weight,
        output_bias,
        first_gain,
        first_bias,
        inner_weight,
        inner_bias,
        outer_weight,
        outer_bias,
        second_gain,
        second_bias,
    ) = params
    queries, key_rows, values, log_total, context, first_sum, middle_low, inner, second_sum = stored
    sequences, slot_count, model_width = row_block.shape
    head_count = model_width // HEAD_DIM
    split_heads = (sequences, slot_count, head_count, HEAD_DIM)
    live = live_keys(lengths_in, slot_count)
    row_mask = live.reshape(-1, 1).astype(jnp.float32)
    grad_out = grad_block.reshape(-1, model_width).astype(jnp.float32) * row_mask
    _, second_back = jax.vjp(
        normalize, second_sum, second_gain.astype(jnp.float32), second_bias.astype(jnp.float32)
    )
    grad_second, grad_second_gain, grad_second_bias = second_back(grad_out)
    grad_outer = grad_second.astype(jnp.bfloat16)
    activated = jax.nn.gelu(inner, approximate=False).astype(jnp.bfloat16)
    _, gelu_back = jax.vjp(partial(jax.nn.gelu, approximate=False), inner)
    grad_inner = gelu_back(dense_right(grad_outer, outer_weight))[0].astype(jnp.bfloat16)
    grad_middle = grad_second + dense_right(grad_inner, inner_weight)
    _, first_back = jax.vjp(
        normalize, first_sum, first_gain.astype(jnp.float32), first_bias.astype(jnp.float32)
    )
    grad_first, grad_first_gain, grad_first_bias = first_back(grad_middle)
    grad_attended = grad_first.astype(jnp.bfloat16)
    grad_context = (
        dense_right(grad_attended, output_weight).astype(jnp.bfloat16).reshape(split_heads)
    )
    scores = score_block(queries, key_rows, live)
    attention_probs = jnp.exp(scores - log_total)
    grad_values = jnp.einsum(
        "shqk,sqhd->skhd",
        attention_probs.astype(jnp.bfloat16),
        grad_context,
        preferred_element_type=jnp.float32,
    )
    grad_values = grad_values.astype(jnp.bfloat16).reshape(-1, model_width)
    grad_probs = jnp.einsum(
        "sqhd,skhd->shqk", grad_context, values, preferred_element_type=jnp.float32
    )
    inner_product = jnp.sum(attention_probs * grad_probs, axis=-1, keepdims=True)
    grad_scores = (attention_probs * (grad_probs - inner_product)).astype(jnp.bfloat16)
    score_scale = HEAD_DIM ** (-0.5)
    grad_queries = jnp.einsum(
        "shqk,skhd->sqhd", grad_scores, key_rows, preferred_element_type=jnp.float32
    )
    grad_queries = (grad_queries * score_scale).astype(jnp.bfloat16).reshape(-1, model_width)
    grad_keys = jnp.einsum(
        "shqk,sqhd->skhd", grad_scores, queries, preferred_element_type=jnp.float32
    )
    grad_keys = (grad_keys * score_scale).astype(jnp.bfloat16).reshape(-1, model_width)
    grad_rows = (
        grad_first
        + dense_right(grad_queries, query_weight)
        + dense_right(grad_keys, key_weight)
        + dense_right(grad_values, value_weight)
    )
    small = (grad_first_gain, grad_first_bias, grad_second_gain, grad_second_bias)
    operands = (
        activated,
        grad_outer,
        middle_low,
        grad_inner,
        context,
        grad_attended,
        grad_queries,
        grad_keys,
        grad_values,
    )
    return (grad_rows.reshape(row_block.shape), small, operands)


def empty_backward(grad_block, row_block, lengths_in, params, stored):
    sequences, slot_count, model_width = row_block.shape
    hidden_width = params[9].shape[1]
    flat_count = sequences * slot_count
    small = tuple((jnp.zeros((model_width,), jnp.float32) for number in range(4)))
    narrow = jnp.zeros((flat_count, model_width), jnp.bfloat16)
    broad = jnp.zeros((flat_count, hidden_width), jnp.bfloat16)
    operands = (broad, narrow, narrow, broad, narrow, narrow, narrow, narrow, narrow)
    return (jnp.zeros(row_block.shape, jnp.float32), small, operands)


def weight_pass(flat_rows, small, operands):
    (
        activated,
        grad_outer,
        middle_low,
        grad_inner,
        context,
        grad_attended,
        grad_queries,
        grad_keys,
        grad_values,
    ) = operands
    grad_first_gain, grad_first_bias, grad_second_gain, grad_second_bias = small
    return (
        dense_left(flat_rows, grad_queries),
        column_sum(grad_queries),
        dense_left(flat_rows, grad_keys),
        dense_left(flat_rows, grad_values),
        column_sum(grad_values),
        dense_left(context, grad_attended),
        column_sum(grad_attended),
        grad_first_gain,
        grad_first_bias,
        dense_left(middle_low, grad_inner),
        column_sum(grad_inner),
        dense_left(activated, grad_outer),
        column_sum(grad_outer),
        grad_second_gain,
        grad_second_bias,
    )


def during(leading, moment, forward_pass):
    if 0 < moment < MICRO:
        return jnp.ones((), jnp.bool_)
    if (moment == 0) == forward_pass:
        return leading
    return jnp.logical_not(leading)


def pick(leading, upper_side, lower_side):
    return jax.tree.map(
        lambda one_side, other_side: jnp.where(leading, one_side, other_side),
        upper_side,
        lower_side,
    )


def on_device(
    inputs,
    cotangent,
    lengths,
    permutation,
    query_weight,
    query_bias,
    key_weight,
    value_weight,
    value_bias,
    output_weight,
    output_bias,
    first_gain,
    first_bias,
    inner_weight,
    inner_bias,
    outer_weight,
    outer_bias,
    second_gain,
    second_bias,
):
    shards = (
        query_weight,
        query_bias,
        key_weight,
        value_weight,
        value_bias,
        output_weight,
        output_bias,
        first_gain,
        first_bias,
        inner_weight,
        inner_bias,
        outer_weight,
        outer_bias,
        second_gain,
        second_bias,
    )
    leading = lax.axis_index("section") == 0
    local_count = inputs.shape[0]
    total_count = permutation.shape[0]
    model_width = inputs.shape[2]
    group = lax.axis_index(("shard", "replica"))
    first_slot = group * local_count
    wanted = lax.dynamic_slice_in_dim(permutation, first_slot, local_count)
    everyone = jnp.arange(total_count, dtype=jnp.int32)
    dealt_lengths = jnp.sum(
        jnp.where(wanted[:, None] == everyone[None, :], lengths[None, :], 0), axis=1
    )
    own_numbers = first_slot + jnp.arange(local_count, dtype=jnp.int32)
    home_slots = jnp.sum(
        jnp.where(permutation[None, :] == own_numbers[:, None], everyone[None, :], 0), axis=1
    )
    dealt = choose_rows(
        wanted,
        (jnp.zeros_like(inputs),),
        (lax.all_gather(inputs, ("shard", "replica"), axis=0, tiled=True),),
    )
    inputs = dealt[0]
    lengths = dealt_lengths
    block_count = local_count // MICRO
    gathered = (
        lax.all_gather(shards[0], "shard", axis=1, tiled=True),
        lax.all_gather(shards[1], "shard", axis=1, tiled=True),
        lax.all_gather(shards[2], "shard", axis=1, tiled=True),
        lax.all_gather(shards[3], "shard", axis=1, tiled=True),
        lax.all_gather(shards[4], "shard", axis=1, tiled=True),
        lax.all_gather(shards[5], "shard", axis=1, tiled=True),
        lax.all_gather(shards[6], "shard", axis=1, tiled=True),
        lax.all_gather(shards[7], "shard", axis=1, tiled=True),
        lax.all_gather(shards[8], "shard", axis=1, tiled=True),
        lax.all_gather(shards[9], "shard", axis=1, tiled=True),
        lax.all_gather(shards[10], "shard", axis=1, tiled=True),
        lax.all_gather(shards[11], "shard", axis=1, tiled=True),
        lax.all_gather(shards[12], "shard", axis=1, tiled=True),
        lax.all_gather(shards[13], "shard", axis=1, tiled=True),
        lax.all_gather(shards[14], "shard", axis=1, tiled=True),
    )
    params = tuple((weight[0] for weight in gathered))
    received = jnp.zeros_like(inputs[:block_count])
    feeding_list = []
    storage = []
    results = []
    for moment in range(MICRO + 1):
        own_index = min(moment, MICRO - 1)
        previous = max(moment - 1, 0)
        own_start = own_index * block_count
        prev_start = previous * block_count
        feeding = jnp.where(leading, inputs[own_start : own_start + block_count], received)
        piece_lengths = jnp.where(
            leading,
            lengths[own_start : own_start + block_count],
            lengths[prev_start : prev_start + block_count],
        )
        result, stored = lax.cond(
            during(leading, moment, True),
            forward_part,
            empty_forward,
            feeding,
            piece_lengths,
            params,
        )
        feeding_list.append(feeding)
        storage.append(stored)
        results.append(result)
        if moment < MICRO:
            received = passed_along(result, "section", 1)
    regathered = (
        lax.all_gather(shards[0], "shard", axis=1, tiled=True),
        lax.all_gather(shards[1], "shard", axis=1, tiled=True),
        lax.all_gather(shards[2], "shard", axis=1, tiled=True),
        lax.all_gather(shards[3], "shard", axis=1, tiled=True),
        lax.all_gather(shards[4], "shard", axis=1, tiled=True),
        lax.all_gather(shards[5], "shard", axis=1, tiled=True),
        lax.all_gather(shards[6], "shard", axis=1, tiled=True),
        lax.all_gather(shards[7], "shard", axis=1, tiled=True),
        lax.all_gather(shards[8], "shard", axis=1, tiled=True),
        lax.all_gather(shards[9], "shard", axis=1, tiled=True),
        lax.all_gather(shards[10], "shard", axis=1, tiled=True),
        lax.all_gather(shards[11], "shard", axis=1, tiled=True),
        lax.all_gather(shards[12], "shard", axis=1, tiled=True),
        lax.all_gather(shards[13], "shard", axis=1, tiled=True),
        lax.all_gather(shards[14], "shard", axis=1, tiled=True),
    )
    back_params = tuple((weight[0] for weight in regathered))
    accumulated = tuple((jnp.zeros(weight.shape[1:], jnp.float32) for weight in shards))
    small_total = tuple((jnp.zeros((model_width,), jnp.float32) for number in range(4)))
    operand_list = []
    row_list = []
    received = jnp.zeros_like(inputs[:block_count])
    grad_list = []
    for moment in range(MICRO + 1):
        own_index = min(moment, MICRO - 1)
        previous = max(moment - 1, 0)
        own_start = own_index * block_count
        prev_start = previous * block_count
        lower_index = max(moment - 1, 0)
        upper_index = min(moment + 1, MICRO)
        feeding = jnp.where(leading, received, cotangent[own_start : own_start + block_count])
        piece_lengths = jnp.where(
            leading,
            lengths[prev_start : prev_start + block_count],
            lengths[own_start : own_start + block_count],
        )
        row_block = jnp.where(leading, feeding_list[lower_index], feeding_list[upper_index])
        stored = pick(leading, storage[lower_index], storage[upper_index])
        grad_rows, small, operands = lax.cond(
            during(leading, moment, False),
            backward_part,
            empty_backward,
            feeding,
            row_block,
            piece_lengths,
            back_params,
            stored,
        )
        grad_low = grad_rows.astype(jnp.bfloat16)
        grad_list.append(grad_low)
        if moment < MICRO:
            received = passed_along(grad_low, "section", -1)
        small_total = tuple((before + added for before, added in zip(small_total, small)))
        operand_list.append(operands)
        row_list.append(row_block.reshape(-1, model_width))
    chosen_ops = [
        pick(leading, operand_list[number + 1], operand_list[number]) for number in range(MICRO)
    ]
    chosen_rows = [
        jnp.where(leading, row_list[number + 1], row_list[number]) for number in range(MICRO)
    ]
    joined_ops = tuple(
        (
            jnp.concatenate([one[slot] for one in chosen_ops], axis=0)
            for slot in range(len(chosen_ops[0]))
        )
    )
    joined_rows = jnp.concatenate(chosen_rows, axis=0)
    gradients = weight_pass(joined_rows, small_total, joined_ops)
    owned_part = (
        lax.psum_scatter(
            gradients[0].astype(jnp.bfloat16), "shard", scatter_dimension=0, tiled=True
        ).astype(jnp.float32),
        lax.psum_scatter(
            gradients[1].astype(jnp.bfloat16), "shard", scatter_dimension=0, tiled=True
        ).astype(jnp.float32),
        lax.psum_scatter(
            gradients[2].astype(jnp.bfloat16), "shard", scatter_dimension=0, tiled=True
        ).astype(jnp.float32),
        lax.psum_scatter(
            gradients[3].astype(jnp.bfloat16), "shard", scatter_dimension=0, tiled=True
        ).astype(jnp.float32),
        lax.psum_scatter(
            gradients[4].astype(jnp.bfloat16), "shard", scatter_dimension=0, tiled=True
        ).astype(jnp.float32),
        lax.psum_scatter(
            gradients[5].astype(jnp.bfloat16), "shard", scatter_dimension=0, tiled=True
        ).astype(jnp.float32),
        lax.psum_scatter(
            gradients[6].astype(jnp.bfloat16), "shard", scatter_dimension=0, tiled=True
        ).astype(jnp.float32),
        lax.psum_scatter(
            gradients[7].astype(jnp.bfloat16), "shard", scatter_dimension=0, tiled=True
        ).astype(jnp.float32),
        lax.psum_scatter(
            gradients[8].astype(jnp.bfloat16), "shard", scatter_dimension=0, tiled=True
        ).astype(jnp.float32),
        lax.psum_scatter(
            gradients[9].astype(jnp.bfloat16), "shard", scatter_dimension=0, tiled=True
        ).astype(jnp.float32),
        lax.psum_scatter(
            gradients[10].astype(jnp.bfloat16), "shard", scatter_dimension=0, tiled=True
        ).astype(jnp.float32),
        lax.psum_scatter(
            gradients[11].astype(jnp.bfloat16), "shard", scatter_dimension=0, tiled=True
        ).astype(jnp.float32),
        lax.psum_scatter(
            gradients[12].astype(jnp.bfloat16), "shard", scatter_dimension=0, tiled=True
        ).astype(jnp.float32),
        lax.psum_scatter(
            gradients[13].astype(jnp.bfloat16), "shard", scatter_dimension=0, tiled=True
        ).astype(jnp.float32),
        lax.psum_scatter(
            gradients[14].astype(jnp.bfloat16), "shard", scatter_dimension=0, tiled=True
        ).astype(jnp.float32),
    )
    accumulated = (
        lax.psum(owned_part[0].astype(jnp.bfloat16), "replica").astype(jnp.float32),
        lax.psum(owned_part[1].astype(jnp.bfloat16), "replica").astype(jnp.float32),
        lax.psum(owned_part[2].astype(jnp.bfloat16), "replica").astype(jnp.float32),
        lax.psum(owned_part[3].astype(jnp.bfloat16), "replica").astype(jnp.float32),
        lax.psum(owned_part[4].astype(jnp.bfloat16), "replica").astype(jnp.float32),
        lax.psum(owned_part[5].astype(jnp.bfloat16), "replica").astype(jnp.float32),
        lax.psum(owned_part[6].astype(jnp.bfloat16), "replica").astype(jnp.float32),
        lax.psum(owned_part[7].astype(jnp.bfloat16), "replica").astype(jnp.float32),
        lax.psum(owned_part[8].astype(jnp.bfloat16), "replica").astype(jnp.float32),
        lax.psum(owned_part[9].astype(jnp.bfloat16), "replica").astype(jnp.float32),
        lax.psum(owned_part[10].astype(jnp.bfloat16), "replica").astype(jnp.float32),
        lax.psum(owned_part[11].astype(jnp.bfloat16), "replica").astype(jnp.float32),
        lax.psum(owned_part[12].astype(jnp.bfloat16), "replica").astype(jnp.float32),
        lax.psum(owned_part[13].astype(jnp.bfloat16), "replica").astype(jnp.float32),
        lax.psum(owned_part[14].astype(jnp.bfloat16), "replica").astype(jnp.float32),
    )
    dealt_outputs = jnp.concatenate(
        [jnp.where(leading, results[number], results[number + 1]) for number in range(MICRO)],
        axis=0,
    )
    returned = choose_rows(
        home_slots,
        (jnp.zeros_like(dealt_outputs),),
        (lax.all_gather(dealt_outputs, ("shard", "replica"), axis=0, tiled=True),),
    )
    activations = returned[0][None]
    input_grads = jnp.concatenate(
        [jnp.where(leading, grad_list[number + 1], grad_list[number]) for number in range(MICRO)],
        axis=0,
    )[None]
    return (activations, input_grads) + tuple((total[None] for total in accumulated))


def solution(mesh):
    in_specs = (
        P(("shard", "replica"), None, None),
        P(("shard", "replica"), None, None),
        P(),
        P(),
        P("section", "shard", None),
        P("section", "shard"),
        P("section", "shard", None),
        P("section", "shard", None),
        P("section", "shard"),
        P("section", "shard", None),
        P("section", "shard"),
        P("section", "shard"),
        P("section", "shard"),
        P("section", "shard", None),
        P("section", "shard"),
        P("section", "shard", None),
        P("section", "shard"),
        P("section", "shard"),
        P("section", "shard"),
    )
    out_specs = (
        P("section", ("shard", "replica"), None, None),
        P("section", ("shard", "replica"), None, None),
        P("section", "shard", None),
        P("section", "shard"),
        P("section", "shard", None),
        P("section", "shard", None),
        P("section", "shard"),
        P("section", "shard", None),
        P("section", "shard"),
        P("section", "shard"),
        P("section", "shard"),
        P("section", "shard", None),
        P("section", "shard"),
        P("section", "shard", None),
        P("section", "shard"),
        P("section", "shard"),
        P("section", "shard"),
    )
    return jax.shard_map(
        on_device, mesh=mesh, in_specs=in_specs, out_specs=out_specs, check_vma=False
    )
```

profile of v0, /device:TPU:0, one launch (start us, length us, event | category | flops | bytes accessed | tf_op | source)
XLA Modules:
  0.0 2496.2 jit_solution(3068147556769768025)
XLA Ops:
  54.2 309.7 %all-gather.9.cloned.1.call-done = bf16[32,512,1024]{2,1,0:T(8,128)(2,1)} async-done(((bf16[2,512,1024]{2,1,0:T(8,128)(2,1)}), bf16[32,512,1024]{2,1,0:T(8,128)(2,1)}) %all-gather.9.cloned.1.call-update) | async-done | bytes 33554448 | tf_op jit(solution)/shard_map/all_gather | solution.py:349
  367.8 29.0 %all-gather.13.cloned.1.call-done = bf16[1,1024,1024]{2,1,0:T(8,128)(2,1)} async-done(((bf16[1,512,1024]{2,1,0:T(8,128)(2,1)}), bf16[1,1024,1024]{2,1,0:T(8,128)(2,1)}) %all-gather.13.cloned.1.call-update) | async-done | bytes 2097168 | tf_op jit(solution)/shard_map/all_gather | solution.py:355
  396.8 34.7 %all-gather.15.cloned.1.call-done = bf16[1,1024,1024]{2,1,0:T(8,128)(2,1)} async-done(((bf16[1,512,1024]{2,1,0:T(8,128)(2,1)}), bf16[1,1024,1024]{2,1,0:T(8,128)(2,1)}) %all-gather.15.cloned.1.call-update) | async-done | bytes 2097168 | tf_op jit(solution)/shard_map/all_gather | solution.py:357
  431.4 34.5 %all-gather.11.cloned.1.call-done = bf16[1,1024,1024]{2,1,0:T(8,128)(2,1)} async-done(((bf16[1,512,1024]{2,1,0:T(8,128)(2,1)}), bf16[1,1024,1024]{2,1,0:T(8,128)(2,1)}) %all-gather.11.cloned.1.call-update) | async-done | bytes 2097168 | tf_op jit(solution)/shard_map/all_gather | solution.py:358
  466.0 34.5 %all-gather.17.cloned.1.call-done = bf16[1,1024,1024]{2,1,0:T(8,128)(2,1)} async-done(((bf16[1,512,1024]{2,1,0:T(8,128)(2,1)}), bf16[1,1024,1024]{2,1,0:T(8,128)(2,1)}) %all-gather.17.cloned.1.call-update) | async-done | bytes 2097168 | tf_op jit(solution)/shard_map/all_gather | solution.py:360
  500.5 105.4 %all-gather.19.cloned.1.call-done = bf16[1,1024,4096]{2,1,0:T(8,128)(2,1)} async-done(((bf16[1,512,4096]{2,1,0:T(8,128)(2,1)}), bf16[1,1024,4096]{2,1,0:T(8,128)(2,1)}) %all-gather.19.cloned.1.call-update) | async-done | bytes 8388624 | tf_op jit(solution)/shard_map/all_gather | solution.py:364
  605.9 105.6 %all-gather.21.cloned.1.call-done = bf16[1,4096,1024]{2,1,0:T(8,128)(2,1)} async-done(((bf16[1,2048,1024]{2,1,0:T(8,128)(2,1)}), bf16[1,4096,1024]{2,1,0:T(8,128)(2,1)}) %all-gather.21.cloned.1.call-update) | async-done | bytes 8388624 | tf_op jit(solution)/shard_map/all_gather | solution.py:366
  711.5 80.7 %conditional.4 = (bf16[1,512,1024]{2,1,0:T(8,128)(2,1)S(1)}, bf16[1,512,16,64]{1,3,2,0:T(8,128)(2,1)S(1)}, bf16[1,512,16,64]{1,3,2,0:T(8,128)(2,1)}, bf16[1,512,...) conditional(s32[]{:T(128)} %convert_element_type.536, () %tuple.50, ...), branch_computations={%region_2.4_spmd, %region_3.0_spmd} | conditional | flops 14165220352 | bytes 188143984 | solution.py:387
  751.1 11.7 convolution_add_fusion
  762.9 25.0 %fusion.375 = (f32[512]{0:T(512)S(1)}, f32[512,1024]{1,0:T(8,128)}) fusion(f32[1024]{0:T(1024)S(1)} %convert_element_type.419, bf16[4096,1024]{1,0:T(8,128)(2,1)S(1)} %bitcast.408, f32[512,4096]{1,0:T(8,128)} %convolution_add_fusion, f32[1024]{0:T(1024)S(1)} %convert_element_type.415, f32[1024]{0:T(1024)S(1)} %convert_element_type.414, ...), kind=kOutput, calls=%fused_computation.601 | convolution fusion | flops 4434951680 | bytes 20989952 | tf_op jit(solution)/shard_map/cond/branch_1_fun/dot_general | solution.py:30
  830.6 12.7 broadcast_add_fusion
  843.3 24.3 fusion.381
  880.7 25.4 %conditional.6 = (f32[1024]{0:T(1024)}, f32[1024]{0:T(1024)}, f32[1024]{0:T(1024)}, f32[1024]{0:T(1024)}, bf16[512,4096]{1,0:T(8,128)(2,1)}, /*index=5*/bf16[512...) conditional(s32[]{:T(128)} %convert_element_type.549, () %tuple.54, ...), branch_computations={%region_24.26_spmd, %region_25.40_spmd} | conditional | flops 15810959360 | bytes 566050624 | solution.py:439
  911.2 19.9 conditional.5
  935.4 89.5 %collective-permute-done.2 = bf16[1,512,1024]{2,1,0:T(8,128)(2,1)} collective-permute-done((bf16[1,512,1024]{2,1,0:T(8,128)(2,1)}, bf16[1,512,1024]{2,1,0:T(8,128)(2,1)}, u32[]{:S(2)}, u32[]{:S(2)}) %collective-permute-start.2) | collective-permute-done | bytes 1048608 | tf_op jit(solution)/shard_map/ppermute | solution.py:19
  1029.7 24.6 broadcast_select_fusion.5
  1056.3 13.4 add_convert_fusion.12
  1095.6 14.7 multiply_reduce_fusion.14
  1152.8 88.0 %collective-permute-done.3 = bf16[1,512,1024]{2,1,0:T(8,128)(2,1)} collective-permute-done((bf16[1,512,1024]{2,1,0:T(8,128)(2,1)}, bf16[1,512,1024]{2,1,0:T(8,128)(2,1)}, u32[]{:S(2)}, u32[]{:S(2)}) %collective-permute-start.3) | collective-permute-done | bytes 1048608 | tf_op jit(solution)/shard_map/ppermute | solution.py:19
  1240.8 143.9 %conditional.7 = (f32[1024]{0:T(1024)}, f32[1024]{0:T(1024)}, f32[1024]{0:T(1024)}, f32[1024]{0:T(1024)}, bf16[512,4096]{1,0:T(8,128)(2,1)}, /*index=5*/bf16[512...) conditional(s32[]{:T(128)} %convert_element_type.536, () %tuple.56, ...), branch_computations={%region_48.50_spmd, %region_49.64_spmd} | conditional | flops 15810959360 | bytes 556613376 | solution.py:439
  1261.2 21.1 multiply_convert_fusion.7
  1282.3 12.4 add_convert_fusion.8
  1324.2 12.9 multiply_reduce_fusion.9
  1337.1 15.3 multiply_convert_fusion.6
  1421.8 12.3 fusion.211
  1458.6 34.6 %reduce-scatter.7.cloned.1.call-done = bf16[512,1024]{1,0:T(8,128)(2,1)} async-done(((bf16[1024,1024]{1,0:T(8,128)(2,1)}), bf16[512,1024]{1,0:T(8,128)(2,1)}) %reduce-scatter.7.cloned.1.call-update) | async-done | bytes 1048592 | tf_op jit(solution)/shard_map/reduce_scatter | solution.py:471
  1493.2 34.8 %reduce-scatter.11.cloned.1.call-done = bf16[512,1024]{1,0:T(8,128)(2,1)} async-done(((bf16[1024,1024]{1,0:T(8,128)(2,1)}), bf16[512,1024]{1,0:T(8,128)(2,1)}) %reduce-scatter.11.cloned.1.call-update) | async-done | bytes 1048592 | tf_op jit(solution)/shard_map/reduce_scatter | solution.py:480
  1527.9 102.1 %reduce-scatter.17.cloned.1.call-done = bf16[2048,1024]{1,0:T(8,128)(2,1)} async-done(((bf16[4096,1024]{1,0:T(8,128)(2,1)}), bf16[2048,1024]{1,0:T(8,128)(2,1)}) %reduce-scatter.17.cloned.1.call-update) | async-done | bytes 4194320 | tf_op jit(solution)/shard_map/reduce_scatter | solution.py:504
  1630.0 102.2 %reduce-scatter.15.cloned.1.call-done = bf16[512,4096]{1,0:T(8,128)(2,1)} async-done(((bf16[1024,4096]{1,0:T(8,128)(2,1)}), bf16[512,4096]{1,0:T(8,128)(2,1)}) %reduce-scatter.15.cloned.1.call-update) | async-done | bytes 4194320 | tf_op jit(solution)/shard_map/reduce_scatter | solution.py:498
  1748.1 39.6 %all-reduce.9 = (bf16[1,512]{1,0:T(2,128)(2,1)S(1)}, bf16[1,512]{1,0:T(2,128)(2,1)S(1)}, bf16[1,512]{1,0:T(2,128)(2,1)S(1)}, bf16[1,512]{1,0:T(2,128)(2,1)S(1)},...) all-reduce(bf16[1,512]{1,0:T(2,128)(2,1)S(1)} %broadcast_in_dim.337, ...), channel_id=1, replica_groups=mesh['section'=2,'shard'=2,'replica'=8] {'replica'}, use_global_device_ids=true, to_apply=%region_68.70 | all-reduce | flops 6144 | bytes 24576 | tf_op jit(solution)/shard_map/psum | solution.py:519
  1796.3 336.8 %all-reduce.14.cloned.1.call-done = (bf16[1,512,1024]{2,1,0:T(8,128)(2,1)}, bf16[1,512,1024]{2,1,0:T(8,128)(2,1)}, bf16[1,512,1024]{2,1,0:T(8,128)(2,1)}, bf16[1...) async-done(((bf16[1,512,1024]{2,1,0:T(8,128)(2,1)}, bf16[1,512,1024]{2,1,0:T(8,128)(2,1)}, bf16[1,512,1024]{2,1,0:T(8,128)(2,1)}, ...) | async-done | bytes 12582928 | tf_op jit(solution)/shard_map/psum | solution.py:518
  2152.7 332.9 %all-gather.23.cloned.1.call-done = bf16[32,512,1024]{2,1,0:T(8,128)(2,1)} async-done(((bf16[2,512,1024]{2,1,0:T(8,128)(2,1)}), bf16[32,512,1024]{2,1,0:T(8,128)(2,1)}) %all-gather.23.cloned.1.call-update) | async-done | bytes 33554448 | tf_op jit(solution)/shard_map/all_gather | solution.py:541
  (577 shorter events, 443.4 us)
Async XLA Ops:
  7.3 356.6 %all-gather.9.cloned.1.call-start = ((), (), s32[]{:S(2)}) async-start(), calls=%async_computation.6 | async-start | bytes 35651584 | tf_op jit(solution)/shard_map/all_gather | solution.py:349
  8.0 388.7 %all-gather.13.cloned.1.call-start = ((), (), s32[]{:S(2)}) async-start(), calls=%async_computation.8 | async-start | bytes 3145728 | tf_op jit(solution)/shard_map/all_gather | solution.py:355
  8.8 422.7 %all-gather.15.cloned.1.call-start = ((), (), s32[]{:S(2)}) async-start(), calls=%async_computation.9 | async-start | bytes 3145728 | tf_op jit(solution)/shard_map/all_gather | solution.py:357
  9.5 456.4 %all-gather.11.cloned.1.call-start = ((), (), s32[]{:S(2)}) async-start(), calls=%async_computation.7 | async-start | bytes 3145728 | tf_op jit(solution)/shard_map/all_gather | solution.py:358
  10.1 490.4 %all-gather.17.cloned.1.call-start = ((), (), s32[]{:S(2)}) async-start(), calls=%async_computation.10 | async-start | bytes 3145728 | tf_op jit(solution)/shard_map/all_gather | solution.py:360
  10.7 595.2 %all-gather.19.cloned.1.call-start = ((), (), s32[]{:S(2)}) async-start(), calls=%async_computation.11 | async-start | bytes 12582912 | tf_op jit(solution)/shard_map/all_gather | solution.py:364
  11.3 700.2 %all-gather.21.cloned.1.call-start = ((), (), s32[]{:S(2)}) async-start(), calls=%async_computation.12 | async-start | bytes 12582912 | tf_op jit(solution)/shard_map/all_gather | solution.py:366
  12.0 1441.4 %reduce-scatter.9.cloned.1.call-start = ((), (), s32[]{:S(2)}) async-start(), calls=%async_computation.15 | async-start | bytes 3145728 | tf_op jit(solution)/shard_map/reduce_scatter | solution.py:477
  17.4 776.2 %copy-start.120 = (bf16[1024]{0:T(1024)(128)(2,1)}, bf16[1024]{0:T(1024)(128)(2,1)S(1)}, u32[]{:S(2)}) copy-start(bf16[1024]{0:T(1024)(128)(2,1)S(1)} %reduce.35) | copy-start | bytes 6148
  21.8 689.6 %copy-start.122 = (bf16[1024]{0:T(1024)(128)(2,1)}, bf16[1024]{0:T(1024)(128)(2,1)S(1)}, u32[]{:S(2)}) copy-start(bf16[1024]{0:T(1024)(128)(2,1)S(1)} %reduce.34) | copy-start | bytes 6148
  26.2 768.1 %copy-start.123 = (bf16[1024]{0:T(1024)(128)(2,1)}, bf16[1024]{0:T(1024)(128)(2,1)S(1)}, u32[]{:S(2)}) copy-start(bf16[1024]{0:T(1024)(128)(2,1)S(1)} %reduce.36) | copy-start | bytes 6148
  30.8 680.6 %copy-start.108 = (bf16[1024]{0:T(1024)(128)(2,1)}, bf16[1024]{0:T(1024)(128)(2,1)S(1)}, u32[]{:S(2)}) copy-start(bf16[1024]{0:T(1024)(128)(2,1)S(1)} %reduce.37) | copy-start | bytes 6148
  35.4 676.0 %copy-start.125 = (bf16[1024]{0:T(1024)(128)(2,1)}, bf16[1024]{0:T(1024)(128)(2,1)S(1)}, u32[]{:S(2)}) copy-start(bf16[1024]{0:T(1024)(128)(2,1)S(1)} %reduce.38) | copy-start | bytes 6148
  40.0 755.7 %copy-start.126 = (bf16[1024]{0:T(1024)(128)(2,1)}, bf16[1024]{0:T(1024)(128)(2,1)S(1)}, u32[]{:S(2)}) copy-start(bf16[1024]{0:T(1024)(128)(2,1)S(1)} %reduce.40) | copy-start | bytes 6148
  44.4 751.3 %copy-start.110 = (bf16[1024]{0:T(1024)(128)(2,1)}, bf16[1024]{0:T(1024)(128)(2,1)S(1)}, u32[]{:S(2)}) copy-start(bf16[1024]{0:T(1024)(128)(2,1)S(1)} %reduce.41) | copy-start | bytes 6148
  48.8 747.5 %copy-start.128 = (bf16[1024]{0:T(1024)(128)(2,1)}, bf16[1024]{0:T(1024)(128)(2,1)S(1)}, u32[]{:S(2)}) copy-start(bf16[1024]{0:T(1024)(128)(2,1)S(1)} %reduce.42) | copy-start | bytes 6148
  53.2 743.6 %copy-start.106 = (bf16[4096]{0:T(1024)(128)(2,1)}, bf16[4096]{0:T(1024)(128)(2,1)S(1)}, u32[]{:S(2)}) copy-start(bf16[4096]{0:T(1024)(128)(2,1)S(1)} %reduce.39) | copy-start | bytes 24580
  792.2 6.5 collective-permute-start
  871.1 36.4 %collective-permute-start.1 = (bf16[1,512,1024]{2,1,0:T(8,128)(2,1)}, bf16[1,512,1024]{2,1,0:T(8,128)(2,1)}, u32[]{:S(2)}, u32[]{:S(2)}) collective-permute-start(bf16[1,512,1024]{2,1,0:T(8,128)(2,1)} %get-tuple-element.1102), channel_id=1, source_target_pairs={{0,16},{1,17},{2,18},{3,19},{4,20},{5,21},{6,22},{7,23},{8,24},{9,... | collective-permute-start | bytes 3145736 | tf_op jit(solution)/shard_map/ppermute | solution.py:19
  906.1 118.7 %collective-permute-start.2 = (bf16[1,512,1024]{2,1,0:T(8,128)(2,1)}, bf16[1,512,1024]{2,1,0:T(8,128)(2,1)}, u32[]{:S(2)}, u32[]{:S(2)}) collective-permute-start(bf16[1,512,1024]{2,1,0:T(8,128)(2,1)} %get-tuple-element.489), channel_id=1, source_target_pairs={{16,0},{17,1},{18,2},{19,3},{20,4},{21,5},{22,6},{23,7},{24,8},{25... | collective-permute-start | bytes 3145736 | tf_op jit(solution)/shard_map/ppermute | solution.py:19
  931.1 156.3 %copy-start.52 = (bf16[1,512,16,64]{1,3,2,0:T(8,128)(2,1)}, bf16[1,512,16,64]{1,3,2,0:T(8,128)(2,1)S(1)}, u32[]{:S(2)}) copy-start(bf16[1,512,16,64]{1,3,2,0:T(8,128)(2,1)S(1)} %get-tuple-element.496) | copy-start | bytes 3145732
  1142.5 98.3 %copy-start.112 = (bf16[1024]{0:T(1024)(128)(2,1)S(1)}, bf16[1024]{0:T(1024)(128)(2,1)}, u32[]{:S(2)}) copy-start(bf16[1024]{0:T(1024)(128)(2,1)} %copy-done.110) | copy-start | bytes 6148
  1145.2 95.6 %collective-permute-start.3 = (bf16[1,512,1024]{2,1,0:T(8,128)(2,1)}, bf16[1,512,1024]{2,1,0:T(8,128)(2,1)}, u32[]{:S(2)}, u32[]{:S(2)}) collective-permute-start(bf16[1,512,1024]{2,1,0:T(8,128)(2,1)} %fusion.273), channel_id=1, source_target_pairs={{16,0},{17,1},{18,2},{19,3},{20,4},{21,5},{22,6},{23,7},{24,8},{25... | collective-permute-start | bytes 3145736 | tf_op jit(solution)/shard_map/ppermute | solution.py:19
  1391.8 66.8 %reduce-scatter.13.cloned.1.call-start = ((), (), s32[]{:S(2)}) async-start(), calls=%async_computation.17 | async-start | bytes 3145728 | tf_op jit(solution)/shard_map/reduce_scatter | solution.py:486
  1401.7 91.4 %reduce-scatter.7.cloned.1.call-start = ((), (), s32[]{:S(2)}) async-start(), calls=%async_computation.14 | async-start | bytes 3145728 | tf_op jit(solution)/shard_map/reduce_scatter | solution.py:471
  1409.3 118.7 %reduce-scatter.11.cloned.1.call-start = ((), (), s32[]{:S(2)}) async-start(), calls=%async_computation.16 | async-start | bytes 3145728 | tf_op jit(solution)/shard_map/reduce_scatter | solution.py:480
  1417.2 212.8 %reduce-scatter.17.cloned.1.call-start = ((), (), s32[]{:S(2)}) async-start(), calls=%async_computation.19 | async-start | bytes 12582912 | tf_op jit(solution)/shard_map/reduce_scatter | solution.py:504
  1434.2 298.1 %reduce-scatter.15.cloned.1.call-start = ((), (), s32[]{:S(2)}) async-start(), calls=%async_computation.18 | async-start | bytes 12582912 | tf_op jit(solution)/shard_map/reduce_scatter | solution.py:498
  1453.4 279.0 %copy-start.92 = (bf16[1,512,1024]{2,1,0:T(8,128)(2,1)S(1)}, bf16[1,512,1024]{2,1,0:T(8,128)(2,1)}, u32[]{:S(2)}) copy-start(bf16[1,512,1024]{2,1,0:T(8,128)(2,1)} %copy-done.91) | copy-start | bytes 3145732
  1453.4 280.4 %copy-start.99 = (bf16[1,512,1024]{2,1,0:T(8,128)(2,1)S(1)}, bf16[1,512,1024]{2,1,0:T(8,128)(2,1)}, u32[]{:S(2)}) copy-start(bf16[1,512,1024]{2,1,0:T(8,128)(2,1)} %get-tuple-element.1101) | copy-start | bytes 3145732
  1453.4 679.7 %all-reduce.14.cloned.1.call-start = ((), (), s32[]{:S(2)}) async-start(), calls=%async_computation.20 | async-start | bytes 25165824 | tf_op jit(solution)/shard_map/psum | solution.py:518
  1732.3 753.3 %all-gather.23.cloned.1.call-start = ((), (), s32[]{:S(2)}) async-start(), calls=%async_computation.13 | async-start | bytes 35651584 | tf_op jit(solution)/shard_map/all_gather | solution.py:541
  (125 other events, 2284.4 us)
Sparse Core Ops, SparseCore 0:
  10.9 352.9 all-gather.8
  365.4 31.2 all-gather.12
  398.3 33.0 all-gather.14
  432.8 33.0 all-gather.10
  467.4 33.0 all-gather.16
  501.9 103.9 all-gather.18
  607.4 103.9 all-gather.20
  1391.9 31.8 reduce-scatter.8
  1426.6 31.8 reduce-scatter.12
  1461.2 31.8 reduce-scatter.6
  1496.0 31.8 reduce-scatter.10
  1530.7 99.3 reduce-scatter.16
  1632.9 99.3 reduce-scatter.14
  1737.6 395.5 all-reduce.13
  2136.3 349.2 all-gather.22
where the time goes:
time: 2500 us
  waiting for transfers between devices  1780 us (71%)
  matrix products  306 us (12%)
  other arithmetic  191 us (8%)
  blocking collectives  87.6 us (4%)
  local copies, waits for them, and re-layouts  82.3 us (3%)
    psum x1, waiting for transfers between devices, on_device(): lax.psum(owned_part[0].astype(jnp.bfloat16), 'replica').astype(jnp.float32)  337 us
    all_gather x1, waiting for transfers between devices, on_device(): lax.all_gather(dealt_outputs, ('shard', 'replica'), axis=0, tiled=True)  333 us
    all_gather x1, waiting for transfers between devices, on_device(): lax.all_gather(inputs, ('shard', 'replica'), axis=0, tiled=True)  310 us
    ppermute x4, waiting for transfers between devices, passed_along(): return lax.ppermute(value, axis, pairs)  178 us
    all_gather x1, waiting for transfers between devices, on_device(): lax.all_gather(shards[11], 'shard', axis=1, tiled=True)  106 us
    all_gather x1, waiting for transfers between devices, on_device(): lax.all_gather(shards[9], 'shard', axis=1, tiled=True)  105 us
    reduce_scatter x1, waiting for transfers between devices, on_device(): lax.psum_scatter(gradients[9].astype(jnp.bfloat16), 'shard', scatter_dime...  102 us
    reduce_scatter x1, waiting for transfers between devices, on_device(): lax.psum_scatter(gradients[11].astype(jnp.bfloat16), 'shard', scatter_dim...  102 us
  transfers between devices with their start and end apart: 19, of which 16 were waited for; matrix products, arithmetic and copies ran while one was open for 6% of the time, Pallas kernels for 0%

commit v1 on v0

v1 whole, which is shorter than its diff:
```python
import jax
import jax.numpy as jnp
from jax import lax
from jax.experimental import pallas as pl
from jax.experimental.pallas import tpu as pltpu

ALL = ("section", "shard", "replica")
GROUP = ("shard", "replica")
UNITS = 12
DIRECT = (0, 1, 2)
DOUBLED = (3, 4, 5, 6, 7, 8, 9, 10, 11)
VMEM_LIMIT = 64000000


def my_bits(count):
    replica = lax.axis_index("replica")
    return tuple((lax.rem(replica // (1 << (count - 1 - p)), 2) for p in range(count)))


def across(p, count, bits):
    replica = lax.axis_index("replica")
    weight = 1 << (count - 1 - p)
    return {"replica": replica + weight * (1 - 2 * bits[p])}


def greet(partners):
    barrier = pltpu.get_barrier_semaphore()
    for partner in partners:
        pl.semaphore_signal(barrier, inc=1, device_id=partner, device_id_type=pl.DeviceIdType.MESH)
    pl.semaphore_wait(barrier, len(partners))


def remote(src, dst, send_sem, recv_sem, partner):
    return pltpu.make_async_remote_copy(
        src_ref=src,
        dst_ref=dst,
        send_sem=send_sem,
        recv_sem=recv_sem,
        device_id=partner,
        device_id_type=pl.DeviceIdType.MESH,
    )


def gather_kernel(
    count, wq, wk, wv, wo, w1, w2, small,
    oq, ok, ov, oo, o1, o2, osmall,
    stage, send_sem, recv_sem, load_sem, store_sem,
):
    core = lax.axis_index("section")
    side = lax.axis_index("shard")
    bits = my_bits(count)
    sibling = {"section": 1 - core}
    facing = {"shard": 1 - side}
    corner = {"section": 1 - core, "shard": 1 - side}
    everything = (slice(None),) * count

    def source(unit, index):
        if unit < 4:
            return (wq, wk, wv, wo)[unit].at[index]
        if unit < 8:
            return w1.at[index + (slice(None), pl.ds(1024 * (unit - 4), 1024))]
        return w2.at[(unit - 8,) + index]

    def target(unit, layer, half, index):
        if unit < 4:
            return (oq, ok, ov, oo)[unit].at[(layer, half) + index]
        if unit < 8:
            return o1.at[(layer, half) + index + (slice(None), pl.ds(1024 * (unit - 4), 1024))]
        return o2.at[(layer, half, unit - 8) + index]

    greet([sibling, facing, corner] + [across(p, count, bits) for p in range(count)])
    number = [0]
    sends = []

    def start(src, dst, partner):
        at = number[0]
        number[0] += 1
        copy = remote(src, dst, send_sem.at[at], recv_sem.at[at], partner)
        copy.start()
        sends.append(copy)
        return at

    def arrive(at, dst, partner):
        remote(dst, dst, send_sem.at[at], recv_sem.at[at], partner).wait_recv()

    first = {}
    for unit in DOUBLED:
        first[unit] = start(source(unit, bits), target(unit, core, side, bits), facing)
    small_at = [
        start(small, osmall.at[core, side], partner) for partner in (sibling, facing, corner)
    ]
    for unit in DIRECT:
        first[unit] = start(source(unit, everything), target(unit, core, side, everything), facing)
    loads = []
    for unit in range(UNITS):
        copy = pltpu.make_async_copy(source(unit, everything), stage.at[unit], load_sem.at[unit])
        copy.start()
        loads.append(copy)
    small_copy = pltpu.make_async_copy(small, osmall.at[core, side], store_sem.at[UNITS])
    small_copy.start()
    own = {}
    for unit in DOUBLED + DIRECT:
        own[unit] = start(source(unit, everything), target(unit, core, side, everything), sibling)
    stores = []
    for unit in range(UNITS):
        loads[unit].wait()
        copy = pltpu.make_async_copy(
            stage.at[unit], target(unit, core, side, everything), store_sem.at[unit]
        )
        copy.start()
        stores.append(copy)
    inflight = {unit: first[unit] for unit in range(UNITS)}
    passed = {}
    waiting = list(DIRECT)

    def finish_direct(unit):
        landed = target(unit, core, 1 - side, everything)
        arrive(inflight[unit], landed, facing)
        passed[unit] = start(landed, landed, sibling)

    for tick in range(len(DOUBLED) + count + 1):
        for step in reversed(range(count + 1)):
            j = tick - step
            if not 0 <= j < len(DOUBLED):
                continue
            unit = DOUBLED[j]
            if step == 0:
                arrive(inflight[unit], target(unit, core, 1 - side, bits), facing)
            else:
                p = step - 1
                landed = everything[:p] + (1 - bits[p],) + bits[p + 1 :]
                arrive(
                    inflight[unit], target(unit, core, 1 - side, landed), across(p, count, bits)
                )
            if step < count:
                held = target(unit, core, 1 - side, everything[:step] + bits[step:])
                inflight[unit] = start(held, held, across(step, count, bits))
            else:
                held = target(unit, core, 1 - side, everything)
                passed[unit] = start(held, held, sibling)
        if tick >= count + 2 and tick % 2 == 1 and waiting:
            finish_direct(waiting.pop(0))
    for unit in waiting:
        finish_direct(unit)
    for unit in range(UNITS):
        arrive(own[unit], target(unit, 1 - core, side, everything), sibling)
        arrive(passed[unit], target(unit, 1 - core, 1 - side, everything), sibling)
        stores[unit].wait()
    small_copy.wait()
    arrive(small_at[0], osmall.at[1 - core, side], sibling)
    arrive(small_at[1], osmall.at[core, 1 - side], facing)
    arrive(small_at[2], osmall.at[1 - core, 1 - side], corner)
    for copy in sends:
        copy.wait_send()


def gather_weights(shards, small, count):
    cut = (2,) * count
    rows = 512 // (1 << count)
    wq, wk, wv, wo, w1, w2 = shards
    narrow = cut + (rows, 1024)
    args = (
        [w.reshape(narrow) for w in (wq, wk, wv, wo)]
        + [w1.reshape(cut + (rows, 4096)), w2.reshape((4,) + narrow), small]
    )
    outs = (
        [jax.ShapeDtypeStruct((2, 2) + narrow, jnp.bfloat16)] * 4
        + [
            jax.ShapeDtypeStruct((2, 2) + cut + (rows, 4096), jnp.bfloat16),
            jax.ShapeDtypeStruct((2, 2, 4) + narrow, jnp.bfloat16),
            jax.ShapeDtypeStruct((2, 2) + small.shape, small.dtype),
        ]
    )
    copies = len(DOUBLED) * (count + 3) + len(DIRECT) * 3 + 3

    def kernel(*refs):
        args, outs, scratch = refs[:7], refs[7:14], refs[14:]
        flat = (scratch[0],) + scratch[1:]
        gather_kernel(count, *args, *outs, *flat)

    result = pl.pallas_call(
        kernel,
        out_shape=outs,
        in_specs=[pl.BlockSpec(memory_space=pl.ANY)] * 7,
        out_specs=[pl.BlockSpec(memory_space=pl.ANY)] * 7,
        scratch_shapes=[
            pltpu.VMEM((UNITS,) + narrow, jnp.bfloat16),
            pltpu.SemaphoreType.DMA((copies,)),
            pltpu.SemaphoreType.DMA((copies,)),
            pltpu.SemaphoreType.DMA((UNITS,)),
            pltpu.SemaphoreType.DMA((UNITS + 1,)),
        ],
        compiler_params=pltpu.CompilerParams(
            collective_id=0, has_side_effects=True, vmem_limit_bytes=VMEM_LIMIT
        ),
        name="gather_weights",
    )(*args)
    full = [w.reshape(2, 1024, 1024) for w in result[:4]]
    full += [result[4].reshape(2, 1024, 4096), result[5].reshape(2, 4096, 1024), result[6]]
    return full


def reduce_kernel(
    count, grads, small,
    total, small_total, landing,
    own, came, across_half, kept, from_x, *rest
):
    halves, rest = rest[:count], rest[count:]
    (small_own, small_recv, send0, recv0, send_x, recv_x, send_rs, recv_rs, send_ag, recv_ag,
     load_sem, came_sem, piece_sem, small_send, small_arrive) = rest
    core = lax.axis_index("section")
    side = lax.axis_index("shard")
    bits = my_bits(count)
    sibling = {"section": 1 - core}
    facing = {"shard": 1 - side}
    everything = (slice(None),) * count
    rows = kept.shape[-2]
    greet([sibling, facing] + [across(p, count, bits) for p in range(count)])

    def core_copy(unit):
        return remote(
            grads.at[1 - core, :, unit], landing.at[unit], send0.at[unit], recv0.at[unit], sibling
        )

    def x_copy(unit):
        return remote(
            across_half.at[unit], from_x.at[unit], send_x.at[unit], recv_x.at[unit], facing
        )

    def rs_copy(unit, p):
        return remote(
            kept.at[(unit,) + everything[:p] + (1 - bits[p],) + bits[p + 1 :]],
            halves[p].at[unit],
            send_rs.at[p, unit],
            recv_rs.at[p, unit],
            across(p, count, bits),
        )

    def ag_copy(unit, p):
        where = (unit,) + everything[:p] + bits[p:]
        source = kept.at[(unit,) + bits] if p == 0 else total.at[where]
        return remote(
            source, total.at[where], send_ag.at[p, unit], recv_ag.at[p, unit],
            across(p, count, bits),
        )

    def ag_arrive(unit, p):
        where = total.at[(unit,) + everything[:p] + (1 - bits[p],) + bits[p + 1 :]]
        remote(
            where, where, send_ag.at[p, unit], recv_ag.at[p, unit], across(p, count, bits)
        ).wait_recv()

    def piece_copy(unit):
        return pltpu.make_async_copy(
            kept.at[(unit,) + bits], total.at[(unit,) + bits], piece_sem.at[unit]
        )

    def own_load(unit):
        slot = lax.rem(unit, 2)
        return pltpu.make_async_copy(grads.at[core, :, unit], own.at[slot], load_sem.at[slot])

    def small_copy(step):
        partner = [sibling, facing] + [across(p, count, bits) for p in range(count)]
        source = small.at[1 - core] if step == 0 else small_own.at[step - 1]
        return remote(
            source, small_recv.at[step], small_send.at[step], small_arrive.at[step], partner[step]
        )

    small_copy(0).start()

    def first(unit, carry):
        core_copy(unit).start()
        return carry

    lax.fori_loop(0, UNITS, first, 0)
    own_load(0).start()
    small_steps = count + 2

    def tick(now, carry):
        for step in range(small_steps):
            @pl.when(now == step + 1)
            def _():
                small_copy(step).wait_recv()
                before = small[core] if step == 0 else small_own[step - 1]
                small_own[step] = before + small_recv[step]
                if step + 1 < small_steps:
                    small_copy(step + 1).start()

        @pl.when(now < UNITS)
        def _():
            unit = now
            slot = lax.rem(unit, 2)

            @pl.when(unit + 1 < UNITS)
            def _():
                own_load(unit + 1).start()

            core_copy(unit).wait_recv()
            arrived = pltpu.make_async_copy(landing.at[unit], came, came_sem)
            arrived.start()
            own_load(unit).wait()
            arrived.wait()
            def add(block, c):
                where = pl.ds(pl.multiple_of(block * 32, 32), 32)
                across_half[unit, where] = own[slot, 1 - side, where] + came[1 - side, where]
                return c

            lax.fori_loop(0, 16, add, 0)
            x_copy(unit).start()

            def add_kept(index, c):
                where = pl.ds(pl.multiple_of(index * rows, rows), rows)
                places = tuple(
                    (lax.rem(index // (1 << (count - 1 - p)), 2) for p in range(count))
                )
                kept[(unit,) + places] = own[slot, side, where] + came[side, where]
                return c

            lax.fori_loop(0, 1 << count, add_kept, 0)

        @pl.when(jnp.logical_and(now >= 1, now < UNITS + 1))
        def _():
            unit = now - 1
            x_copy(unit).wait_recv()

            def add(index, c):
                where = pl.ds(pl.multiple_of(index * rows, rows), rows)
                places = tuple(
                    (lax.rem(index // (1 << (count - 1 - p)), 2) for p in range(count))
                )
                kept[(unit,) + places] = kept[(unit,) + places] + from_x[unit, where]
                return c

            lax.fori_loop(0, 1 << count, add, 0)
            rs_copy(unit, count - 1).start()

        for step in range(count):
            p = count - 1 - step

            @pl.when(jnp.logical_and(now >= 2 + step, now < UNITS + 2 + step))
            def _():
                unit = now - (2 + step)
                rs_copy(unit, p).wait_recv()

                def add(index, c):
                    places = tuple((lax.rem(index // (1 << (p - 1 - q)), 2) for q in range(p)))
                    mine = (unit,) + places + bits[p:]
                    kept[mine] = kept[mine] + halves[p][(unit,) + places]
                    return c

                if p == 0:
                    add(0, 0)
                    piece_copy(unit).start()
                    ag_copy(unit, 0).start()
                else:
                    lax.fori_loop(0, 1 << p, add, 0)
                    rs_copy(unit, p - 1).start()

        for p in range(count):
            lag = 2 + count + p

            @pl.when(jnp.logical_and(now >= lag, now < UNITS + lag))
            def _():
                unit = now - lag
                ag_arrive(unit, p)
                if p == 0:
                    piece_copy(unit).wait()
                if p + 1 < count:
                    ag_copy(unit, p + 1).start()

        return carry

    lax.fori_loop(0, UNITS + 2 + 2 * count, tick, 0)
    out = pltpu.make_async_copy(small_own.at[small_steps - 1], small_total, piece_sem.at[UNITS])
    out.start()

    def last(unit, carry):
        core_copy(unit).wait_send()
        x_copy(unit).wait_send()
        for p in range(count):
            rs_copy(unit, p).wait_send()
            ag_copy(unit, p).wait_send()
        return carry

    lax.fori_loop(0, UNITS, last, 0)
    for step in range(small_steps):
        small_copy(step).wait_send()
    out.wait()


def reduce_grads(grads, small, count):
    cut = (2,) * count
    rows = 512 // (1 << count)
    narrow = cut + (rows, 1024)
    dma = pltpu.SemaphoreType.DMA

    def kernel(*refs):
        reduce_kernel(count, *refs)

    vectors = small.shape[1:]
    total, small_total, _ = pl.pallas_call(
        kernel,
        out_shape=[
            jax.ShapeDtypeStruct((UNITS,) + narrow, jnp.bfloat16),
            jax.ShapeDtypeStruct(vectors, jnp.float32),
            jax.ShapeDtypeStruct((UNITS, 2, 512, 1024), jnp.bfloat16),
        ],
        in_specs=[
            pl.BlockSpec(memory_space=pl.ANY),
            pl.BlockSpec(memory_space=pltpu.VMEM),
        ],
        out_specs=[pl.BlockSpec(memory_space=pl.ANY)] * 3,
        scratch_shapes=[
            pltpu.VMEM((2, 2, 512, 1024), jnp.bfloat16),
            pltpu.VMEM((2, 512, 1024), jnp.bfloat16),
            pltpu.VMEM((UNITS, 512, 1024), jnp.bfloat16),
            pltpu.VMEM((UNITS,) + narrow, jnp.bfloat16),
            pltpu.VMEM((UNITS, 512, 1024), jnp.bfloat16),
        ]
        + [pltpu.VMEM((UNITS,) + (2,) * p + (rows, 1024), jnp.bfloat16) for p in range(count)]
        + [
            pltpu.VMEM((count + 2,) + vectors, jnp.float32),
            pltpu.VMEM((count + 2,) + vectors, jnp.float32),
            dma((UNITS,)),
            dma((UNITS,)),
            dma((UNITS,)),
            dma((UNITS,)),
            dma((count, UNITS)),
            dma((count, UNITS)),
            dma((count, UNITS)),
            dma((count, UNITS)),
            dma((2,)),
            dma,
            dma((UNITS + 1,)),
            dma((count + 2,)),
            dma((count + 2,)),
        ],
        compiler_params=pltpu.CompilerParams(
            collective_id=1, has_side_effects=True, vmem_limit_bytes=VMEM_LIMIT
        ),
        name="reduce_grads",
    )(grads, small)
    return total.reshape(UNITS, 512, 1024), small_total
from jax.sharding import PartitionSpec as P

HEAD_DIM = 64
EPSILON = 1e-12
MASKED = -1000000000.0
VECTORS = (1, 1, 1, 1, 1, 4, 1, 1, 1)


def dense(left_side, right_side):
    return jnp.dot(left_side, right_side, preferred_element_type=jnp.float32)


def dense_left(left_side, right_side):
    return jnp.einsum("ra,rb->ab", left_side, right_side, preferred_element_type=jnp.float32)


def dense_right(left_side, right_side):
    return jnp.einsum("rb,ab->ra", left_side, right_side, preferred_element_type=jnp.float32)


def normalized(values):
    average = jnp.mean(values, axis=-1, keepdims=True)
    centred = values - average
    variance = jnp.mean(centred * centred, axis=-1, keepdims=True)
    scale = lax.rsqrt(variance + EPSILON)
    return centred * scale, scale


def normalize_back(grad, unit, scale, gain):
    gs = grad * gain
    mean_gs = jnp.mean(gs, axis=-1, keepdims=True)
    mean_gn = jnp.mean(gs * unit, axis=-1, keepdims=True)
    return (gs - mean_gs - unit * mean_gn) * scale


def layer_forward(x, live, params):
    wq, wk, wv, wo, w1, w2, (bq, bv, bo, g1, b1, bi, b2, g2, bb2) = params
    slots = x.shape[0]
    heads = (slots, 16, HEAD_DIM)
    q = (dense(x, wq) + bq).astype(jnp.bfloat16).reshape(heads)
    k = dense(x, wk).astype(jnp.bfloat16).reshape(heads)
    v = (dense(x, wv) + bv).astype(jnp.bfloat16).reshape(heads)
    scores = jnp.einsum("qhd,khd->hqk", q, k, preferred_element_type=jnp.float32) * 0.125
    scores = jnp.where(live[None, None, :], scores, MASKED)
    highest = jnp.max(scores, axis=-1, keepdims=True)
    exponent = jnp.exp(scores - highest)
    totals = jnp.sum(exponent, axis=-1, keepdims=True)
    probs = (exponent / totals).astype(jnp.bfloat16)
    log_total = highest + jnp.log(totals)
    context = jnp.einsum("hqk,khd->qhd", probs, v, preferred_element_type=jnp.float32)
    context = context.astype(jnp.bfloat16).reshape(slots, -1)
    first_sum = x.astype(jnp.float32) + (dense(context, wo) + bo)
    unit1, scale1 = normalized(first_sum)
    middle = unit1 * g1 + b1
    middle_low = middle.astype(jnp.bfloat16)
    inner = dense(middle_low, w1) + bi
    cdf = 0.5 * (1.0 + lax.erf(inner * 0.7071067811865476))
    activated = (inner * cdf).astype(jnp.bfloat16)
    slope = (cdf + inner * (jnp.exp(-0.5 * inner * inner) * 0.3989422804014327)).astype(
        jnp.bfloat16
    )
    second_sum = middle + (dense(activated, w2) + b2)
    unit2, scale2 = normalized(second_sum)
    row_mask = live[:, None].astype(jnp.float32)
    result = ((unit2 * g2 + bb2) * row_mask).astype(jnp.bfloat16)
    return result, (q, k, v, log_total, context, unit1, scale1, middle_low, activated, slope, unit2, scale2)


def layer_backward(grad, x, live, params, stored):
    wq, wk, wv, wo, w1, w2, (bq, bv, bo, g1, b1, bi, b2, g2, bb2) = params
    q, k, v, log_total, context, unit1, scale1, middle_low, activated, slope, unit2, scale2 = stored
    slots = x.shape[0]
    heads = (slots, 16, HEAD_DIM)
    g = grad.astype(jnp.float32) * live[:, None].astype(jnp.float32)
    d_second = normalize_back(g, unit2, scale2, g2)
    d_g2, d_bb2 = jnp.sum(g * unit2, axis=0), jnp.sum(g, axis=0)
    d_outer = d_second.astype(jnp.bfloat16)
    d_inner = (dense_right(d_outer, w2) * slope.astype(jnp.float32)).astype(jnp.bfloat16)
    d_middle = d_second + dense_right(d_inner, w1)
    d_first = normalize_back(d_middle, unit1, scale1, g1)
    d_g1, d_b1 = jnp.sum(d_middle * unit1, axis=0), jnp.sum(d_middle, axis=0)
    d_att = d_first.astype(jnp.bfloat16)
    d_context = dense_right(d_att, wo).astype(jnp.bfloat16).reshape(heads)
    scores = jnp.einsum("qhd,khd->hqk", q, k, preferred_element_type=jnp.float32) * 0.125
    scores = jnp.where(live[None, None, :], scores, MASKED)
    probs = jnp.exp(scores - log_total)
    d_v = jnp.einsum(
        "hqk,qhd->khd", probs.astype(jnp.bfloat16), d_context, preferred_element_type=jnp.float32
    )
    d_v = d_v.astype(jnp.bfloat16).reshape(slots, -1)
    d_probs = jnp.einsum("qhd,khd->hqk", d_context, v, preferred_element_type=jnp.float32)
    dots = jnp.sum(probs * d_probs, axis=-1, keepdims=True)
    d_scores = (probs * (d_probs - dots)).astype(jnp.bfloat16)
    d_q = jnp.einsum("hqk,khd->qhd", d_scores, k, preferred_element_type=jnp.float32) * 0.125
    d_k = jnp.einsum("hqk,qhd->khd", d_scores, q, preferred_element_type=jnp.float32) * 0.125
    d_q = d_q.astype(jnp.bfloat16).reshape(slots, -1)
    d_k = d_k.astype(jnp.bfloat16).reshape(slots, -1)
    d_x = d_first + dense_right(d_q, wq) + dense_right(d_k, wk) + dense_right(d_v, wv)

    def sums(values):
        return jnp.sum(values, axis=0, dtype=jnp.float32)

    vectors = (
        sums(d_q), sums(d_v), sums(d_att), d_g1, d_b1, sums(d_inner), sums(d_outer), d_g2, d_bb2
    )
    matrices = [
        dense_left(x, d_q), dense_left(x, d_k), dense_left(x, d_v), dense_left(context, d_att),
        dense_left(middle_low, d_inner), dense_left(activated, d_outer),
    ]
    low = [m.astype(jnp.bfloat16) for m in matrices]
    packed = [m.reshape(2, 1, 512, 1024) for m in low[:4]]
    packed += [low[4].reshape(2, 512, 4, 1024).transpose(0, 2, 1, 3), low[5].reshape(2, 4, 512, 1024)]
    return (
        d_x.astype(jnp.bfloat16),
        jnp.concatenate(packed, axis=1),
        jnp.concatenate([v.reshape(2, -1) for v in vectors], axis=1).reshape(96, 128),
    )


def split_vectors(packed):
    halves = packed.reshape(2, -1)
    out, at = [], 0
    for width in VECTORS:
        out.append(halves[:, at : at + 512 * width].reshape(-1).astype(jnp.float32))
        at += 512 * width
    return tuple(out)


def device_of(number, groups):
    return lax.rem(number, 2) * groups + number // 2


def own_cotangent(cotangent, permutation, groups):
    core = lax.axis_index("section")
    total = permutation.shape[0]
    mine = lax.dynamic_index_in_dim(cotangent, core, 0, keepdims=False)
    shape = mine.shape
    chunks = mine.reshape(2 * groups, shape[0] // (2 * groups), shape[1])
    spread = lax.all_to_all(chunks, ALL, 0, 0, tiled=True)
    device = jnp.arange(total, dtype=jnp.int32)
    number = 2 * lax.rem(device, groups) + device // groups
    slot = jnp.sum(
        jnp.where(permutation[None, :] == number[:, None], device[None, :], 0), axis=1
    )
    ordered = jnp.take(spread, device_of(slot, groups), axis=0)
    return lax.all_to_all(ordered, ALL, 0, 0, tiled=True).reshape(shape)


def dealt_grads(both, permutation, groups):
    slots, width = both.shape[1:]
    rows = slots // groups
    spread = lax.all_to_all(both.reshape(2 * groups, rows, width), ALL, 0, 0, tiled=True)
    ordered = jnp.take(spread, device_of(permutation, groups), axis=0)
    ordered = ordered.reshape(groups, 2, rows, width)
    home = lax.all_to_all(ordered, GROUP, 0, 0, tiled=True)
    return home.transpose(1, 0, 2, 3).reshape(2, slots, width)


def on_device(
    inputs, cotangent, lengths, permutation, query_weight, query_bias, key_weight, value_weight,
    value_bias, output_weight, output_bias, first_gain, first_bias, inner_weight, inner_bias,
    outer_weight, outer_bias, second_gain, second_bias,
):
    core = lax.axis_index("section")
    group = lax.axis_index(GROUP)
    groups = lax.axis_size(GROUP)
    count = lax.axis_size("replica").bit_length() - 1
    slots = inputs.shape[1]
    shards = [
        w[0] for w in (query_weight, key_weight, value_weight, output_weight, inner_weight, outer_weight)
    ]
    vectors = [
        v[0] for v in (query_bias, value_bias, output_bias, first_gain, first_bias, inner_bias,
                       outer_bias, second_gain, second_bias)
    ]
    full = gather_weights(shards, jnp.concatenate(vectors).reshape(48, 128), count)
    layers = [tuple(w[s] for w in full[:6]) + (split_vectors(full[6][s]),) for s in range(2)]
    length = lax.dynamic_index_in_dim(lengths, 2 * group + core, 0, keepdims=False)
    live = jnp.arange(slots, dtype=jnp.int32) < length
    x = lax.dynamic_index_in_dim(inputs, core, 0, keepdims=False)
    grad = own_cotangent(cotangent, permutation, groups)
    lower, lower_stored = layer_forward(x, live, layers[0])
    upper, upper_stored = layer_forward(lower, live, layers[1])
    upper_grad, upper_packed, upper_small = layer_backward(grad, lower, live, layers[1], upper_stored)
    lower_grad, lower_packed, lower_small = layer_backward(
        upper_grad, x, live, layers[0], lower_stored
    )
    total, small = reduce_grads(
        jnp.stack([lower_packed, upper_packed]), jnp.stack([lower_small, upper_small]), count
    )
    sent = jnp.where(core == 0, upper, lower)
    kept = jnp.where(core == 0, lower, upper)
    came = lax.ppermute(sent, "section", [(0, 1), (1, 0)])
    activations = jnp.where(core == 0, jnp.stack([kept, came]), jnp.stack([came, kept]))[None]
    input_grads = dealt_grads(jnp.stack([lower_grad, upper_grad]), permutation, groups)[None]
    wide = total.astype(jnp.float32)
    side = lax.axis_index("shard")
    own = lax.dynamic_index_in_dim(small.reshape(2, -1), side, 0, keepdims=False)
    pieces, at = [], 0
    for width in VECTORS:
        pieces.append(own[None, at : at + 512 * width])
        at += 512 * width
    dq, dk, dv, do = (wide[i][None] for i in range(4))
    d1 = wide[4:8].transpose(1, 0, 2).reshape(1, 512, 4096)
    d2 = wide[8:12].reshape(1, 2048, 1024)
    return (
        activations, input_grads, dq, pieces[0], dk, dv, pieces[1], do, pieces[2], pieces[3],
        pieces[4], d1, pieces[5], d2, pieces[6], pieces[7], pieces[8],
    )


def solution(mesh):
    matrix, vector = P("section", "shard", None), P("section", "shard")
    rows = P(("shard", "replica"), None, None)
    in_specs = (
        rows, rows, P(), P(), matrix, vector, matrix, matrix, vector, matrix, vector, vector,
        vector, matrix, vector, matrix, vector, vector, vector,
    )
    both = P("section", ("shard", "replica"), None, None)
    out_specs = (
        both, both, matrix, vector, matrix, matrix, vector, matrix, vector, vector, vector,
        matrix, vector, matrix, vector, vector, vector,
    )
    return jax.shard_map(
        on_device, mesh=mesh, in_specs=in_specs, out_specs=out_specs, check_vma=False
    )
```

time: 2500 us -> 1120 us (0.45)
  waiting for transfers between devices: 1780 us -> 16.4 us
  Pallas kernels: 0 us -> 521 us
  local copies, waits for them, and re-layouts: 82.3 us -> 200 us
  blocking collectives: 87.6 us -> 0 us
  other arithmetic: 191 us -> 106 us
  matrix products: 306 us -> 242 us
    all_gather x8 -> x0, waiting for transfers between devices: 986 us -> none  [the longest x1 333 us: on_device(): lax.all_gather(dealt_outputs, ('shard', 'replica'), axis=0, tiled=True)]
    pallas_call x0 -> x2, Pallas kernels: none -> 521 us  [the longest x1 375 us: reduce_grads(): pl.pallas_call(kernel, out_shape=[jax.ShapeDtypeStruct((UNITS,) + narrow,...]
    psum x1 -> x0, waiting for transfers between devices: 337 us -> none  [on_device(): lax.psum(owned_part[0].astype(jnp.bfloat16), 'replica').astype(jnp.float32)]
    reduce_scatter x6 -> x0, waiting for transfers between devices: 279 us -> none  [the longest x1 102 us: on_device(): lax.psum_scatter(gradients[9].astype(jnp.bfloat16), 'shard', scatter_dime...]
    ppermute x4 -> x1, waiting for transfers between devices: 178 us -> 0.77 us  [on_device(): came = lax.ppermute(sent, 'section', [(0, 1), (1, 0)])]
    dot_general x12, matrix products: 101 us -> 49.4 us  [dense(): return jnp.dot(left_side, right_side, preferred_element_type=jnp.float32)]
    slice x2 -> x8, local copies, waits for them, and re-layouts: 1.65 us -> 53.1 us  [the longest x4 33.9 us: on_device(): w[s]]
    unnamed x220 -> x281, local copies, waits for them, and re-layouts: 7.7 us -> 55.2 us
  transfers between devices with their start and end apart: 19 -> 5, of which waited for: 16 -> 2; matrix products, arithmetic and copies ran while one was open for 6% -> 30% of each run, Pallas kernels for 0% -> 47%
where the time goes in v1:
time: 1120 us; the launch traced here: 1110 us
  Pallas kernels  521 us (47%)
  matrix products  242 us (22%)
  local copies, waits for them, and re-layouts  200 us (18%)
  other arithmetic  106 us (9%)
  starting transfers between devices  26.1 us (2%)
  waiting for transfers between devices  16.4 us (1%)
    pallas_call x1, Pallas kernels, reduce_grads(): pl.pallas_call(kernel, out_shape=[jax.ShapeDtypeStruct((UNITS,) + narrow,...  375 us
    pallas_call x1, Pallas kernels, gather_weights(): pl.pallas_call(kernel, out_shape=outs, in_specs=[pl.BlockSpec(memory_spac...  146 us
    dot_general x12, matrix products, dense_left(): jnp.einsum('ra,rb->ab', left_side, right_side, preferred_element_type=jnp...  55.8 us
    dot_general x12, matrix products, dense_right(): jnp.einsum('rb,ab->ra', left_side, right_side, preferred_element_type=jnp...  55.3 us
    unnamed x281, local copies, waits for them, and re-layouts  55.2 us
    dot_general x12, matrix products, dense(): return jnp.dot(left_side, right_side, preferred_element_type=jnp.float32)  49.4 us
    slice x4, local copies, waits for them, and re-layouts, on_device(): w[s]  33.9 us
    another operation x1, other arithmetic, on_device(): jnp.stack([lower_packed, upper_packed])  33.7 us
  transfers between devices with their start and end apart: 5, of which 2 were waited for; matrix products, arithmetic and copies ran while one was open for 30% of the time, Pallas kernels for 47%

profile of v1, /device:TPU:0, one launch (start us, length us, event | category | flops | bytes accessed | tf_op | source)
XLA Modules:
  0.0 1113.6 jit_solution(1159284494742985569)
XLA Ops:
  13.7 145.8 %gather_weights.1 = (bf16[2,2,2,2,2,64,1024]{6,5,4,3,2,1,0:T(8,128)(2,1)}, bf16[2,2,2,2,2,64,1024]{6,5,4,3,2,1,0:T(8,128)(2,1)}, bf16[2,2,2,2,2,64,1024]{6,5,4,3...) custom-call(bf16[2,2,2,64,1024]{4,3,2,1,0:T(8,128)(2,1)} %bitcast.35, ...), custom_call_target="tpu_custom_call" | custom-call | tf_op jit(solution)/shard_map/gather_weights/pallas_call | solution.py:181
  162.9 13.0 %fusion.76 = (bf16[1,2,2,2,2,64,4096]{6,5,4,3,2,1,0:T(8,128)(2,1)}, bf16[1,2,2,2,2,64,4096]{6,5,4,3,2,1,0:T(8,128)(2,1)}) fusion(bf16[2,2,2,2,2,64,4096]{6,5,4,3,2,1,0:T(8,128)(2,1)} %get-tuple-element.31), kind=kLoop, calls=%fused_computation.267 | loop fusion | bytes 33554432 | tf_op jit(solution)/shard_map/slice | solution.py:620
  198.0 7.8 fusion.84
  205.8 8.3 fusion
  223.6 11.9 %fusion.75 = (bf16[1,2,4,2,2,2,64,1024]{7,6,5,4,3,2,1,0:T(8,128)(2,1)}, bf16[1,2,4,2,2,2,64,1024]{7,6,5,4,3,2,1,0:T(8,128)(2,1)S(1)}) fusion(bf16[2,2,4,2,2,2,64,1024]{7,6,5,4,3,2,1,0:T(8,128)(2,1)} %get-tuple-element.32), kind=kLoop, calls=%fused_computation.266 | loop fusion | bytes 33554432 | tf_op jit(solution)/shard_map/slice | solution.py:620
  235.6 9.3 multiply_convert_fusion.5
  267.9 9.3 fusion.87
  277.2 8.4 fusion.1
  296.4 9.9 multiply_convert_fusion.4
  315.9 8.5 all-to-all-start.1
  336.3 15.6 %all-to-all-done.1 = bf16[32,16,1024]{2,1,0:T(8,128)(2,1)S(1)} async-done(((bf16[32,16,1024]{2,1,0:T(8,128)(2,1)}), bf16[32,16,1024]{2,1,0:T(8,128)(2,1)S(1)}, u32[]{:S(2)}, u32[]{:S(2)}) %all-to-all-start.1) | async-done | bytes 1048608 | tf_op jit(solution)/shard_map/all_to_all | solution.py:589
  359.0 12.1 %convert_reduce_fusion = (f32[4096]{0:T(1024)}, bf16[512,4096]{1,0:T(8,128)(2,1)S(1)}) fusion(f32[512,4096]{1,0:T(8,128)} %get-tuple-element.120, f32[4096]{0:T(1024)S(1)} %bitcast.390, bf16[4096,1024]{1,0:T(8,128)(2,1)} %bitcast.302, f32[512,1024]{1,0:T(8,128)S(1)} %get-tuple-element.56), kind=kOutput, calls=%fused_computation.35 | convolution fusion | flops 4326944768 | bytes 23101440 | tf_op jit(solution)/shard_map/rb,ab->ra/dot_general | solution.py:461
  371.2 9.8 multiply_reduce_fusion.3
  387.8 9.2 convert_reduce_fusion.4
  397.0 11.4 %multiply_reduce_fusion.1 = (f32[16,512]{1,0:T(8,128)S(1)}, f32[16,512,512]{1,2,0:T(8,128)}) fusion(f32[16,512,512]{1,2,0:T(8,128)} %get-tuple-element.116, f32[16,512]{1,0:T(8,128)S(1)} %log_add_fusion.1, bf16[512,16,64]{0,2,1:T(8,128)(2,1)S(1)} %bitcast.278, bf16[512,16,64]{0,2,1:T(8,128)(2,1)S(1)} %bitcast.324), kind=kOutput, calls=%fused_computation.7 | convolution fusion | flops 549445632 | bytes 35717120 | tf_op jit(solution)/shard_map/qhd,khd->hqk/dot_general | solution.py:534
  408.4 11.8 %multiply_convert_fusion.1 = bf16[16,512,512]{1,2,0:T(8,128)(2,1)S(1)} fusion(f32[16,512,512]{1,2,0:T(8,128)} %get-tuple-element.125, f32[16,512,512]{1,2,0:T(8,128)} %get-tuple-element.116, f32[16,512]{1,0:T(8,128)S(1)} %get-tuple-element.124, f32[16,512]{1,0:T(8,128)S(1)} %log_add_fusion.1), kind=kLoop, calls=%fused_computation.6 | loop fusion | flops 16777216 | bytes 42008576 | tf_op jit(solution)/shard_map/convert_element_type | solution.py:536
  433.8 11.3 %convert_reduce_fusion.1 = (f32[4096]{0:T(1024)S(1)}, bf16[512,4096]{1,0:T(8,128)(2,1)}) fusion(f32[512,4096]{1,0:T(8,128)} %get-tuple-element.112, f32[4096]{0:T(1024)S(1)} %bitcast.388, bf16[4096,1024]{1,0:T(8,128)(2,1)S(1)} %bitcast.299, f32[512,1024]{1,0:T(8,128)} %get-tuple-element.52), kind=kOutput, calls=%fused_computation.36 | convolution fusion | flops 4326944768 | bytes 23101440 | tf_op jit(solution)/shard_map/rb,ab->ra/dot_general | solution.py:461
  445.1 8.0 multiply_reduce_fusion.5
  459.0 8.6 convert_reduce_fusion.8
  467.6 11.2 %multiply_reduce_fusion = (f32[16,512]{1,0:T(8,128)S(1)}, f32[16,512,512]{1,2,0:T(8,128)}) fusion(f32[16,512,512]{1,2,0:T(8,128)} %get-tuple-element.108, f32[16,512]{1,0:T(8,128)S(1)} %log_add_fusion, bf16[512,16,64]{0,2,1:T(8,128)(2,1)S(1)} %bitcast.280, bf16[512,16,64]{0,2,1:T(8,128)(2,1)S(1)} %bitcast.322), kind=kOutput, calls=%fused_computation.4 | convolution fusion | flops 549445632 | bytes 35717120 | tf_op jit(solution)/shard_map/qhd,khd->hqk/dot_general | solution.py:534
  478.9 11.8 %multiply_convert_fusion = bf16[16,512,512]{1,2,0:T(8,128)(2,1)S(1)} fusion(f32[16,512,512]{1,2,0:T(8,128)} %get-tuple-element.129, f32[16,512,512]{1,2,0:T(8,128)} %get-tuple-element.108, f32[16,512]{1,0:T(8,128)S(1)} %get-tuple-element.128, f32[16,512]{1,0:T(8,128)S(1)} %log_add_fusion), kind=kLoop, calls=%fused_computation.3 | loop fusion | flops 16777216 | bytes 42008576 | tf_op jit(solution)/shard_map/convert_element_type | solution.py:536
  543.6 14.5 %reshape.719 = bf16[2,512,4,1024]{3,2,1,0:T(4,128)(2,1)} reshape(bf16[1024,4096]{1,0:T(8,128)(2,1)} %convolution_convert_fusion.1) | data formatting | bytes 16777216 | tf_op jit(solution)/shard_map/reshape | solution.py:555
  569.3 9.7 bitcast_dynamic-update-slice_fusion
  585.9 14.7 %reshape.713 = bf16[2,512,4,1024]{3,2,1,0:T(4,128)(2,1)} reshape(bf16[1024,4096]{1,0:T(8,128)(2,1)} %convolution_convert_fusion.3) | data formatting | bytes 16777216 | tf_op jit(solution)/shard_map/reshape | solution.py:555
  600.6 10.8 convolution_convert_fusion
  619.1 9.8 bitcast_dynamic-update-slice_fusion.1
  628.9 9.0 convolution_convert_fusion.2
  658.0 33.7 %pad_maximum_fusion.refs_0_ = bf16[2,2,12,512,1024]{4,3,2,1,0:T(8,128)(2,1)} fusion(bf16[1,2,12,512,1024]{4,3,2,1,0:T(8,128)(2,1)} %bitcast.272, bf16[1,2,12,512,1024]{4,3,2,1,0:T(8,128)(2,1)} %bitcast.271), kind=kLoop, calls=%fused_computation.2 | loop fusion | flops 25165824 | bytes 100663296 | tf_op jit(solution)/shard_map/stack | solution.py:632
  691.7 375.2 %reduce_grads.1 = (bf16[12,2,2,2,64,1024]{5,4,3,2,1,0:T(8,128)(2,1)}, f32[96,128]{1,0:T(8,128)}, bf16[12,2,512,1024]{3,2,1,0:T(8,128)(2,1)}) custom-call(bf16[2,2,12,512,1024]{4,3,2,1,0:T(8,128)(2,1)} %pad_maximum_fusion.refs_0_, f32[2,96,128]{2,1,0:T(8,128)} %pad_maximum_fusion.2.refs_1_), custom_call_target="tpu_custom_call" | custom-call | tf_op jit(solution)/shard_map/reduce_grads/pallas_call | solution.py:401
  1067.8 11.8 %fusion.77 = (f32[4,2,2,2,64,1024]{5,4,3,2,1,0:T(8,128)}, f32[4,2,2,2,64,1024]{5,4,3,2,1,0:T(8,128)}) fusion(bf16[12,2,2,2,64,1024]{5,4,3,2,1,0:T(8,128)(2,1)} %get-tuple-element.33), kind=kLoop, calls=%fused_computation.268 | loop fusion | bytes 33554432 | tf_op jit(solution)/shard_map/slice | solution.py:648
  1079.7 12.0 %copy.142 = f32[512,4,1024]{2,1,0:T(4,128)} copy(f32[512,4,1024]{2,0,1:T(8,128)} %bitcast.270) | data formatting | bytes 16777216 | tf_op jit(solution)/shard_map/transpose | solution.py:647
  1091.7 10.9 reshape.740
  (432 shorter events, 245.5 us)
Async XLA Ops:
  3.4 309.5 %all-to-all-start = ((bf16[32,16,1024]{2,1,0:T(8,128)(2,1)}), bf16[32,16,1024]{2,1,0:T(8,128)(2,1)}, u32[]{:S(2)}, u32[]{:S(2)}) async-start(bf16[32,16,1024]{2,1,0:T(8,128)(2,1)} %bitcast.33), calls=%async_computation | async-start | bytes 2097152 | tf_op jit(solution)/shard_map/all_to_all | solution.py:582
  13.7 147.2 %copy-start.99 = (s32[32]{0:T(128)S(1)}, s32[32]{0:T(128)}, u32[]{:S(2)}) copy-start(s32[32]{0:T(128)} %param.21) | copy-start | bytes 388
  162.9 13.1 %copy-start.40 = (bf16[2,2,2,2,2,64,1024]{6,5,4,3,2,1,0:T(8,128)(2,1)S(1)}, bf16[2,2,2,2,2,64,1024]{6,5,4,3,2,1,0:T(8,128)(2,1)}, u32[]{:S(2)}) copy-start(bf16[2,2,2,2,2,64,1024]{6,5,4,3,2,1,0:T(8,128)(2,1)} %get-tuple-element.28) | copy-start | bytes 12582916
  162.9 13.1 %copy-start.41 = (bf16[2,2,2,2,2,64,1024]{6,5,4,3,2,1,0:T(8,128)(2,1)S(1)}, bf16[2,2,2,2,2,64,1024]{6,5,4,3,2,1,0:T(8,128)(2,1)}, u32[]{:S(2)}) copy-start(bf16[2,2,2,2,2,64,1024]{6,5,4,3,2,1,0:T(8,128)(2,1)} %get-tuple-element.26) | copy-start | bytes 12582916
  175.9 59.6 %copy-start.77 = (f32[1,16,2,128]{3,1,2,0:T(8,128)}, f32[1,16,2,128]{3,1,2,0:T(8,128)S(1)}, u32[]{:S(2)}) copy-start(f32[1,16,2,128]{3,1,2,0:T(8,128)S(1)} %copy.157) | copy-start | bytes 49156
  182.6 31.5 %copy-start.33 = (bf16[512,1024]{0,1:T(8,128)(2,1)}, bf16[512,1024]{0,1:T(8,128)(2,1)S(1)}, u32[]{:S(2)}) copy-start(bf16[512,1024]{0,1:T(8,128)(2,1)S(1)} %copy.123) | copy-start | bytes 3145732
  198.0 46.9 %copy-start.85 = (f32[1,4,2,128]{3,1,2,0:T(4,128)}, f32[1,4,2,128]{3,1,2,0:T(4,128)S(1)}, u32[]{:S(2)}) copy-start(f32[1,4,2,128]{3,1,2,0:T(4,128)S(1)} %copy.156) | copy-start | bytes 12292
  198.0 46.9 %copy-start.69 = (f32[1,4,2,128]{3,1,2,0:T(4,128)}, f32[1,4,2,128]{3,1,2,0:T(4,128)S(1)}, u32[]{:S(2)}) copy-start(f32[1,4,2,128]{3,1,2,0:T(4,128)S(1)} %copy.155) | copy-start | bytes 12292
  223.2 21.7 %copy-start.3 = (f32[512,1024]{1,0:T(8,128)}, f32[512,1024]{1,0:T(8,128)S(1)}, u32[]{:S(2)}) copy-start(f32[512,1024]{1,0:T(8,128)S(1)} %get-tuple-element.110) | copy-start | bytes 6291460
  223.2 21.7 %copy-start.67 = (f32[512]{0:T(512)}, f32[512]{0:T(512)S(1)}, u32[]{:S(2)}) copy-start(f32[512]{0:T(512)S(1)} %broadcast_multiply_fusion.11) | copy-start | bytes 6148
  223.2 12.3 %slice-start = ((s8[8388608]{0:T(1024)(128)(4,1)}), s8[4194304]{0:T(1024)(128)(4,1)S(1)}, s32[]{:S(2)}) async-start(s8[8388608]{0:T(1024)(128)(4,1)} %bitcast.290), calls=%async_computation.4 | async-start | bytes 8388608
  223.6 21.3 %copy-start.82 = (f32[512]{0:T(512)}, f32[512]{0:T(512)S(1)}, u32[]{:S(2)}) copy-start(f32[512]{0:T(512)S(1)} %add_rsqrt_fusion.3) | copy-start | bytes 6148
  223.6 12.0 %slice-start.1 = ((s8[8388608]{0:T(1024)(128)(4,1)}), s8[4194304]{0:T(1024)(128)(4,1)S(1)}, s32[]{:S(2)}) async-start(s8[8388608]{0:T(1024)(128)(4,1)} %bitcast.290), calls=%async_computation.5 | async-start | bytes 8388608
  250.6 11.9 %copy-start.37 = (bf16[512,1024]{1,0:T(8,128)(2,1)}, bf16[512,1024]{1,0:T(8,128)(2,1)S(1)}, u32[]{:S(2)}) copy-start(bf16[512,1024]{1,0:T(8,128)(2,1)S(1)} %multiply_convert_fusion.11) | copy-start | bytes 3145732
  267.9 38.5 %copy-start.87 = (f32[1,4,2,128]{3,1,2,0:T(4,128)}, f32[1,4,2,128]{3,1,2,0:T(4,128)S(1)}, u32[]{:S(2)}) copy-start(f32[1,4,2,128]{3,1,2,0:T(4,128)S(1)} %copy.166) | copy-start | bytes 12292
  293.3 13.0 %slice-start.6 = ((s8[8388608]{0:T(1024)(128)(4,1)}), s8[4194304]{0:T(1024)(128)(4,1)S(1)}, s32[]{:S(2)}) async-start(s8[8388608]{0:T(1024)(128)(4,1)} %bitcast.303), calls=%async_computation.10 | async-start | bytes 8388608
  294.7 11.6 %copy-start.5 = (f32[512,1024]{1,0:T(8,128)}, f32[512,1024]{1,0:T(8,128)S(1)}, u32[]{:S(2)}) copy-start(f32[512,1024]{1,0:T(8,128)S(1)} %get-tuple-element.118) | copy-start | bytes 6291460
  315.9 36.0 %all-to-all-start.1 = ((bf16[32,16,1024]{2,1,0:T(8,128)(2,1)}), bf16[32,16,1024]{2,1,0:T(8,128)(2,1)S(1)}, u32[]{:S(2)}, u32[]{:S(2)}) async-start(bf16[32,16,1024]{2,1,0:T(8,128)(2,1)} %broadcast_select_fusion.1), calls=%async_computation.1 | async-start | bytes 2097152 | tf_op jit(solution)/shard_map/all_to_all | solution.py:589
  329.3 3.0 collective-permute-start
  359.0 12.1 %copy-start.44 = (f32[512,1024]{1,0:T(8,128)}, f32[512,1024]{1,0:T(8,128)S(1)}, u32[]{:S(2)}) copy-start(f32[512,1024]{1,0:T(8,128)S(1)} %get-tuple-element.56) | copy-start | bytes 6291460
  359.0 12.1 %copy-start.6 = (f32[512,1024]{1,0:T(8,128)S(1)}, f32[512,1024]{1,0:T(8,128)}, u32[]{:S(2)}) copy-start(f32[512,1024]{1,0:T(8,128)} %copy-done.5) | copy-start | bytes 6291460
  397.0 30.7 %copy-start.31 = (bf16[16,64,512]{2,1,0:T(8,128)(2,1)}, bf16[16,64,512]{2,1,0:T(8,128)(2,1)S(1)}, u32[]{:S(2)}) copy-start(bf16[16,64,512]{2,1,0:T(8,128)(2,1)S(1)} %get-tuple-element.133) | copy-start | bytes 3145732
  408.4 11.8 %copy-start.16 = (bf16[512,1024]{0,1:T(8,128)(2,1)S(1)}, bf16[512,1024]{0,1:T(8,128)(2,1)}, u32[]{:S(2)}) copy-start(bf16[512,1024]{0,1:T(8,128)(2,1)} %copy.128) | copy-start | bytes 3145732
  428.6 16.4 %slice-start.2 = ((s8[8388608]{0:T(1024)(128)(4,1)}), s8[4194304]{0:T(1024)(128)(4,1)S(1)}, s32[]{:S(2)}) async-start(s8[8388608]{0:T(1024)(128)(4,1)} %bitcast.293), calls=%async_computation.6 | async-start | bytes 8388608
  433.7 11.4 %copy-start.4 = (f32[512,1024]{1,0:T(8,128)S(1)}, f32[512,1024]{1,0:T(8,128)}, u32[]{:S(2)}) copy-start(f32[512,1024]{1,0:T(8,128)} %copy-done.3) | copy-start | bytes 6291460
  433.7 11.4 %slice-start.3 = ((s8[8388608]{0:T(1024)(128)(4,1)}), s8[4194304]{0:T(1024)(128)(4,1)S(1)}, s32[]{:S(2)}) async-start(s8[8388608]{0:T(1024)(128)(4,1)} %bitcast.293), calls=%async_computation.7 | async-start | bytes 8388608
  433.7 11.4 %copy-start.68 = (f32[512]{0:T(512)S(1)}, f32[512]{0:T(512)}, u32[]{:S(2)}) copy-start(f32[512]{0:T(512)} %copy-done.67) | copy-start | bytes 6148
  433.8 11.4 %copy-start.70 = (f32[1,4,2,128]{3,1,2,0:T(4,128)S(1)}, f32[1,4,2,128]{3,1,2,0:T(4,128)}, u32[]{:S(2)}) copy-start(f32[1,4,2,128]{3,1,2,0:T(4,128)} %copy-done.69) | copy-start | bytes 12292
  433.8 11.4 %copy-start.83 = (f32[512]{0:T(512)S(1)}, f32[512]{0:T(512)}, u32[]{:S(2)}) copy-start(f32[512]{0:T(512)} %copy-done.82) | copy-start | bytes 6148
  478.9 11.8 %copy-start.15 = (bf16[512,1024]{0,1:T(8,128)(2,1)S(1)}, bf16[512,1024]{0,1:T(8,128)(2,1)}, u32[]{:S(2)}) copy-start(bf16[512,1024]{0,1:T(8,128)(2,1)} %copy-done.14) | copy-start | bytes 3145732
  537.7 100.2 %all-to-all-start.2 = ((bf16[32,32,1024]{2,1,0:T(8,128)(2,1)}), bf16[32,32,1024]{2,1,0:T(8,128)(2,1)S(1)}, u32[]{:S(2)}, u32[]{:S(2)}) async-start(bf16[32,32,1024]{2,1,0:T(8,128)(2,1)} %bitcast.288), calls=%async_computation.2 | async-start | bytes 4194304 | tf_op jit(solution)/shard_map/all_to_all | solution.py:595
  643.3 466.6 %all-to-all-start.3 = ((bf16[16,2,32,1024]{3,2,1,0:T(8,128)(2,1)}), bf16[16,2,32,1024]{3,2,1,0:T(8,128)(2,1)}, u32[]{:S(2)}, u32[]{:S(2)}) async-start(bf16[16,2,32,1024]{3,2,1,0:T(8,128)(2,1)} %broadcast_select_fusion), calls=%async_computation.3 | async-start | bytes 4194304 | tf_op jit(solution)/shard_map/all_to_all | solution.py:598
  (87 other events, 403.3 us)

commit v2 on v1

--- a/solution.py
+++ b/solution.py
@@ -201,7 +201,7 @@
 
 
 def reduce_kernel(
-    count, grads, small,
+    count, parts, small,
     total, small_total, landing,
     own, came, across_half, kept, from_x, *rest
 ):
@@ -217,10 +217,17 @@
     rows = kept.shape[-2]
     greet([sibling, facing] + [across(p, count, bits) for p in range(count)])
 
+    ranges, at = [], 0
+    for part in parts:
+        ranges.append((part, at, at + part.shape[2]))
+        at += part.shape[2]
+
     def core_copy(unit):
-        return remote(
-            grads.at[1 - core, :, unit], landing.at[unit], send0.at[unit], recv0.at[unit], sibling
-        )
+        source = landing.at[unit]
+        if isinstance(unit, int):
+            part, low, _ = [entry for entry in ranges if entry[1] <= unit < entry[2]][0]
+            source = part.at[1 - core, :, unit - low]
+        return remote(source, landing.at[unit], send0.at[unit], recv0.at[unit], sibling)
 
     def x_copy(unit):
         return remote(
@@ -255,9 +262,14 @@
             kept.at[(unit,) + bits], total.at[(unit,) + bits], piece_sem.at[unit]
         )
 
-    def own_load(unit):
-        slot = lax.rem(unit, 2)
-        return pltpu.make_async_copy(grads.at[core, :, unit], own.at[slot], load_sem.at[slot])
+    def own_load(part, index, slot):
+        return pltpu.make_async_copy(part.at[core, :, index], own.at[slot], load_sem.at[slot])
+
+    def start_load(unit):
+        for part, low, high in ranges:
+            @pl.when(jnp.logical_and(unit >= low, unit < high))
+            def _():
+                own_load(part, unit - low, lax.rem(unit, 2)).start()
 
     def small_copy(step):
         partner = [sibling, facing] + [across(p, count, bits) for p in range(count)]
@@ -268,12 +280,9 @@
 
     small_copy(0).start()
 
-    def first(unit, carry):
+    for unit in range(UNITS):
         core_copy(unit).start()
-        return carry
-
-    lax.fori_loop(0, UNITS, first, 0)
-    own_load(0).start()
+    own_load(parts[0], 0, 0).start()
     small_steps = count + 2
 
     def tick(now, carry):
@@ -293,12 +302,12 @@
 
             @pl.when(unit + 1 < UNITS)
             def _():
-                own_load(unit + 1).start()
+                start_load(unit + 1)
 
             core_copy(unit).wait_recv()
             arrived = pltpu.make_async_copy(landing.at[unit], came, came_sem)
             arrived.start()
-            own_load(unit).wait()
+            own_load(parts[0], 0, slot).wait()
             arrived.wait()
             def add(block, c):
                 where = pl.ds(pl.multiple_of(block * 32, 32), 32)
@@ -388,14 +397,16 @@
     out.wait()
 
 
-def reduce_grads(grads, small, count):
+def reduce_grads(parts, small, count):
     cut = (2,) * count
     rows = 512 // (1 << count)
     narrow = cut + (rows, 1024)
     dma = pltpu.SemaphoreType.DMA
 
+    held = len(parts)
+
     def kernel(*refs):
-        reduce_kernel(count, *refs)
+        reduce_kernel(count, refs[:held], *refs[held:])
 
     vectors = small.shape[1:]
     total, small_total, _ = pl.pallas_call(
@@ -405,10 +416,8 @@
             jax.ShapeDtypeStruct(vectors, jnp.float32),
             jax.ShapeDtypeStruct((UNITS, 2, 512, 1024), jnp.bfloat16),
         ],
-        in_specs=[
-            pl.BlockSpec(memory_space=pl.ANY),
-            pl.BlockSpec(memory_space=pltpu.VMEM),
-        ],
+        in_specs=[pl.BlockSpec(memory_space=pl.ANY)] * held
+        + [pl.BlockSpec(memory_space=pltpu.VMEM)],
         out_specs=[pl.BlockSpec(memory_space=pl.ANY)] * 3,
         scratch_shapes=[
             pltpu.VMEM((2, 2, 512, 1024), jnp.bfloat16),
@@ -439,26 +448,29 @@
             collective_id=1, has_side_effects=True, vmem_limit_bytes=VMEM_LIMIT
         ),
         name="reduce_grads",
-    )(grads, small)
+    )(*parts, small)
     return total.reshape(UNITS, 512, 1024), small_total
-from jax.sharding import PartitionSpec as P
+
 
 HEAD_DIM = 64
 EPSILON = 1e-12
 MASKED = -1000000000.0
-VECTORS = (1, 1, 1, 1, 1, 4, 1, 1, 1)
-
-
-def dense(left_side, right_side):
-    return jnp.dot(left_side, right_side, preferred_element_type=jnp.float32)
-
-
-def dense_left(left_side, right_side):
-    return jnp.einsum("ra,rb->ab", left_side, right_side, preferred_element_type=jnp.float32)
-
-
-def dense_right(left_side, right_side):
-    return jnp.einsum("rb,ab->ra", left_side, right_side, preferred_element_type=jnp.float32)
+HIDDEN_BLOCK = 512
+WIDE = 256
+BF = jnp.bfloat16
+F32 = jnp.float32
+
+
+def mm(a, b):
+    return lax.dot_general(a, b, (((1,), (0,)), ((), ())), preferred_element_type=F32)
+
+
+def mm_right(a, b):
+    return lax.dot_general(a, b, (((1,), (1,)), ((), ())), preferred_element_type=F32)
+
+
+def mm_left(a, b):
+    return lax.dot_general(a, b, (((0,), (0,)), ((), ())), preferred_element_type=F32)
 
 
 def normalized(values):
@@ -476,88 +488,396 @@
     return (gs - mean_gs - unit * mean_gn) * scale
 
 
-def layer_forward(x, live, params):
-    wq, wk, wv, wo, w1, w2, (bq, bv, bo, g1, b1, bi, b2, g2, bb2) = params
+def head_lanes(head):
+    lane = lax.broadcasted_iota(jnp.int32, (1, WIDE), 1)
+    return lane // HEAD_DIM == head
+
+
+def row_sum(values):
+    return jnp.sum(values, axis=0, keepdims=True)
+
+
+def attend_kernel(
+    length, x, wq, wk, wv, wo, bq, bv, bo, q_out, k_out, v_out, log_out, context_out,
+    unit_out, scale_out, total,
+):
+    step = pl.program_id(0)
     slots = x.shape[0]
-    heads = (slots, 16, HEAD_DIM)
-    q = (dense(x, wq) + bq).astype(jnp.bfloat16).reshape(heads)
-    k = dense(x, wk).astype(jnp.bfloat16).reshape(heads)
-    v = (dense(x, wv) + bv).astype(jnp.bfloat16).reshape(heads)
-    scores = jnp.einsum("qhd,khd->hqk", q, k, preferred_element_type=jnp.float32) * 0.125
-    scores = jnp.where(live[None, None, :], scores, MASKED)
-    highest = jnp.max(scores, axis=-1, keepdims=True)
-    exponent = jnp.exp(scores - highest)
-    totals = jnp.sum(exponent, axis=-1, keepdims=True)
-    probs = (exponent / totals).astype(jnp.bfloat16)
-    log_total = highest + jnp.log(totals)
-    context = jnp.einsum("hqk,khd->qhd", probs, v, preferred_element_type=jnp.float32)
-    context = context.astype(jnp.bfloat16).reshape(slots, -1)
-    first_sum = x.astype(jnp.float32) + (dense(context, wo) + bo)
-    unit1, scale1 = normalized(first_sum)
-    middle = unit1 * g1 + b1
-    middle_low = middle.astype(jnp.bfloat16)
-    inner = dense(middle_low, w1) + bi
+    rows = x[...]
+    q = (mm(rows, wq[...]) + bq[...]).astype(BF)
+    k = mm(rows, wk[...]).astype(BF)
+    v = (mm(rows, wv[...]) + bv[...]).astype(BF)
+    q_out[...] = q
+    k_out[...] = k
+    v_out[...] = v
+    live = lax.broadcasted_iota(jnp.int32, (1, slots), 1) < length[0]
+    scaled = (q.astype(F32) * 0.125).astype(BF)
+    zero = jnp.zeros_like(scaled)
+    context = jnp.zeros((slots, WIDE), F32)
+    logs = jnp.zeros((slots, 128), F32)
+    column = lax.broadcasted_iota(jnp.int32, (1, 128), 1)
+    for head in range(WIDE // HEAD_DIM):
+        lanes = head_lanes(head)
+        scores = mm_right(jnp.where(lanes, scaled, zero), k)
+        scores = jnp.where(live, scores, MASKED)
+        highest = jnp.max(scores, axis=-1, keepdims=True)
+        exponent = jnp.exp(scores - highest)
+        totals = jnp.sum(exponent, axis=-1, keepdims=True)
+        probs = (exponent * (1.0 / totals)).astype(BF)
+        context = jnp.where(lanes, mm(probs, v), context)
+        logs = jnp.where(column == head, highest + jnp.log(totals), logs)
+    log_out[...] = jnp.transpose(logs)[:8]
+    low = context.astype(BF)
+    context_out[...] = low
+
+    @pl.when(step == 0)
+    def _():
+        total[...] = rows.astype(F32) + bo[...]
+
+    total[...] += mm(low, wo[...])
+
+    @pl.when(step == pl.num_programs(0) - 1)
+    def _():
+        unit, scale = normalized(total[...])
+        unit_out[...] = unit
+        scale_out[...] = jnp.broadcast_to(scale, scale_out.shape)
+
+
+def feed_kernel(
+    length, unit1, g1, b1, w1, bi, w2, b2, g2, bb2, act_out, slope_out, unit_out, scale_out,
+    result_out, low, total,
+):
+    step = pl.program_id(0)
+
+    @pl.when(step == 0)
+    def _():
+        middle = unit1[...] * g1[...] + b1[...]
+        low[...] = middle.astype(BF)
+        total[...] = middle + b2[...]
+
+    inner = mm(low[...], w1[...]) + bi[...]
     cdf = 0.5 * (1.0 + lax.erf(inner * 0.7071067811865476))
-    activated = (inner * cdf).astype(jnp.bfloat16)
-    slope = (cdf + inner * (jnp.exp(-0.5 * inner * inner) * 0.3989422804014327)).astype(
-        jnp.bfloat16
-    )
-    second_sum = middle + (dense(activated, w2) + b2)
-    unit2, scale2 = normalized(second_sum)
-    row_mask = live[:, None].astype(jnp.float32)
-    result = ((unit2 * g2 + bb2) * row_mask).astype(jnp.bfloat16)
-    return result, (q, k, v, log_total, context, unit1, scale1, middle_low, activated, slope, unit2, scale2)
-
-
-def layer_backward(grad, x, live, params, stored):
-    wq, wk, wv, wo, w1, w2, (bq, bv, bo, g1, b1, bi, b2, g2, bb2) = params
-    q, k, v, log_total, context, unit1, scale1, middle_low, activated, slope, unit2, scale2 = stored
+    act = (inner * cdf).astype(BF)
+    act_out[...] = act
+    slope_out[...] = (cdf + inner * (jnp.exp(-0.5 * inner * inner) * 0.3989422804014327)).astype(BF)
+    total[...] += mm(act, w2[...])
+
+    @pl.when(step == pl.num_programs(0) - 1)
+    def _():
+        unit, scale = normalized(total[...])
+        unit_out[...] = unit
+        scale_out[...] = jnp.broadcast_to(scale, scale_out.shape)
+        live = lax.broadcasted_iota(jnp.int32, (unit.shape[0], 1), 0) < length[0]
+        result_out[...] = jnp.where(live, unit * g2[...] + bb2[...], 0.0).astype(BF)
+
+
+def feed_back_kernel(
+    length, grad, unit2, scale2, g2, unit1, scale1, g1, b1, act, slope, w1, w2, *refs
+):
+    (d1_out, d2_out, first_out, vectors_out, inner_sum_out, second, outer, low, total) = refs[-9:]
+    step = pl.program_id(0)
+
+    @pl.when(step == 0)
+    def _():
+        live = lax.broadcasted_iota(jnp.int32, (grad.shape[0], 1), 0) < length[0]
+        g = jnp.where(live, grad[...].astype(F32), 0.0)
+        unit = unit2[...]
+        d_second = normalize_back(g, unit, scale2[:, :1], g2[...])
+        second[...] = d_second
+        d_outer = d_second.astype(BF)
+        outer[...] = d_outer
+        vectors_out[0:1] = row_sum(d_outer.astype(F32))
+        vectors_out[1:2] = row_sum(g * unit)
+        vectors_out[2:3] = row_sum(g)
+        low[...] = (unit1[...] * g1[...] + b1[...]).astype(BF)
+        total[...] = jnp.zeros_like(total)
+
+    d_outer = outer[...]
+    d_inner = (mm_right(d_outer, w2[...]) * slope[...].astype(F32)).astype(BF)
+    inner_sum_out[...] = row_sum(d_inner.astype(F32))
+    total[...] += mm_right(d_inner, w1[...])
+    d2_out[...] = mm_left(act[...], d_outer).astype(BF).reshape(d2_out.shape)
+    d1 = mm_left(low[...], d_inner).astype(BF)
+    half = d1.shape[0] // 2
+    d1_out[0, 0, 0] = d1[:half]
+    d1_out[0, 1, 0] = d1[half:]
+
+    @pl.when(step == pl.num_programs(0) - 1)
+    def _():
+        d_middle = second[...] + total[...]
+        unit = unit1[...]
+        d_first = normalize_back(d_middle, unit, scale1[:, :1], g1[...])
+        first_out[...] = d_first
+        vectors_out[3:4] = row_sum(d_middle * unit)
+        vectors_out[4:5] = row_sum(d_middle)
+        vectors_out[5:6] = row_sum(d_first.astype(BF).astype(F32))
+
+
+def attend_back_kernel(
+    length, first, x, q, k, v, log, context, wq, wk, wv, wo, *refs
+):
+    (dqkv_out, do_out, x_out, sums_out, attended, total) = refs[-6:]
+    step = pl.program_id(0)
     slots = x.shape[0]
-    heads = (slots, 16, HEAD_DIM)
-    g = grad.astype(jnp.float32) * live[:, None].astype(jnp.float32)
-    d_second = normalize_back(g, unit2, scale2, g2)
-    d_g2, d_bb2 = jnp.sum(g * unit2, axis=0), jnp.sum(g, axis=0)
-    d_outer = d_second.astype(jnp.bfloat16)
-    d_inner = (dense_right(d_outer, w2) * slope.astype(jnp.float32)).astype(jnp.bfloat16)
-    d_middle = d_second + dense_right(d_inner, w1)
-    d_first = normalize_back(d_middle, unit1, scale1, g1)
-    d_g1, d_b1 = jnp.sum(d_middle * unit1, axis=0), jnp.sum(d_middle, axis=0)
-    d_att = d_first.astype(jnp.bfloat16)
-    d_context = dense_right(d_att, wo).astype(jnp.bfloat16).reshape(heads)
-    scores = jnp.einsum("qhd,khd->hqk", q, k, preferred_element_type=jnp.float32) * 0.125
-    scores = jnp.where(live[None, None, :], scores, MASKED)
-    probs = jnp.exp(scores - log_total)
-    d_v = jnp.einsum(
-        "hqk,qhd->khd", probs.astype(jnp.bfloat16), d_context, preferred_element_type=jnp.float32
-    )
-    d_v = d_v.astype(jnp.bfloat16).reshape(slots, -1)
-    d_probs = jnp.einsum("qhd,khd->hqk", d_context, v, preferred_element_type=jnp.float32)
-    dots = jnp.sum(probs * d_probs, axis=-1, keepdims=True)
-    d_scores = (probs * (d_probs - dots)).astype(jnp.bfloat16)
-    d_q = jnp.einsum("hqk,khd->qhd", d_scores, k, preferred_element_type=jnp.float32) * 0.125
-    d_k = jnp.einsum("hqk,qhd->khd", d_scores, q, preferred_element_type=jnp.float32) * 0.125
-    d_q = d_q.astype(jnp.bfloat16).reshape(slots, -1)
-    d_k = d_k.astype(jnp.bfloat16).reshape(slots, -1)
-    d_x = d_first + dense_right(d_q, wq) + dense_right(d_k, wk) + dense_right(d_v, wv)
-
-    def sums(values):
-        return jnp.sum(values, axis=0, dtype=jnp.float32)
-
-    vectors = (
-        sums(d_q), sums(d_v), sums(d_att), d_g1, d_b1, sums(d_inner), sums(d_outer), d_g2, d_bb2
-    )
-    matrices = [
-        dense_left(x, d_q), dense_left(x, d_k), dense_left(x, d_v), dense_left(context, d_att),
-        dense_left(middle_low, d_inner), dense_left(activated, d_outer),
-    ]
-    low = [m.astype(jnp.bfloat16) for m in matrices]
-    packed = [m.reshape(2, 1, 512, 1024) for m in low[:4]]
-    packed += [low[4].reshape(2, 512, 4, 1024).transpose(0, 2, 1, 3), low[5].reshape(2, 4, 512, 1024)]
-    return (
-        d_x.astype(jnp.bfloat16),
-        jnp.concatenate(packed, axis=1),
-        jnp.concatenate([v.reshape(2, -1) for v in vectors], axis=1).reshape(96, 128),
-    )
+
+    @pl.when(step == 0)
+    def _():
+        attended[...] = first[...].astype(BF)
+        total[...] = first[...]
+
+    d_att = attended[...]
+    d_context = mm_right(d_att, wo[...]).astype(BF)
+    queries = q[...]
+    keys = k[...]
+    values = v[...]
+    scaled = (queries.astype(F32) * 0.125).astype(BF)
+    zero = jnp.zeros_like(scaled)
+    live = lax.broadcasted_iota(jnp.int32, (slots, 1), 0) < length[0]
+    d_q = jnp.zeros((slots, WIDE), F32)
+    d_k = jnp.zeros((slots, WIDE), F32)
+    d_v = jnp.zeros((slots, WIDE), F32)
+    for head in range(WIDE // HEAD_DIM):
+        lanes = head_lanes(head)
+        scores = mm_right(keys, jnp.where(lanes, scaled, zero))
+        scores = jnp.where(live, scores, MASKED)
+        probs = jnp.exp(scores - log[head : head + 1])
+        d_v = jnp.where(lanes, mm(probs.astype(BF), d_context), d_v)
+        d_probs = mm_right(values, jnp.where(lanes, d_context, zero))
+        dots = row_sum(probs * d_probs)
+        d_scores = (probs * (d_probs - dots)).astype(BF)
+        d_k = jnp.where(lanes, mm(d_scores, queries), d_k)
+        d_q = jnp.where(lanes, mm_left(d_scores, keys), d_q)
+    d_q = (d_q * 0.125).astype(BF)
+    d_k = (d_k * 0.125).astype(BF)
+    d_v = d_v.astype(BF)
+    sums_out[0:1] = row_sum(d_q.astype(F32))
+    sums_out[1:2] = row_sum(d_v.astype(F32))
+    total[...] += mm_right(d_q, wq[...]) + mm_right(d_k, wk[...]) + mm_right(d_v, wv[...])
+    rows = x[...]
+    for at, value in enumerate((d_q, d_k, d_v)):
+        weight = mm_left(rows, value).astype(BF)
+        half = weight.shape[0] // 2
+        dqkv_out[0, 0, at] = weight[:half]
+        dqkv_out[0, 1, at] = weight[half:]
+    do_out[...] = mm_left(context[...], d_att).astype(BF).reshape(do_out.shape)
+
+    @pl.when(step == pl.num_programs(0) - 1)
+    def _():
+        x_out[...] = total[...].astype(BF)
+
+
+def whole(shape):
+    return pl.BlockSpec(shape, lambda j, *_: (0,) * len(shape))
+
+
+def struct(shape, dtype):
+    return jax.ShapeDtypeStruct(shape, dtype)
+
+
+def grid_call(kernel, steps, in_specs, out_specs, out_shape, scratch, name, flops, aliases=None):
+    return pl.pallas_call(
+        kernel,
+        grid_spec=pltpu.PrefetchScalarGridSpec(
+            num_scalar_prefetch=1,
+            grid=(steps,),
+            in_specs=in_specs,
+            out_specs=out_specs,
+            scratch_shapes=scratch,
+        ),
+        out_shape=out_shape,
+        input_output_aliases=aliases or {},
+        compiler_params=pltpu.CompilerParams(
+            dimension_semantics=("arbitrary",), vmem_limit_bytes=VMEM_LIMIT
+        ),
+        cost_estimate=pl.CostEstimate(
+            flops=flops, bytes_accessed=30000000, transcendentals=4000000
+        ),
+        name=name,
+    )
+
+
+def rank_two(vector):
+    return vector.reshape(1, -1)
+
+
+def layer_of(shape, layer):
+    return pl.BlockSpec((None,) + shape, None)
+
+
+def attend(length, x, layer, weights, vectors):
+    wq, wk, wv, wo = weights
+    slots, width = x.shape
+    steps = width // WIDE
+    columns = pl.BlockSpec((None, width, WIDE), lambda j, *_: (layer, 0, j))
+    band = pl.BlockSpec((slots, WIDE), lambda j, *_: (0, j))
+    line = pl.BlockSpec((1, WIDE), lambda j, *_: (0, j))
+    return grid_call(
+        attend_kernel,
+        steps,
+        [
+            whole((slots, width)), columns, columns, columns,
+            pl.BlockSpec((None, WIDE, width), lambda j, *_: (layer, j, 0)),
+            line, line, whole((1, width)),
+        ],
+        [
+            band, band, band,
+            pl.BlockSpec((None, 8, slots), lambda j, *_: (j, 0, 0)),
+            band, whole((slots, width)), whole((slots, 128)),
+        ],
+        [
+            struct((slots, width), BF), struct((slots, width), BF), struct((slots, width), BF),
+            struct((steps, 8, slots), F32), struct((slots, width), BF),
+            struct((slots, width), F32), struct((slots, 128), F32),
+        ],
+        [pltpu.VMEM((slots, width), F32)],
+        "attend",
+        9000000000,
+    )(length, x, wq, wk, wv, wo, *(rank_two(v) for v in vectors))
+
+
+def feed(length, unit1, layer, w1, w2, vectors):
+    slots, width = unit1.shape
+    hidden = w1.shape[-1]
+    steps = hidden // HIDDEN_BLOCK
+    g1, b1, bi, b2, g2, bb2 = (rank_two(v) for v in vectors)
+    line = whole((1, width))
+    band = pl.BlockSpec((slots, HIDDEN_BLOCK), lambda j, *_: (0, j))
+    return grid_call(
+        feed_kernel,
+        steps,
+        [
+            whole((slots, width)), line, line,
+            pl.BlockSpec((None, width, HIDDEN_BLOCK), lambda j, *_: (layer, 0, j)),
+            pl.BlockSpec((1, HIDDEN_BLOCK), lambda j, *_: (0, j)),
+            pl.BlockSpec((None, HIDDEN_BLOCK, width), lambda j, *_: (layer, j, 0)),
+            line, line, line,
+        ],
+        [band, band, whole((slots, width)), whole((slots, 128)), whole((slots, width))],
+        [
+            struct((slots, hidden), BF), struct((slots, hidden), BF), struct((slots, width), F32),
+            struct((slots, 128), F32), struct((slots, width), BF),
+        ],
+        [pltpu.VMEM((slots, width), BF), pltpu.VMEM((slots, width), F32)],
+        "feed",
+        9000000000,
+    )(length, unit1, g1, b1, w1, bi, w2, b2, g2, bb2)
+
+
+def feed_back(length, grad, unit2, scale2, unit1, scale1, act, slope, layer, w1, w2, vectors, held):
+    slots, width = unit1.shape
+    hidden = w1.shape[-1]
+    steps = hidden // HIDDEN_BLOCK
+    per = 1024 // HIDDEN_BLOCK
+    g1, b1, g2 = (rank_two(v) for v in vectors)
+    line = whole((1, width))
+    row = whole((slots, width))
+    thin = whole((slots, 128))
+    band = pl.BlockSpec((slots, HIDDEN_BLOCK), lambda j, *_: (0, j))
+    d1_block = pl.BlockSpec(
+        (1, 2, 1, 512, HIDDEN_BLOCK), lambda j, *_: (layer, 0, j // per, 0, j % per)
+    )
+    pairs = HIDDEN_BLOCK // 512
+    d2_block = pl.BlockSpec(
+        (1, 1, pairs, 512, width),
+        lambda j, *_: (layer, j // (steps // 2), j % (steps // 2), 0, 0),
+    )
+    extra = () if held is None else tuple(held)
+    return grid_call(
+        feed_back_kernel,
+        steps,
+        [
+            row, row, thin, line, row, thin, line, line, band, band,
+            pl.BlockSpec((None, width, HIDDEN_BLOCK), lambda j, *_: (layer, 0, j)),
+            pl.BlockSpec((None, HIDDEN_BLOCK, width), lambda j, *_: (layer, j, 0)),
+        ]
+        + [pl.BlockSpec(memory_space=pl.ANY)] * len(extra),
+        [
+            d1_block, d2_block, row, whole((6, width)),
+            pl.BlockSpec((1, HIDDEN_BLOCK), lambda j, *_: (0, j)),
+        ],
+        [
+            struct((2, 2, 4, 512, 1024), BF), struct((2, 2, 4, 512, 1024), BF),
+            struct((slots, width), F32), struct((6, width), F32), struct((1, hidden), F32),
+        ],
+        [
+            pltpu.VMEM((slots, width), F32), pltpu.VMEM((slots, width), BF),
+            pltpu.VMEM((slots, width), BF), pltpu.VMEM((slots, width), F32),
+        ],
+        "feed_back",
+        18000000000,
+        {13 + i: i for i in range(len(extra))},
+    )(length, grad, unit2, scale2, g2, unit1, scale1, g1, b1, act, slope, w1, w2, *extra)
+
+
+def attend_back(length, first, x, q, k, v, log, context, layer, weights, held):
+    wq, wk, wv, wo = weights
+    slots, width = x.shape
+    steps = width // WIDE
+    columns = pl.BlockSpec((None, width, WIDE), lambda j, *_: (layer, 0, j))
+    band = pl.BlockSpec((slots, WIDE), lambda j, *_: (0, j))
+    row = whole((slots, width))
+    per = 512 // WIDE
+    extra = () if held is None else tuple(held)
+    return grid_call(
+        attend_back_kernel,
+        steps,
+        [
+            row, row, band, band, band,
+            pl.BlockSpec((None, 8, slots), lambda j, *_: (j, 0, 0)),
+            band, columns, columns, columns,
+            pl.BlockSpec((None, WIDE, width), lambda j, *_: (layer, j, 0)),
+        ]
+        + [pl.BlockSpec(memory_space=pl.ANY)] * len(extra),
+        [
+            pl.BlockSpec((1, 2, 3, 512, WIDE), lambda j, *_: (layer, 0, 0, 0, j)),
+            pl.BlockSpec((1, 1, 1, WIDE, width), lambda j, *_: (layer, j // per, 0, j % per, 0)),
+            row,
+            pl.BlockSpec((2, WIDE), lambda j, *_: (0, j)),
+        ],
+        [
+            struct((2, 2, 3, 512, 1024), BF), struct((2, 2, 1, 512, 1024), BF),
+            struct((slots, width), BF), struct((2, width), F32),
+        ],
+        [pltpu.VMEM((slots, width), BF), pltpu.VMEM((slots, width), F32)],
+        "attend_back",
+        20000000000,
+        {12 + i: i for i in range(len(extra))},
+    )(length, first, x, q, k, v, log, context, wq, wk, wv, wo, *extra)
+
+
+from jax.sharding import PartitionSpec as P
+
+VECTORS = (1, 1, 1, 1, 1, 4, 1, 1, 1)
+
+
+def unpack_kernel(narrow, first, second, *outs):
+    for at in range(4):
+        outs[at][0] = narrow[at].astype(F32)
+    for at in range(4):
+        outs[4][0, :, pl.ds(1024 * at, 1024)] = first[at].astype(F32)
+    outs[5][0] = second[0].astype(F32)
+
+
+def unpack(total):
+    square = pl.BlockSpec((1, 128, 1024), lambda j: (0, j, 0))
+    return pl.pallas_call(
+        unpack_kernel,
+        grid=(4,),
+        in_specs=[
+            pl.BlockSpec((4, 128, 1024), lambda j: (0, j, 0)),
+            pl.BlockSpec((4, 128, 1024), lambda j: (1, j, 0)),
+            pl.BlockSpec((1, 512, 1024), lambda j: (8 + j, 0, 0)),
+        ],
+        out_specs=[square] * 4
+        + [
+            pl.BlockSpec((1, 128, 4096), lambda j: (0, j, 0)),
+            pl.BlockSpec((1, 512, 1024), lambda j: (0, j, 0)),
+        ],
+        out_shape=[struct((1, 512, 1024), F32)] * 4
+        + [struct((1, 512, 4096), F32), struct((1, 2048, 1024), F32)],
+        compiler_params=pltpu.CompilerParams(vmem_limit_bytes=VMEM_LIMIT),
+        name="unpack",
+    )(total, total, total)
 
 
 def split_vectors(packed):
@@ -599,6 +919,31 @@
     return home.transpose(1, 0, 2, 3).reshape(2, slots, width)
 
 
+def layer_forward(length, x, layer, weights, vectors):
+    bq, bv, bo, g1, b1, bi, b2, g2, bb2 = vectors
+    q, k, v, log, context, unit1, scale1 = attend(length, x, layer, weights[:4], (bq, bv, bo))
+    act, slope, unit2, scale2, result = feed(
+        length, unit1, layer, weights[4], weights[5], (g1, b1, bi, b2, g2, bb2)
+    )
+    return result, (q, k, v, log, context, unit1, scale1, act, slope, unit2, scale2)
+
+
+def layer_backward(length, grad, x, layer, weights, vectors, stored, held):
+    q, k, v, log, context, unit1, scale1, act, slope, unit2, scale2 = stored
+    g1, b1, g2 = vectors[3], vectors[4], vectors[7]
+    d1, d2, first, rows, inner = feed_back(
+        length, grad, unit2, scale2, unit1, scale1, act, slope, layer, weights[4], weights[5],
+        (g1, b1, g2), None if held is None else held[2:],
+    )
+    d_qkv, d_o, d_x, sums = attend_back(
+        length, first, x, q, k, v, log, context, layer, weights[:4],
+        None if held is None else held[:2],
+    )
+    vectors = (sums[0], sums[1], rows[5], rows[3], rows[4], inner[0], rows[0], rows[1], rows[2])
+    small = jnp.concatenate([v.reshape(2, -1) for v in vectors], axis=1).reshape(96, 128)
+    return d_x, small, (d_qkv, d_o, d1, d2)
+
+
 def on_device(
     inputs, cotangent, lengths, permutation, query_weight, query_bias, key_weight, value_weight,
     value_bias, output_weight, output_bias, first_gain, first_bias, inner_weight, inner_bias,
@@ -608,7 +953,6 @@
     group = lax.axis_index(GROUP)
     groups = lax.axis_size(GROUP)
     count = lax.axis_size("replica").bit_length() - 1
-    slots = inputs.shape[1]
     shards = [
         w[0] for w in (query_weight, key_weight, value_weight, output_weight, inner_weight, outer_weight)
     ]
@@ -617,35 +961,31 @@
                        outer_bias, second_gain, second_bias)
     ]
     full = gather_weights(shards, jnp.concatenate(vectors).reshape(48, 128), count)
-    layers = [tuple(w[s] for w in full[:6]) + (split_vectors(full[6][s]),) for s in range(2)]
-    length = lax.dynamic_index_in_dim(lengths, 2 * group + core, 0, keepdims=False)
-    live = jnp.arange(slots, dtype=jnp.int32) < length
+    weights, shared = full[:6], [split_vectors(full[6][s]) for s in range(2)]
+    length = lax.dynamic_slice_in_dim(lengths, 2 * group + core, 1)
     x = lax.dynamic_index_in_dim(inputs, core, 0, keepdims=False)
     grad = own_cotangent(cotangent, permutation, groups)
-    lower, lower_stored = layer_forward(x, live, layers[0])
-    upper, upper_stored = layer_forward(lower, live, layers[1])
-    upper_grad, upper_packed, upper_small = layer_backward(grad, lower, live, layers[1], upper_stored)
-    lower_grad, lower_packed, lower_small = layer_backward(
-        upper_grad, x, live, layers[0], lower_stored
-    )
-    total, small = reduce_grads(
-        jnp.stack([lower_packed, upper_packed]), jnp.stack([lower_small, upper_small]), count
-    )
+    lower, lower_stored = layer_forward(length, x, 0, weights, shared[0])
+    upper, upper_stored = layer_forward(length, lower, 1, weights, shared[1])
+    upper_grad, upper_small, parts = layer_backward(
+        length, grad, lower, 1, weights, shared[1], upper_stored, None
+    )
+    lower_grad, lower_small, parts = layer_backward(
+        length, upper_grad, x, 0, weights, shared[0], lower_stored, parts
+    )
+    total, small = reduce_grads(parts, jnp.stack([lower_small, upper_small]), count)
     sent = jnp.where(core == 0, upper, lower)
     kept = jnp.where(core == 0, lower, upper)
     came = lax.ppermute(sent, "section", [(0, 1), (1, 0)])
     activations = jnp.where(core == 0, jnp.stack([kept, came]), jnp.stack([came, kept]))[None]
     input_grads = dealt_grads(jnp.stack([lower_grad, upper_grad]), permutation, groups)[None]
-    wide = total.astype(jnp.float32)
     side = lax.axis_index("shard")
     own = lax.dynamic_index_in_dim(small.reshape(2, -1), side, 0, keepdims=False)
     pieces, at = [], 0
     for width in VECTORS:
         pieces.append(own[None, at : at + 512 * width])
         at += 512 * width
-    dq, dk, dv, do = (wide[i][None] for i in range(4))
-    d1 = wide[4:8].transpose(1, 0, 2).reshape(1, 512, 4096)
-    d2 = wide[8:12].reshape(1, 2048, 1024)
+    dq, dk, dv, do, d1, d2 = unpack(total)
     return (
         activations, input_grads, dq, pieces[0], dk, dv, pieces[1], do, pieces[2], pieces[3],
         pieces[4], d1, pieces[5], d2, pieces[6], pieces[7], pieces[8],

time: 1120 us -> 872 us (0.78)
  matrix products: 242 us -> 0 us
  Pallas kernels: 521 us -> 743 us
  local copies, waits for them, and re-layouts: 200 us -> 29.1 us
  other arithmetic: 106 us -> 15.4 us
  waiting for transfers between devices: 16.4 us -> 46.8 us
    dot_general x48 -> x0, matrix products: 242 us -> none  [the longest x12 55.8 us: dense_left(): jnp.einsum('ra,rb->ab', left_side, right_side, preferred_element_type=jnp...]
    pallas_call x0 -> x9, Pallas kernels: none -> 213 us  [the longest x2 60.4 us: attend_back(): grid_call(attend_back_kernel, steps, [row, row, band, band, band, pl.Bloc...]
    slice x6 -> x4, local copies, waits for them, and re-layouts: 51.7 us -> 0.18 us  [the longest x2 0.13 us: layer_backward(): rows[2]]
    all_to_all x1, waiting for transfers between devices: 0.01 us -> 46.8 us  [dealt_grads(): lax.all_to_all(both.reshape(2 * groups, rows, width), ALL, 0, 0, tiled=True)]
    reshape x21 -> x0, local copies, waits for them, and re-layouts: 40.5 us -> none  [the longest x2 29.1 us: layer_backward(): low[4].reshape(2, 512, 4, 1024).transpose(0, 2, 1, 3)]
    unnamed x281 -> x89, local copies, waits for them, and re-layouts: 55.2 us -> 16.7 us
    another operation x1 -> x0, other arithmetic: 33.7 us -> none  [on_device(): jnp.stack([lower_packed, upper_packed])]
    reduce_sum x12 -> x0, other arithmetic: 29 us -> none  [the longest x2 16.6 us: layer_forward(): totals = jnp.sum(exponent, axis=-1, keepdims=True)]
  transfers between devices with their start and end apart: 5 -> 5, of which waited for: 2 -> 1; matrix products, arithmetic and copies ran while one was open for 30% -> 4% of each run, Pallas kernels for 47% -> 72%
where the time goes in v2:
time: 872 us; the launch traced here: 863 us
  Pallas kernels  743 us (85%)
  waiting for transfers between devices  46.8 us (5%)
  local copies, waits for them, and re-layouts  29.1 us (3%)
  starting transfers between devices  27 us (3%)
  other arithmetic  15.4 us (2%)
    pallas_call x1, Pallas kernels, reduce_grads(): pl.pallas_call(kernel, out_shape=[jax.ShapeDtypeStruct((UNITS,) + narrow,...  383 us
    pallas_call x1, Pallas kernels, gather_weights(): pl.pallas_call(kernel, out_shape=outs, in_specs=[pl.BlockSpec(memory_spac...  146 us
    pallas_call x2, Pallas kernels, attend_back(): grid_call(attend_back_kernel, steps, [row, row, band, band, band, pl.Bloc...  60.4 us
    pallas_call x2, Pallas kernels, feed_back(): grid_call(feed_back_kernel, steps, [row, row, thin, line, row, thin, line...  60 us
    all_to_all x1, waiting for transfers between devices, dealt_grads(): lax.all_to_all(both.reshape(2 * groups, rows, width), ALL, 0, 0, tiled=True)  46.8 us
    pallas_call x2, Pallas kernels, attend(): grid_call(attend_kernel, steps, [whole((slots, width)), columns, columns,...  40.7 us
    pallas_call x2, Pallas kernels, feed(): grid_call(feed_kernel, steps, [whole((slots, width)), line, line, pl.Bloc...  39.8 us
  transfers between devices with their start and end apart: 5, of which 1 were waited for; matrix products, arithmetic and copies ran while one was open for 4% of the time, Pallas kernels for 72%

profile of v2, /device:TPU:0, one launch (start us, length us, event | category | flops | bytes accessed | tf_op | source)
XLA Modules:
  0.0 862.6 jit_solution(4479262939880511601)
XLA Ops:
  0.7 1.6 copy-done
  2.3 1.0 constant_dynamic-slice_fusion.1
  3.4 7.3 all-to-all-start
  13.6 145.9 %gather_weights.1 = (bf16[2,2,2,2,2,64,1024]{6,5,4,3,2,1,0:T(8,128)(2,1)}, bf16[2,2,2,2,2,64,1024]{6,5,4,3,2,1,0:T(8,128)(2,1)}, bf16[2,2,2,2,2,64,1024]{6,5,4,3...) custom-call(bf16[2,2,2,64,1024]{4,3,2,1,0:T(8,128)(2,1)} %bitcast.14, ...), custom_call_target="tpu_custom_call" | custom-call | tf_op jit(solution)/shard_map/gather_weights/pallas_call | solution.py:181
  159.5 0.8 slice_bitcast_fusion
  160.6 2.3 dynamic-slice_bitcast_fusion.x
  171.8 20.3 %attend.2 = (bf16[512,1024]{1,0:T(8,128)(2,1)}, bf16[512,1024]{1,0:T(8,128)(2,1)}, bf16[512,1024]{1,0:T(8,128)(2,1)}, f32[4,8,512]{2,1,0:T(8,128)}, bf16[512,102...) custom-call(s32[1]{0:T(128)} %dynamic_slice.14.length, bf16[512,1024]{1,0:T(8,128)(2,1)} %dynamic-slice_bitcast_fusion.x, ...), custom_call_target="tpu_custom_call" | custom-call | flops 8999999488 | bytes 30000000 | tf_op jit(solution)/shard_map/attend/pallas_call | solution.py:714
  192.2 19.9 %feed.2 = (bf16[512,4096]{1,0:T(8,128)(2,1)}, bf16[512,4096]{1,0:T(8,128)(2,1)}, f32[512,1024]{1,0:T(8,128)}, f32[512,128]{1,0:T(8,128)}, bf16[512,1024]{1,0:T(8,128)(2,1)}) custom-call(s32[1]{0:T(128)} %dynamic_slice.14.length, f32[512,1024]{1,0:T(8,128)} %get-tuple-element.79.unit1, f32[1,1024]{1,0:T(1,128)} %bitcast.150, f32[1,1024]{1,0:T(1,128)} %bitcast.152, ...), custom_call_target="tpu_custom_call" | custom-call | flops 8999999488 | bytes 30000000 | tf_op jit(solution)/shard_map/feed/pallas_call | solution.py:745
  212.7 1.1 broadcast_select_fusion.1
  213.8 8.7 %all-to-all-start.1 = ((bf16[32,16,1024]{2,1,0:T(8,128)(2,1)}), bf16[32,16,1024]{2,1,0:T(8,128)(2,1)S(1)}, u32[]{:S(2)}, u32[]{:S(2)}) async-start(bf16[32,16,1024]{2,1,0:T(8,128)(2,1)} %broadcast_select_fusion.1), calls=%async_computation.1 | async-start | bytes 2097152 | tf_op jit(solution)/shard_map/all_to_all | solution.py:909
  225.0 20.3 %attend.3 = (bf16[512,1024]{1,0:T(8,128)(2,1)}, bf16[512,1024]{1,0:T(8,128)(2,1)}, bf16[512,1024]{1,0:T(8,128)(2,1)}, f32[4,8,512]{2,1,0:T(8,128)}, bf16[512,102...) custom-call(s32[1]{0:T(128)} %dynamic_slice.14.length, bf16[512,1024]{1,0:T(8,128)(2,1)} %get-tuple-element.82.x, ...), custom_call_target="tpu_custom_call" | custom-call | flops 8999999488 | bytes 30000000 | tf_op jit(solution)/shard_map/attend/pallas_call | solution.py:714
  245.3 19.9 %feed.3 = (bf16[512,4096]{1,0:T(8,128)(2,1)}, bf16[512,4096]{1,0:T(8,128)(2,1)}, f32[512,1024]{1,0:T(8,128)}, f32[512,128]{1,0:T(8,128)}, bf16[512,1024]{1,0:T(8,128)(2,1)}) custom-call(s32[1]{0:T(128)} %dynamic_slice.14.length, f32[512,1024]{1,0:T(8,128)} %get-tuple-element.83.unit1, f32[1,1024]{1,0:T(1,128)} %bitcast.156, f32[1,1024]{1,0:T(1,128)} %bitcast.158, ...), custom_call_target="tpu_custom_call" | custom-call | flops 8999999488 | bytes 30000000 | tf_op jit(solution)/shard_map/feed/pallas_call | solution.py:745
  265.2 1.0 copy-done.3
  266.3 30.1 %feed_back.2 = (bf16[2,2,4,512,1024]{4,3,2,1,0:T(8,128)(2,1)}, bf16[2,2,4,512,1024]{4,3,2,1,0:T(8,128)(2,1)}, f32[512,1024]{1,0:T(8,128)}, f32[6,1024]{1,0:T(8,128)}, f32[1,4096]{1,0:T(1,128)}) custom-call(s32[1]{0:T(128)} %dynamic_slice.14.length, bf16[512,1024]{1,0:T(8,128)(2,1)} %bitcast.146, f32[512,1024]{1,0:T(8,128)} %get-tuple-element.85.unit2, ...), custom_call_target="tpu_custom_call" | custom-call | flops 17999998976 | bytes 30000000 | tf_op jit(solution)/shard_map/feed_back/pallas_call | solution.py:785
  296.4 30.1 %attend_back.2 = (bf16[2,2,3,512,1024]{4,3,2,1,0:T(8,128)(2,1)}, bf16[2,2,1,512,1024]{4,3,2,1,0:T(8,128)(2,1)}, bf16[512,1024]{1,0:T(8,128)(2,1)}, f32[2,1024]{1,0:T(2,128)}) custom-call(s32[1]{0:T(128)} %dynamic_slice.14.length, f32[512,1024]{1,0:T(8,128)} %get-tuple-element.90.first, bf16[512,1024]{1,0:T(8,128)(2,1)} %get-tuple-element.82.x, ...), custom_call_target="tpu_custom_call" | custom-call | flops 20000000000 | bytes 30000000 | tf_op jit(solution)/shard_map/attend_back/pallas_call | solution.py:821
  326.6 29.9 %feed_back.3 = (bf16[2,2,4,512,1024]{4,3,2,1,0:T(8,128)(2,1)}, bf16[2,2,4,512,1024]{4,3,2,1,0:T(8,128)(2,1)}, f32[512,1024]{1,0:T(8,128)}, f32[6,1024]{1,0:T(8,128)}, f32[1,4096]{1,0:T(1,128)}) custom-call(s32[1]{0:T(128)} %dynamic_slice.14.length, bf16[512,1024]{1,0:T(8,128)(2,1)} %get-tuple-element.96.grad, ...), custom_call_target="tpu_custom_call", output_to_operand_aliasing={{0}: (13, {}), {1}: (14, {})} | custom-call | flops 17999998976 | bytes 30000000 | tf_op jit(solution)/shard_map/feed_back/pallas_call | solution.py:785
  356.5 30.2 %attend_back.3 = (bf16[2,2,3,512,1024]{4,3,2,1,0:T(8,128)(2,1)}, bf16[2,2,1,512,1024]{4,3,2,1,0:T(8,128)(2,1)}, bf16[512,1024]{1,0:T(8,128)(2,1)}, f32[2,1024]{1,0:T(2,128)}) custom-call(s32[1]{0:T(128)} %dynamic_slice.14.length, f32[512,1024]{1,0:T(8,128)} %get-tuple-element.104.first, ...), custom_call_target="tpu_custom_call", output_to_operand_aliasing={{0}: (12, {}), {1}: (13, {})} | custom-call | flops 20000000000 | bytes 30000000 | tf_op jit(solution)/shard_map/attend_back/pallas_call | solution.py:821
  386.7 2.7 pad_maximum_fusion
  389.5 6.2 all-to-all-start.2
  395.6 2.7 select_bitcast_fusion
  398.8 46.8 %all-to-all-done.2 = bf16[32,32,1024]{2,1,0:T(8,128)(2,1)S(1)} async-done(((bf16[32,32,1024]{2,1,0:T(8,128)(2,1)}), bf16[32,32,1024]{2,1,0:T(8,128)(2,1)S(1)}, u32[]{:S(2)}, u32[]{:S(2)}) %all-to-all-start.2) | async-done | bytes 2097184 | tf_op jit(solution)/shard_map/all_to_all | solution.py:915
  445.6 2.0 gather_fusion.1
  447.6 3.2 broadcast_select_fusion
  450.7 4.4 all-to-all-start.3
  455.2 3.2 maximum_select_fusion
  459.1 0.7 reduce.79
  460.2 0.7 reduce.80
  461.8 383.4 %reduce_grads.1 = (bf16[12,2,2,2,64,1024]{5,4,3,2,1,0:T(8,128)(2,1)}, f32[96,128]{1,0:T(8,128)}, bf16[12,2,512,1024]{3,2,1,0:T(8,128)(2,1)}) custom-call(bf16[2,2,3,512,1024]{4,3,2,1,0:T(8,128)(2,1)} %get-tuple-element.113.refs_0_, bf16[2,2,1,512,1024]{4,3,2,1,0:T(8,128)(2,1)} %get-tuple-element.114.refs_1_, ...), custom_call_target="tpu_custom_call" | custom-call | tf_op jit(solution)/shard_map/reduce_grads/pallas_call | solution.py:412
  845.2 12.5 %unpack.1 = (f32[1,512,1024]{2,1,0:T(8,128)}, f32[1,512,1024]{2,1,0:T(8,128)}, f32[1,512,1024]{2,1,0:T(8,128)}, f32[1,512,1024]{2,1,0:T(8,128)}, f32[1,512,4096]{2,1,0:T(8,128)}, /*index=5*/f32[1,2048,1024]{2,1,0:T(8,128)}) custom-call(bf16[12,512,1024]{2,1,0:T(8,128)(2,1)} %bitcast.133, bf16[12,512,1024]{2,1,0:T(8,128)(2,1)} %bitcast.134, ...), custom_call_target="tpu_custom_call" | custom-call | tf_op jit(solution)/shard_map/unpack/pallas_call | solution.py:863
  857.8 0.7 dynamic-slice.5
  858.5 0.7 fusion.3
  859.2 3.2 copy.45
  (146 shorter events, 17.4 us)
Async XLA Ops:
  0.7 1.6 copy-start
  2.3 8.5 copy-start.13
  2.3 8.5 copy-start.14
  2.3 8.5 copy-start.15
  2.3 8.5 copy-start.16
  2.3 8.6 copy-start.17
  2.3 8.6 copy-start.10
  2.3 8.6 %copy-start.18 = (bf16[1,512]{1,0:T(2,128)(2,1)S(1)}, bf16[1,512]{1,0:T(2,128)(2,1)}, u32[]{:S(2)}) copy-start(bf16[1,512]{1,0:T(2,128)(2,1)} %param.35) | copy-start | bytes 3076
  2.3 8.7 %copy-start.19 = (bf16[1,512]{1,0:T(2,128)(2,1)S(1)}, bf16[1,512]{1,0:T(2,128)(2,1)}, u32[]{:S(2)}) copy-start(bf16[1,512]{1,0:T(2,128)(2,1)} %param.36) | copy-start | bytes 3076
  2.3 8.7 %copy-start.20 = (bf16[1,512]{1,0:T(2,128)(2,1)S(1)}, bf16[1,512]{1,0:T(2,128)(2,1)}, u32[]{:S(2)}) copy-start(bf16[1,512]{1,0:T(2,128)(2,1)} %param.37) | copy-start | bytes 3076
  3.4 208.7 %all-to-all-start = ((bf16[32,16,1024]{2,1,0:T(8,128)(2,1)}), bf16[32,16,1024]{2,1,0:T(8,128)(2,1)S(1)}, u32[]{:S(2)}, u32[]{:S(2)}) async-start(bf16[32,16,1024]{2,1,0:T(8,128)(2,1)} %bitcast.16), calls=%async_computation | async-start | bytes 2097152 | tf_op jit(solution)/shard_map/all_to_all | solution.py:902
  13.0 0.6 copy-start.9
  13.6 146.8 %copy-start.22 = (s32[32]{0:T(128)S(1)}, s32[32]{0:T(128)}, u32[]{:S(2)}) copy-start(s32[32]{0:T(128)} %param.22) | copy-start | bytes 388
  159.5 11.7 %copy-start.21 = (s32[32]{0:T(128)S(1)}, s32[32]{0:T(128)}, u32[]{:S(2)}) copy-start(s32[32]{0:T(128)} %param.21) | copy-start | bytes 388
  213.8 51.4 %all-to-all-start.1 = ((bf16[32,16,1024]{2,1,0:T(8,128)(2,1)}), bf16[32,16,1024]{2,1,0:T(8,128)(2,1)S(1)}, u32[]{:S(2)}, u32[]{:S(2)}) async-start(bf16[32,16,1024]{2,1,0:T(8,128)(2,1)} %broadcast_select_fusion.1), calls=%async_computation.1 | async-start | bytes 2097152 | tf_op jit(solution)/shard_map/all_to_all | solution.py:909
  265.2 1.1 copy-start.3
  356.5 30.2 %copy-start.2 = (bf16[512,1024]{1,0:T(8,128)(2,1)S(1)}, bf16[512,1024]{1,0:T(8,128)(2,1)}, u32[]{:S(2)}) copy-start(bf16[512,1024]{1,0:T(8,128)(2,1)} %get-tuple-element.96.grad) | copy-start | bytes 3145732
  389.5 56.1 %all-to-all-start.2 = ((bf16[32,32,1024]{2,1,0:T(8,128)(2,1)}), bf16[32,32,1024]{2,1,0:T(8,128)(2,1)S(1)}, u32[]{:S(2)}, u32[]{:S(2)}) async-start(bf16[32,32,1024]{2,1,0:T(8,128)(2,1)} %bitcast.136), calls=%async_computation.2 | async-start | bytes 4194304 | tf_op jit(solution)/shard_map/all_to_all | solution.py:915
  398.3 56.9 %collective-permute-start = (bf16[512,1024]{1,0:T(8,128)(2,1)}, bf16[512,1024]{1,0:T(8,128)(2,1)}, u32[]{:S(2)}, u32[]{:S(2)}) collective-permute-start(bf16[512,1024]{1,0:T(8,128)(2,1)} %get-tuple-element.150), channel_id=1, source_target_pairs={{0,16},{16,0},{1,17},{17,1},{2,18},{18,2},{3,19},{19,3},{4,20},{20... | collective-permute-start | bytes 3145736 | tf_op jit(solution)/shard_map/ppermute | solution.py:979
  450.7 408.5 %all-to-all-start.3 = ((bf16[16,2,32,1024]{3,2,1,0:T(8,128)(2,1)}), bf16[16,2,32,1024]{3,2,1,0:T(8,128)(2,1)}, u32[]{:S(2)}, u32[]{:S(2)}) async-start(bf16[16,2,32,1024]{3,2,1,0:T(8,128)(2,1)} %broadcast_select_fusion), calls=%async_computation.3 | async-start | bytes 4194304 | tf_op jit(solution)/shard_map/all_to_all | solution.py:918
  455.2 3.3 copy-start.12
  455.2 3.3 copy-start.6
  455.2 3.9 copy-start.8
  455.2 4.8 copy-start.11
  455.2 4.9 copy-start.5
  455.2 5.0 copy-start.7
  845.2 12.5 %copy-start.4 = (f32[96,128]{1,0:T(8,128)S(1)}, f32[96,128]{1,0:T(8,128)}, u32[]{:S(2)}) copy-start(f32[96,128]{1,0:T(8,128)} %get-tuple-element.125) | copy-start | bytes 147460
  858.5 3.9 copy-start.1

commit v3 on v2

--- a/solution.py
+++ b/solution.py
@@ -200,44 +200,90 @@
     return full
 
 
-def reduce_kernel(
-    count, parts, small,
-    total, small_total, landing,
-    own, came, across_half, kept, from_x, *rest
-):
+SENT_RING = 4
+LAND_RING = 5
+
+
+def device_of(number, groups):
+    return lax.rem(number, 2) * groups + number // 2
+
+
+def reduce_kernel(count, layers, small, grads, results, permutation, outs, scratch):
+    total, small_total, landing, dealt, acts = outs
+    (own, came, across_half, kept, from_x), rest = scratch[:5], scratch[5:]
     halves, rest = rest[:count], rest[count:]
-    (small_own, small_recv, send0, recv0, send_x, recv_x, send_rs, recv_rs, send_ag, recv_ag,
-     load_sem, came_sem, piece_sem, small_send, small_arrive) = rest
+    (spread, ordered, small_own, small_recv, send0, recv0, send_x, recv_x, send_rs, recv_rs,
+     send_ag, recv_ag, load_sem, came_sem, piece_sem, small_send, small_arrive, deal_send,
+     deal_recv, home_send, home_recv, act_sem, total_sem) = rest
     core = lax.axis_index("section")
     side = lax.axis_index("shard")
+    replica = lax.axis_index("replica")
     bits = my_bits(count)
     sibling = {"section": 1 - core}
     facing = {"shard": 1 - side}
     everything = (slice(None),) * count
     rows = kept.shape[-2]
-    greet([sibling, facing] + [across(p, count, bits) for p in range(count)])
+    keep_ring = kept.shape[0]
+    replicas = 1 << count
+    groups = 2 * replicas
+    group = side * replicas + replica
+    me = core * groups + group
+    chunk = spread.shape[1]
+
+    barrier = pltpu.get_barrier_semaphore()
+
+    def place(device):
+        return {
+            "section": device // groups,
+            "shard": lax.rem(device, groups) // replicas,
+            "replica": lax.rem(device, replicas),
+        }
+
+    def hello(step, carry):
+        pl.semaphore_signal(
+            barrier, inc=1, device_id=place(lax.rem(me + step, 2 * groups)),
+            device_id_type=pl.DeviceIdType.MESH,
+        )
+        return carry
+
+    lax.fori_loop(1, 2 * groups, hello, 0)
+    pl.semaphore_wait(barrier, 2 * groups - 1)
 
     ranges, at = [], 0
-    for part in parts:
-        ranges.append((part, at, at + part.shape[2]))
-        at += part.shape[2]
-
-    def core_copy(unit):
-        source = landing.at[unit]
-        if isinstance(unit, int):
-            part, low, _ = [entry for entry in ranges if entry[1] <= unit < entry[2]][0]
-            source = part.at[1 - core, :, unit - low]
+    for index in range(len(layers[0])):
+        ranges.append((index, at, at + layers[0][index].shape[1]))
+        at += layers[0][index].shape[1]
+
+    def core_copy(unit, source=None):
+        source = landing.at[unit] if source is None else source
         return remote(source, landing.at[unit], send0.at[unit], recv0.at[unit], sibling)
+
+    def send_core(owner):
+        for index, low, high in ranges:
+            for unit in range(low, high):
+                core_copy(unit, layers[owner][index].at[:, unit - low]).start()
+
+    def own_load(source, slot):
+        return pltpu.make_async_copy(source, own.at[slot], load_sem.at[slot])
+
+    def start_load(unit):
+        for owner in range(2):
+            for index, low, high in ranges:
+                @pl.when(jnp.logical_and(core == owner, jnp.logical_and(unit >= low, unit < high)))
+                def _():
+                    own_load(layers[owner][index].at[:, unit - low], lax.rem(unit, 2)).start()
 
     def x_copy(unit):
         return remote(
-            across_half.at[unit], from_x.at[unit], send_x.at[unit], recv_x.at[unit], facing
+            across_half.at[lax.rem(unit, SENT_RING)], from_x.at[lax.rem(unit, LAND_RING)],
+            send_x.at[unit], recv_x.at[unit], facing,
         )
 
     def rs_copy(unit, p):
+        slot = lax.rem(unit, keep_ring)
         return remote(
-            kept.at[(unit,) + everything[:p] + (1 - bits[p],) + bits[p + 1 :]],
-            halves[p].at[unit],
+            kept.at[(slot,) + everything[:p] + (1 - bits[p],) + bits[p + 1 :]],
+            halves[p].at[lax.rem(unit, LAND_RING)],
             send_rs.at[p, unit],
             recv_rs.at[p, unit],
             across(p, count, bits),
@@ -245,7 +291,7 @@
 
     def ag_copy(unit, p):
         where = (unit,) + everything[:p] + bits[p:]
-        source = kept.at[(unit,) + bits] if p == 0 else total.at[where]
+        source = kept.at[(lax.rem(unit, keep_ring),) + bits] if p == 0 else total.at[where]
         return remote(
             source, total.at[where], send_ag.at[p, unit], recv_ag.at[p, unit],
             across(p, count, bits),
@@ -259,17 +305,9 @@
 
     def piece_copy(unit):
         return pltpu.make_async_copy(
-            kept.at[(unit,) + bits], total.at[(unit,) + bits], piece_sem.at[unit]
+            kept.at[(lax.rem(unit, keep_ring),) + bits], total.at[(unit,) + bits],
+            piece_sem.at[unit],
         )
-
-    def own_load(part, index, slot):
-        return pltpu.make_async_copy(part.at[core, :, index], own.at[slot], load_sem.at[slot])
-
-    def start_load(unit):
-        for part, low, high in ranges:
-            @pl.when(jnp.logical_and(unit >= low, unit < high))
-            def _():
-                own_load(part, unit - low, lax.rem(unit, 2)).start()
 
     def small_copy(step):
         partner = [sibling, facing] + [across(p, count, bits) for p in range(count)]
@@ -278,12 +316,95 @@
             source, small_recv.at[step], small_send.at[step], small_arrive.at[step], partner[step]
         )
 
+    def spread_copy(target):
+        layer_rows = pl.ds(pl.multiple_of(lax.rem(target, groups) * chunk, chunk), chunk)
+        return [
+            remote(
+                grads[layer].at[layer_rows], spread.at[me], deal_send.at[target],
+                deal_recv.at[me], place(target),
+            )
+            for layer in range(2)
+        ]
+
+    def spread_own():
+        layer_rows = pl.ds(pl.multiple_of(group * chunk, chunk), chunk)
+        return [
+            pltpu.make_async_copy(grads[layer].at[layer_rows], spread.at[me], deal_recv.at[me])
+            for layer in range(2)
+        ]
+
+    def spread_start(step, carry):
+        target = lax.rem(me + step, 2 * groups)
+        for layer in range(2):
+            @pl.when(target // groups == layer)
+            def _():
+                spread_copy(target)[layer].start()
+        return carry
+
+    def spread_wait(step, carry):
+        source = lax.rem(me + step, 2 * groups)
+        remote(
+            spread.at[source], spread.at[source], deal_send.at[source], deal_recv.at[source],
+            place(source),
+        ).wait_recv()
+        return carry
+
+    def home_copy(target):
+        there = lax.rem(target, groups)
+        return remote(
+            ordered.at[pl.ds(2 * there, 2)], dealt.at[:, group], home_send.at[there],
+            home_recv.at[group], {"shard": there // replicas, "replica": lax.rem(there, replicas)},
+        )
+
+    def home_own():
+        return pltpu.make_async_copy(
+            ordered.at[pl.ds(2 * group, 2)], dealt.at[:, group], home_recv.at[group]
+        )
+
+    def home_start(step, carry):
+        home_copy(lax.rem(group + step, groups)).start()
+        return carry
+
+    def home_wait(step, carry):
+        source = lax.rem(group + step, groups)
+        remote(
+            dealt.at[:, source], dealt.at[:, source], home_send.at[source], home_recv.at[source],
+            {"shard": source // replicas, "replica": lax.rem(source, replicas)},
+        ).wait_recv()
+        return carry
+
+    def act_copies(layer):
+        sent = remote(
+            results[1 - layer], acts.at[layer], act_sem.at[0], act_sem.at[1], sibling
+        )
+        held = pltpu.make_async_copy(results[layer], came.at[0], act_sem.at[2])
+        return sent, held
+
     small_copy(0).start()
-
-    for unit in range(UNITS):
-        core_copy(unit).start()
-    own_load(parts[0], 0, 0).start()
+    for owner in range(2):
+        @pl.when(core == 1 - owner)
+        def _():
+            send_core(owner)
+    start_load(0)
+    for layer in range(2):
+        @pl.when(core == layer)
+        def _():
+            spread_own()[layer].start()
+    lax.fori_loop(1, 2 * groups, spread_start, 0)
+    for layer in range(2):
+        @pl.when(core == layer)
+        def _():
+            sent, held = act_copies(layer)
+            sent.start()
+            held.start()
+            held.wait()
+    store = pltpu.make_async_copy(came.at[0], acts.at[core], act_sem.at[3])
+    store.start()
+    store.wait()
     small_steps = count + 2
+
+    def places_of(index, dims):
+        return tuple((lax.rem(index // (1 << (dims - 1 - q)), 2) for q in range(dims)))
 
     def tick(now, carry):
         for step in range(small_steps):
@@ -295,6 +416,29 @@
                 if step + 1 < small_steps:
                     small_copy(step + 1).start()
 
+        @pl.when(now == DEAL_TICK)
+        def _():
+            spread_own()[0].wait()
+            lax.fori_loop(1, 2 * groups, spread_wait, 0)
+
+            def reorder(slot, c):
+                ordered[slot] = spread[device_of(permutation[slot], groups)]
+                return c
+
+            lax.fori_loop(0, 2 * groups, reorder, 0)
+            home_own().start()
+            lax.fori_loop(1, groups, home_start, 0)
+
+        @pl.when(jnp.logical_and(now >= SENT_RING, now < UNITS + SENT_RING))
+        def _():
+            x_copy(now - SENT_RING).wait_send()
+
+        @pl.when(jnp.logical_and(now >= keep_ring, now < UNITS + keep_ring))
+        def _():
+            for p in range(count):
+                rs_copy(now - keep_ring, p).wait_send()
+            ag_copy(now - keep_ring, 0).wait_send()
+
         @pl.when(now < UNITS)
         def _():
             unit = now
@@ -307,11 +451,14 @@
             core_copy(unit).wait_recv()
             arrived = pltpu.make_async_copy(landing.at[unit], came, came_sem)
             arrived.start()
-            own_load(parts[0], 0, slot).wait()
+            own_load(landing.at[unit], slot).wait()
             arrived.wait()
+            out_slot = lax.rem(unit, SENT_RING)
+            kept_slot = lax.rem(unit, keep_ring)
+
             def add(block, c):
                 where = pl.ds(pl.multiple_of(block * 32, 32), 32)
-                across_half[unit, where] = own[slot, 1 - side, where] + came[1 - side, where]
+                across_half[out_slot, where] = own[slot, 1 - side, where] + came[1 - side, where]
                 return c
 
             lax.fori_loop(0, 16, add, 0)
@@ -319,10 +466,8 @@
 
             def add_kept(index, c):
                 where = pl.ds(pl.multiple_of(index * rows, rows), rows)
-                places = tuple(
-                    (lax.rem(index // (1 << (count - 1 - p)), 2) for p in range(count))
-                )
-                kept[(unit,) + places] = own[slot, side, where] + came[side, where]
+                mine = (kept_slot,) + places_of(index, count)
+                kept[mine] = own[slot, side, where] + came[side, where]
                 return c
 
             lax.fori_loop(0, 1 << count, add_kept, 0)
@@ -330,14 +475,14 @@
         @pl.when(jnp.logical_and(now >= 1, now < UNITS + 1))
         def _():
             unit = now - 1
+            slot = lax.rem(unit, keep_ring)
+            land = lax.rem(unit, LAND_RING)
             x_copy(unit).wait_recv()
 
             def add(index, c):
                 where = pl.ds(pl.multiple_of(index * rows, rows), rows)
-                places = tuple(
-                    (lax.rem(index // (1 << (count - 1 - p)), 2) for p in range(count))
-                )
-                kept[(unit,) + places] = kept[(unit,) + places] + from_x[unit, where]
+                mine = (slot,) + places_of(index, count)
+                kept[mine] = kept[mine] + from_x[land, where]
                 return c
 
             lax.fori_loop(0, 1 << count, add, 0)
@@ -349,12 +494,13 @@
             @pl.when(jnp.logical_and(now >= 2 + step, now < UNITS + 2 + step))
             def _():
                 unit = now - (2 + step)
+                slot = lax.rem(unit, keep_ring)
+                land = lax.rem(unit, LAND_RING)
                 rs_copy(unit, p).wait_recv()
 
                 def add(index, c):
-                    places = tuple((lax.rem(index // (1 << (p - 1 - q)), 2) for q in range(p)))
-                    mine = (unit,) + places + bits[p:]
-                    kept[mine] = kept[mine] + halves[p][(unit,) + places]
+                    mine = (slot,) + places_of(index, p) + bits[p:]
+                    kept[mine] = kept[mine] + halves[p][(land,) + places_of(index, p)]
                     return c
 
                 if p == 0:
@@ -379,55 +525,85 @@
 
         return carry
 
-    lax.fori_loop(0, UNITS + 2 + 2 * count, tick, 0)
-    out = pltpu.make_async_copy(small_own.at[small_steps - 1], small_total, piece_sem.at[UNITS])
+    lax.fori_loop(0, UNITS + max(keep_ring, 2 + 2 * count), tick, 0)
+    out = pltpu.make_async_copy(small_own.at[small_steps - 1], small_total, total_sem)
     out.start()
 
     def last(unit, carry):
         core_copy(unit).wait_send()
-        x_copy(unit).wait_send()
-        for p in range(count):
-            rs_copy(unit, p).wait_send()
+        for p in range(1, count):
             ag_copy(unit, p).wait_send()
         return carry
 
     lax.fori_loop(0, UNITS, last, 0)
     for step in range(small_steps):
         small_copy(step).wait_send()
+
+    def spread_done(step, carry):
+        spread_copy(lax.rem(me + step, 2 * groups))[0].wait_send()
+        return carry
+
+    def home_done(step, carry):
+        home_copy(lax.rem(group + step, groups)).wait_send()
+        return carry
+
+    lax.fori_loop(1, 2 * groups, spread_done, 0)
+    home_own().wait()
+    lax.fori_loop(1, groups, home_wait, 0)
+    lax.fori_loop(1, groups, home_done, 0)
+    act = remote(results[0], acts.at[1 - core], act_sem.at[0], act_sem.at[1], sibling)
+    act.wait_send()
+    act.wait_recv()
     out.wait()
 
 
-def reduce_grads(parts, small, count):
+DEAL_TICK = 5
+
+
+def reduce_grads(layers, small, grads, results, permutation, count):
     cut = (2,) * count
     rows = 512 // (1 << count)
     narrow = cut + (rows, 1024)
     dma = pltpu.SemaphoreType.DMA
-
-    held = len(parts)
+    held = len(layers[0])
+    groups = 2 << count
+    slots, width = grads[0].shape
+    chunk = slots // groups
+    keep_ring = count + 5
 
     def kernel(*refs):
-        reduce_kernel(count, refs[:held], *refs[held:])
+        lower, upper, refs = refs[:held], refs[held : 2 * held], refs[2 * held :]
+        reduce_kernel(
+            count, (lower, upper), refs[0], refs[1:3], refs[3:5], refs[5], refs[6:11], refs[11:]
+        )
 
     vectors = small.shape[1:]
-    total, small_total, _ = pl.pallas_call(
+    anywhere = pl.BlockSpec(memory_space=pl.ANY)
+    total, small_total, _, dealt, acts = pl.pallas_call(
         kernel,
         out_shape=[
             jax.ShapeDtypeStruct((UNITS,) + narrow, jnp.bfloat16),
             jax.ShapeDtypeStruct(vectors, jnp.float32),
             jax.ShapeDtypeStruct((UNITS, 2, 512, 1024), jnp.bfloat16),
-        ],
-        in_specs=[pl.BlockSpec(memory_space=pl.ANY)] * held
-        + [pl.BlockSpec(memory_space=pltpu.VMEM)],
-        out_specs=[pl.BlockSpec(memory_space=pl.ANY)] * 3,
+            jax.ShapeDtypeStruct((2, groups, chunk, width), jnp.bfloat16),
+            jax.ShapeDtypeStruct((2, slots, width), jnp.bfloat16),
+        ],
+        in_specs=[anywhere] * (2 * held)
+        + [pl.BlockSpec(memory_space=pltpu.VMEM)]
+        + [anywhere] * 4
+        + [pl.BlockSpec(memory_space=pltpu.SMEM)],
+        out_specs=[anywhere] * 5,
         scratch_shapes=[
             pltpu.VMEM((2, 2, 512, 1024), jnp.bfloat16),
             pltpu.VMEM((2, 512, 1024), jnp.bfloat16),
-            pltpu.VMEM((UNITS, 512, 1024), jnp.bfloat16),
-            pltpu.VMEM((UNITS,) + narrow, jnp.bfloat16),
-            pltpu.VMEM((UNITS, 512, 1024), jnp.bfloat16),
+            pltpu.VMEM((SENT_RING, 512, 1024), jnp.bfloat16),
+            pltpu.VMEM((keep_ring,) + narrow, jnp.bfloat16),
+            pltpu.VMEM((LAND_RING, 512, 1024), jnp.bfloat16),
         ]
-        + [pltpu.VMEM((UNITS,) + (2,) * p + (rows, 1024), jnp.bfloat16) for p in range(count)]
+        + [pltpu.VMEM((LAND_RING,) + (2,) * p + (rows, 1024), jnp.bfloat16) for p in range(count)]
         + [
+            pltpu.VMEM((2 * groups, chunk, width), jnp.bfloat16),
+            pltpu.VMEM((2 * groups, chunk, width), jnp.bfloat16),
             pltpu.VMEM((count + 2,) + vectors, jnp.float32),
             pltpu.VMEM((count + 2,) + vectors, jnp.float32),
             dma((UNITS,)),
@@ -440,16 +616,24 @@
             dma((count, UNITS)),
             dma((2,)),
             dma,
-            dma((UNITS + 1,)),
+            dma((UNITS,)),
             dma((count + 2,)),
             dma((count + 2,)),
+            dma((2 * groups,)),
+            dma((2 * groups,)),
+            dma((groups,)),
+            dma((groups,)),
+            dma((4,)),
+            dma,
         ],
         compiler_params=pltpu.CompilerParams(
             collective_id=1, has_side_effects=True, vmem_limit_bytes=VMEM_LIMIT
         ),
         name="reduce_grads",
-    )(*parts, small)
-    return total.reshape(UNITS, 512, 1024), small_total
+    )(*layers[0], *layers[1], small, *grads, *results, permutation)
+    return (
+        total.reshape(UNITS, 512, 1024), small_total, dealt.reshape(2, slots, width), acts
+    )
 
 
 HEAD_DIM = 64
@@ -599,8 +783,8 @@
     d2_out[...] = mm_left(act[...], d_outer).astype(BF).reshape(d2_out.shape)
     d1 = mm_left(low[...], d_inner).astype(BF)
     half = d1.shape[0] // 2
-    d1_out[0, 0, 0] = d1[:half]
-    d1_out[0, 1, 0] = d1[half:]
+    d1_out[0, 0] = d1[:half]
+    d1_out[1, 0] = d1[half:]
 
     @pl.when(step == pl.num_programs(0) - 1)
     def _():
@@ -657,8 +841,8 @@
     for at, value in enumerate((d_q, d_k, d_v)):
         weight = mm_left(rows, value).astype(BF)
         half = weight.shape[0] // 2
-        dqkv_out[0, 0, at] = weight[:half]
-        dqkv_out[0, 1, at] = weight[half:]
+        dqkv_out[0, at] = weight[:half]
+        dqkv_out[1, at] = weight[half:]
     do_out[...] = mm_left(context[...], d_att).astype(BF).reshape(do_out.shape)
 
     @pl.when(step == pl.num_programs(0) - 1)
@@ -674,7 +858,7 @@
     return jax.ShapeDtypeStruct(shape, dtype)
 
 
-def grid_call(kernel, steps, in_specs, out_specs, out_shape, scratch, name, flops, aliases=None):
+def grid_call(kernel, steps, in_specs, out_specs, out_shape, scratch, name, flops):
     return pl.pallas_call(
         kernel,
         grid_spec=pltpu.PrefetchScalarGridSpec(
@@ -685,7 +869,6 @@
             scratch_shapes=scratch,
         ),
         out_shape=out_shape,
-        input_output_aliases=aliases or {},
         compiler_params=pltpu.CompilerParams(
             dimension_semantics=("arbitrary",), vmem_limit_bytes=VMEM_LIMIT
         ),
@@ -698,10 +881,6 @@
 
 def rank_two(vector):
     return vector.reshape(1, -1)
-
-
-def layer_of(shape, layer):
-    return pl.BlockSpec((None,) + shape, None)
 
 
 def attend(length, x, layer, weights, vectors):
@@ -763,7 +942,7 @@
     )(length, unit1, g1, b1, w1, bi, w2, b2, g2, bb2)
 
 
-def feed_back(length, grad, unit2, scale2, unit1, scale1, act, slope, layer, w1, w2, vectors, held):
+def feed_back(length, grad, unit2, scale2, unit1, scale1, act, slope, layer, w1, w2, vectors):
     slots, width = unit1.shape
     hidden = w1.shape[-1]
     steps = hidden // HIDDEN_BLOCK
@@ -774,14 +953,13 @@
     thin = whole((slots, 128))
     band = pl.BlockSpec((slots, HIDDEN_BLOCK), lambda j, *_: (0, j))
     d1_block = pl.BlockSpec(
-        (1, 2, 1, 512, HIDDEN_BLOCK), lambda j, *_: (layer, 0, j // per, 0, j % per)
+        (2, 1, 512, HIDDEN_BLOCK), lambda j, *_: (0, j // per, 0, j % per)
     )
     pairs = HIDDEN_BLOCK // 512
     d2_block = pl.BlockSpec(
-        (1, 1, pairs, 512, width),
-        lambda j, *_: (layer, j // (steps // 2), j % (steps // 2), 0, 0),
-    )
-    extra = () if held is None else tuple(held)
+        (1, pairs, 512, width),
+        lambda j, *_: (j // (steps // 2), j % (steps // 2), 0, 0),
+    )
     return grid_call(
         feed_back_kernel,
         steps,
@@ -789,14 +967,13 @@
             row, row, thin, line, row, thin, line, line, band, band,
             pl.BlockSpec((None, width, HIDDEN_BLOCK), lambda j, *_: (layer, 0, j)),
             pl.BlockSpec((None, HIDDEN_BLOCK, width), lambda j, *_: (layer, j, 0)),
-        ]
-        + [pl.BlockSpec(memory_space=pl.ANY)] * len(extra),
+        ],
         [
             d1_block, d2_block, row, whole((6, width)),
             pl.BlockSpec((1, HIDDEN_BLOCK), lambda j, *_: (0, j)),
         ],
         [
-            struct((2, 2, 4, 512, 1024), BF), struct((2, 2, 4, 512, 1024), BF),
+            struct((2, 4, 512, 1024), BF), struct((2, 4, 512, 1024), BF),
             struct((slots, width), F32), struct((6, width), F32), struct((1, hidden), F32),
         ],
         [
@@ -805,11 +982,10 @@
         ],
         "feed_back",
         18000000000,
-        {13 + i: i for i in range(len(extra))},
-    )(length, grad, unit2, scale2, g2, unit1, scale1, g1, b1, act, slope, w1, w2, *extra)
-
-
-def attend_back(length, first, x, q, k, v, log, context, layer, weights, held):
+    )(length, grad, unit2, scale2, g2, unit1, scale1, g1, b1, act, slope, w1, w2)
+
+
+def attend_back(length, first, x, q, k, v, log, context, layer, weights):
     wq, wk, wv, wo = weights
     slots, width = x.shape
     steps = width // WIDE
@@ -817,7 +993,6 @@
     band = pl.BlockSpec((slots, WIDE), lambda j, *_: (0, j))
     row = whole((slots, width))
     per = 512 // WIDE
-    extra = () if held is None else tuple(held)
     return grid_call(
         attend_back_kernel,
         steps,
@@ -826,23 +1001,21 @@
             pl.BlockSpec((None, 8, slots), lambda j, *_: (j, 0, 0)),
             band, columns, columns, columns,
             pl.BlockSpec((None, WIDE, width), lambda j, *_: (layer, j, 0)),
-        ]
-        + [pl.BlockSpec(memory_space=pl.ANY)] * len(extra),
+        ],
         [
-            pl.BlockSpec((1, 2, 3, 512, WIDE), lambda j, *_: (layer, 0, 0, 0, j)),
-            pl.BlockSpec((1, 1, 1, WIDE, width), lambda j, *_: (layer, j // per, 0, j % per, 0)),
+            pl.BlockSpec((2, 3, 512, WIDE), lambda j, *_: (0, 0, 0, j)),
+            pl.BlockSpec((1, 1, WIDE, width), lambda j, *_: (j // per, 0, j % per, 0)),
             row,
             pl.BlockSpec((2, WIDE), lambda j, *_: (0, j)),
         ],
         [
-            struct((2, 2, 3, 512, 1024), BF), struct((2, 2, 1, 512, 1024), BF),
+            struct((2, 3, 512, 1024), BF), struct((2, 1, 512, 1024), BF),
             struct((slots, width), BF), struct((2, width), F32),
         ],
         [pltpu.VMEM((slots, width), BF), pltpu.VMEM((slots, width), F32)],
         "attend_back",
         20000000000,
-        {12 + i: i for i in range(len(extra))},
-    )(length, first, x, q, k, v, log, context, wq, wk, wv, wo, *extra)
+    )(length, first, x, q, k, v, log, context, wq, wk, wv, wo)
 
 
 from jax.sharding import PartitionSpec as P
@@ -887,10 +1060,6 @@
         out.append(halves[:, at : at + 512 * width].reshape(-1).astype(jnp.float32))
         at += 512 * width
     return tuple(out)
-
-
-def device_of(number, groups):
-    return lax.rem(number, 2) * groups + number // 2
 
 
 def own_cotangent(cotangent, permutation, groups):
@@ -909,16 +1078,6 @@
     return lax.all_to_all(ordered, ALL, 0, 0, tiled=True).reshape(shape)
 
 
-def dealt_grads(both, permutation, groups):
-    slots, width = both.shape[1:]
-    rows = slots // groups
-    spread = lax.all_to_all(both.reshape(2 * groups, rows, width), ALL, 0, 0, tiled=True)
-    ordered = jnp.take(spread, device_of(permutation, groups), axis=0)
-    ordered = ordered.reshape(groups, 2, rows, width)
-    home = lax.all_to_all(ordered, GROUP, 0, 0, tiled=True)
-    return home.transpose(1, 0, 2, 3).reshape(2, slots, width)
-
-
 def layer_forward(length, x, layer, weights, vectors):
     bq, bv, bo, g1, b1, bi, b2, g2, bb2 = vectors
     q, k, v, log, context, unit1, scale1 = attend(length, x, layer, weights[:4], (bq, bv, bo))
@@ -928,16 +1087,15 @@
     return result, (q, k, v, log, context, unit1, scale1, act, slope, unit2, scale2)
 
 
-def layer_backward(length, grad, x, layer, weights, vectors, stored, held):
+def layer_backward(length, grad, x, layer, weights, vectors, stored):
     q, k, v, log, context, unit1, scale1, act, slope, unit2, scale2 = stored
     g1, b1, g2 = vectors[3], vectors[4], vectors[7]
     d1, d2, first, rows, inner = feed_back(
         length, grad, unit2, scale2, unit1, scale1, act, slope, layer, weights[4], weights[5],
-        (g1, b1, g2), None if held is None else held[2:],
+        (g1, b1, g2),
     )
     d_qkv, d_o, d_x, sums = attend_back(
-        length, first, x, q, k, v, log, context, layer, weights[:4],
-        None if held is None else held[:2],
+        length, first, x, q, k, v, log, context, layer, weights[:4]
     )
     vectors = (sums[0], sums[1], rows[5], rows[3], rows[4], inner[0], rows[0], rows[1], rows[2])
     small = jnp.concatenate([v.reshape(2, -1) for v in vectors], axis=1).reshape(96, 128)
@@ -967,18 +1125,16 @@
     grad = own_cotangent(cotangent, permutation, groups)
     lower, lower_stored = layer_forward(length, x, 0, weights, shared[0])
     upper, upper_stored = layer_forward(length, lower, 1, weights, shared[1])
-    upper_grad, upper_small, parts = layer_backward(
-        length, grad, lower, 1, weights, shared[1], upper_stored, None
-    )
-    lower_grad, lower_small, parts = layer_backward(
-        length, upper_grad, x, 0, weights, shared[0], lower_stored, parts
-    )
-    total, small = reduce_grads(parts, jnp.stack([lower_small, upper_small]), count)
-    sent = jnp.where(core == 0, upper, lower)
-    kept = jnp.where(core == 0, lower, upper)
-    came = lax.ppermute(sent, "section", [(0, 1), (1, 0)])
-    activations = jnp.where(core == 0, jnp.stack([kept, came]), jnp.stack([came, kept]))[None]
-    input_grads = dealt_grads(jnp.stack([lower_grad, upper_grad]), permutation, groups)[None]
+    upper_grad, upper_small, upper_parts = layer_backward(
+        length, grad, lower, 1, weights, shared[1], upper_stored
+    )
+    lower_grad, lower_small, lower_parts = layer_backward(
+        length, upper_grad, x, 0, weights, shared[0], lower_stored
+    )
+    total, small, input_grads, activations = reduce_grads(
+        (lower_parts, upper_parts), jnp.stack([lower_small, upper_small]),
+        (lower_grad, upper_grad), (lower, upper), permutation, count,
+    )
     side = lax.axis_index("shard")
     own = lax.dynamic_index_in_dim(small.reshape(2, -1), side, 0, keepdims=False)
     pieces, at = [], 0
@@ -987,7 +1143,7 @@
         at += 512 * width
     dq, dk, dv, do, d1, d2 = unpack(total)
     return (
-        activations, input_grads, dq, pieces[0], dk, dv, pieces[1], do, pieces[2], pieces[3],
+        activations[None], input_grads[None], dq, pieces[0], dk, dv, pieces[1], do, pieces[2], pieces[3],
         pieces[4], d1, pieces[5], d2, pieces[6], pieces[7], pieces[8],
     )
 

time: 872 us -> 838 us (0.961)
  waiting for transfers between devices: 46.8 us -> 0.01 us
  Pallas kernels: 743 us -> 774 us
  other arithmetic: 15.4 us -> 4.34 us
  starting transfers between devices: 27 us -> 16 us
    all_to_all x2 -> x0, waiting for transfers between devices: 46.8 us -> none  [the longest x1 46.8 us: dealt_grads(): lax.all_to_all(both.reshape(2 * groups, rows, width), ALL, 0, 0, tiled=True)]
    pallas_call x1, Pallas kernels: 383 us -> 415 us  [reduce_grads(): pl.pallas_call(kernel, out_shape=[jax.ShapeDtypeStruct((UNITS,) + narrow,...]
    all_to_all x2 -> x0, starting transfers between devices: 10.6 us -> none  [the longest x1 6.16 us: dealt_grads(): lax.all_to_all(both.reshape(2 * groups, rows, width), ALL, 0, 0, tiled=True)]
    unnamed x89 -> x81, local copies, waits for them, and re-layouts: 16.7 us -> 21.1 us
  transfers between devices with their start and end apart: 5 -> 2, of which waited for: 1 -> 0; matrix products, arithmetic and copies ran while one was open for 4% -> 2% of each run, Pallas kernels for 72% -> 27%
where the time goes in v3:
time: 838 us; the launch traced here: 828 us
  Pallas kernels  774 us (92%)
  local copies, waits for them, and re-layouts  31.7 us (4%)
  starting transfers between devices  16 us (2%)
    pallas_call x1, Pallas kernels, reduce_grads(): pl.pallas_call(kernel, out_shape=[jax.ShapeDtypeStruct((UNITS,) + narrow,...  415 us
    pallas_call x1, Pallas kernels, gather_weights(): pl.pallas_call(kernel, out_shape=outs, in_specs=[pl.BlockSpec(memory_spac...  146 us
    pallas_call x2, Pallas kernels, attend_back(): grid_call(attend_back_kernel, steps, [row, row, band, band, band, pl.Bloc...  60.3 us
    pallas_call x2, Pallas kernels, feed_back(): grid_call(feed_back_kernel, steps, [row, row, thin, line, row, thin, line...  60 us
    pallas_call x2, Pallas kernels, attend(): grid_call(attend_kernel, steps, [whole((slots, width)), columns, columns,...  40.8 us
    pallas_call x2, Pallas kernels, feed(): grid_call(feed_kernel, steps, [whole((slots, width)), line, line, pl.Bloc...  39.9 us
    unnamed x81, local copies, waits for them, and re-layouts  21.1 us
  transfers between devices with their start and end apart: 2, of which 0 were waited for; matrix products, arithmetic and copies ran while one was open for 2% of the time, Pallas kernels for 27%

profile of v3, /device:TPU:0, one launch (start us, length us, event | category | flops | bytes accessed | tf_op | source)
XLA Modules:
  0.0 828.0 jit_solution(2656913323307818513)
XLA Ops:
  0.8 1.5 copy-done
  2.3 1.0 constant_dynamic-slice_fusion.1
  3.3 7.3 all-to-all-start
  13.5 145.9 %gather_weights.1 = (bf16[2,2,2,2,2,64,1024]{6,5,4,3,2,1,0:T(8,128)(2,1)}, bf16[2,2,2,2,2,64,1024]{6,5,4,3,2,1,0:T(8,128)(2,1)}, bf16[2,2,2,2,2,64,1024]{6,5,4,3...) custom-call(bf16[2,2,2,64,1024]{4,3,2,1,0:T(8,128)(2,1)} %bitcast.13, ...), custom_call_target="tpu_custom_call" | custom-call | tf_op jit(solution)/shard_map/gather_weights/pallas_call | solution.py:181
  159.4 0.8 slice_bitcast_fusion
  160.4 2.3 dynamic-slice_bitcast_fusion.x
  162.7 0.6 copy.42
  168.7 20.4 %attend.2 = (bf16[512,1024]{1,0:T(8,128)(2,1)}, bf16[512,1024]{1,0:T(8,128)(2,1)}, bf16[512,1024]{1,0:T(8,128)(2,1)}, f32[4,8,512]{2,1,0:T(8,128)}, bf16[512,102...) custom-call(s32[1]{0:T(128)} %dynamic_slice.14.length, bf16[512,1024]{1,0:T(8,128)(2,1)} %dynamic-slice_bitcast_fusion.x, ...), custom_call_target="tpu_custom_call" | custom-call | flops 8999999488 | bytes 30000000 | tf_op jit(solution)/shard_map/attend/pallas_call | solution.py:893
  189.1 20.0 %feed.2 = (bf16[512,4096]{1,0:T(8,128)(2,1)}, bf16[512,4096]{1,0:T(8,128)(2,1)}, f32[512,1024]{1,0:T(8,128)}, f32[512,128]{1,0:T(8,128)}, bf16[512,1024]{1,0:T(8,128)(2,1)}) custom-call(s32[1]{0:T(128)} %dynamic_slice.14.length, f32[512,1024]{1,0:T(8,128)} %get-tuple-element.81.unit1, f32[1,1024]{1,0:T(1,128)} %bitcast.143, f32[1,1024]{1,0:T(1,128)} %bitcast.141, ...), custom_call_target="tpu_custom_call" | custom-call | flops 8999999488 | bytes 30000000 | tf_op jit(solution)/shard_map/feed/pallas_call | solution.py:924
  209.7 1.1 broadcast_select_fusion
  210.9 8.7 %all-to-all-start.1 = ((bf16[32,16,1024]{2,1,0:T(8,128)(2,1)}), bf16[32,16,1024]{2,1,0:T(8,128)(2,1)S(1)}, u32[]{:S(2)}, u32[]{:S(2)}) async-start(bf16[32,16,1024]{2,1,0:T(8,128)(2,1)} %broadcast_select_fusion), calls=%async_computation.1 | async-start | bytes 2097152 | tf_op jit(solution)/shard_map/all_to_all | solution.py:1078
  219.6 0.6 copy.52
  225.0 20.4 %attend.3 = (bf16[512,1024]{1,0:T(8,128)(2,1)}, bf16[512,1024]{1,0:T(8,128)(2,1)}, bf16[512,1024]{1,0:T(8,128)(2,1)}, f32[4,8,512]{2,1,0:T(8,128)}, bf16[512,102...) custom-call(s32[1]{0:T(128)} %dynamic_slice.14.length, bf16[512,1024]{1,0:T(8,128)(2,1)} %get-tuple-element.84.x.refs_11_, ...), custom_call_target="tpu_custom_call" | custom-call | flops 8999999488 | bytes 30000000 | tf_op jit(solution)/shard_map/attend/pallas_call | solution.py:893
  245.4 19.9 %feed.3 = (bf16[512,4096]{1,0:T(8,128)(2,1)}, bf16[512,4096]{1,0:T(8,128)(2,1)}, f32[512,1024]{1,0:T(8,128)}, f32[512,128]{1,0:T(8,128)}, bf16[512,1024]{1,0:T(8,128)(2,1)}) custom-call(s32[1]{0:T(128)} %dynamic_slice.14.length, f32[512,1024]{1,0:T(8,128)} %get-tuple-element.85.unit1, f32[1,1024]{1,0:T(1,128)} %bitcast.149, f32[1,1024]{1,0:T(1,128)} %bitcast.147, ...), custom_call_target="tpu_custom_call" | custom-call | flops 8999999488 | bytes 30000000 | tf_op jit(solution)/shard_map/feed/pallas_call | solution.py:924
  265.4 1.0 copy-done.3
  266.4 30.1 %feed_back.2 = (bf16[2,4,512,1024]{3,2,1,0:T(8,128)(2,1)}, bf16[2,4,512,1024]{3,2,1,0:T(8,128)(2,1)}, f32[512,1024]{1,0:T(8,128)}, f32[6,1024]{1,0:T(8,128)}, f32[1,4096]{1,0:T(1,128)}) custom-call(s32[1]{0:T(128)} %dynamic_slice.14.length, bf16[512,1024]{1,0:T(8,128)(2,1)} %bitcast.136, f32[512,1024]{1,0:T(8,128)} %get-tuple-element.86.unit2, ...), custom_call_target="tpu_custom_call" | custom-call | flops 17999998976 | bytes 30000000 | tf_op jit(solution)/shard_map/feed_back/pallas_call | solution.py:963
  297.0 1.4 reduce.79
  298.4 1.2 slice_reduce_fusion
  299.7 30.1 %attend_back.2 = (bf16[2,3,512,1024]{3,2,1,0:T(8,128)(2,1)}, bf16[2,1,512,1024]{3,2,1,0:T(8,128)(2,1)}, bf16[512,1024]{1,0:T(8,128)(2,1)}, f32[2,1024]{1,0:T(2,128)}) custom-call(s32[1]{0:T(128)} %dynamic_slice.14.length, f32[512,1024]{1,0:T(8,128)} %get-tuple-element.91.first, bf16[512,1024]{1,0:T(8,128)(2,1)} %get-tuple-element.84.x.refs_11_, ...), custom_call_target="tpu_custom_call" | custom-call | flops 20000000000 | bytes 30000000 | tf_op jit(solution)/shard_map/attend_back/pallas_call | solution.py:996
  329.8 0.8 slice_reduce_fusion.6
  330.6 29.9 %feed_back.3 = (bf16[2,4,512,1024]{3,2,1,0:T(8,128)(2,1)}, bf16[2,4,512,1024]{3,2,1,0:T(8,128)(2,1)}, f32[512,1024]{1,0:T(8,128)}, f32[6,1024]{1,0:T(8,128)}, f32[1,4096]{1,0:T(1,128)}) custom-call(s32[1]{0:T(128)} %dynamic_slice.14.length, bf16[512,1024]{1,0:T(8,128)(2,1)} %get-tuple-element.97.grad.refs_10_, f32[512,1024]{1,0:T(8,128)} %get-tuple-element.98.unit2, ...), custom_call_target="tpu_custom_call" | custom-call | flops 17999998976 | bytes 30000000 | tf_op jit(solution)/shard_map/feed_back/pallas_call | solution.py:963
  360.6 30.1 %attend_back.3 = (bf16[2,3,512,1024]{3,2,1,0:T(8,128)(2,1)}, bf16[2,1,512,1024]{3,2,1,0:T(8,128)(2,1)}, bf16[512,1024]{1,0:T(8,128)(2,1)}, f32[2,1024]{1,0:T(2,128)}) custom-call(s32[1]{0:T(128)} %dynamic_slice.14.length, f32[512,1024]{1,0:T(8,128)} %get-tuple-element.103.first, bf16[512,1024]{1,0:T(8,128)(2,1)} %dynamic-slice_bitcast_fusion.x, ...), custom_call_target="tpu_custom_call" | custom-call | flops 20000000000 | bytes 30000000 | tf_op jit(solution)/shard_map/attend_back/pallas_call | solution.py:996
  390.7 0.8 slice_reduce_fusion.14
  391.6 0.7 reduce.80
  392.7 0.6 pad_maximum_fusion.refs_8_
  393.4 415.1 %reduce_grads.1 = (bf16[12,2,2,2,64,1024]{5,4,3,2,1,0:T(8,128)(2,1)}, f32[96,128]{1,0:T(8,128)}, bf16[12,2,512,1024]{3,2,1,0:T(8,128)(2,1)}, bf16[2,16,32,1024]{3,2,1,0:T(8,128)(2,1)}, bf16[2,512,1024]{2,1,0:T(8,128)(2,1)}) custom-call(bf16[2,3,512,1024]{3,2,1,0:T(8,128)(2,1)} %get-tuple-element.109.refs_0_, ...), custom_call_target="tpu_custom_call" | custom-call | tf_op jit(solution)/shard_map/reduce_grads/pallas_call | solution.py:582
  808.5 0.8 reshape.439
  809.3 12.5 %unpack.1 = (f32[1,512,1024]{2,1,0:T(8,128)}, f32[1,512,1024]{2,1,0:T(8,128)}, f32[1,512,1024]{2,1,0:T(8,128)}, f32[1,512,1024]{2,1,0:T(8,128)}, f32[1,512,4096]{2,1,0:T(8,128)}, /*index=5*/f32[1,2048,1024]{2,1,0:T(8,128)}) custom-call(bf16[12,512,1024]{2,1,0:T(8,128)(2,1)} %bitcast.117, bf16[12,512,1024]{2,1,0:T(8,128)(2,1)} %bitcast.118, ...), custom_call_target="tpu_custom_call" | custom-call | tf_op jit(solution)/shard_map/unpack/pallas_call | solution.py:1036
  821.8 0.7 dynamic-slice.5
  822.5 0.7 fusion.3
  823.2 3.2 copy.85
  826.4 1.3 copy.86
  (123 shorter events, 14.9 us)
Async XLA Ops:
  0.7 1.6 copy-start
  0.7 10.0 %copy-start.8 = (bf16[1,512]{1,0:T(2,128)(2,1)S(1)}, bf16[1,512]{1,0:T(2,128)(2,1)}, u32[]{:S(2)}) copy-start(bf16[1,512]{1,0:T(2,128)(2,1)} %param.24) | copy-start | bytes 3076
  0.7 10.0 %copy-start.9 = (bf16[1,512]{1,0:T(2,128)(2,1)S(1)}, bf16[1,512]{1,0:T(2,128)(2,1)}, u32[]{:S(2)}) copy-start(bf16[1,512]{1,0:T(2,128)(2,1)} %param.27) | copy-start | bytes 3076
  0.7 10.0 %copy-start.10 = (bf16[1,512]{1,0:T(2,128)(2,1)S(1)}, bf16[1,512]{1,0:T(2,128)(2,1)}, u32[]{:S(2)}) copy-start(bf16[1,512]{1,0:T(2,128)(2,1)} %param.29) | copy-start | bytes 3076
  0.7 10.0 %copy-start.11 = (bf16[1,512]{1,0:T(2,128)(2,1)S(1)}, bf16[1,512]{1,0:T(2,128)(2,1)}, u32[]{:S(2)}) copy-start(bf16[1,512]{1,0:T(2,128)(2,1)} %param.30) | copy-start | bytes 3076
  0.7 10.1 %copy-start.12 = (bf16[1,512]{1,0:T(2,128)(2,1)S(1)}, bf16[1,512]{1,0:T(2,128)(2,1)}, u32[]{:S(2)}) copy-start(bf16[1,512]{1,0:T(2,128)(2,1)} %param.31) | copy-start | bytes 3076
  0.7 10.1 %copy-start.13 = (bf16[1,512]{1,0:T(2,128)(2,1)S(1)}, bf16[1,512]{1,0:T(2,128)(2,1)}, u32[]{:S(2)}) copy-start(bf16[1,512]{1,0:T(2,128)(2,1)} %param.35) | copy-start | bytes 3076
  0.7 10.1 %copy-start.14 = (bf16[1,512]{1,0:T(2,128)(2,1)S(1)}, bf16[1,512]{1,0:T(2,128)(2,1)}, u32[]{:S(2)}) copy-start(bf16[1,512]{1,0:T(2,128)(2,1)} %param.36) | copy-start | bytes 3076
  0.7 10.1 %copy-start.15 = (bf16[1,512]{1,0:T(2,128)(2,1)S(1)}, bf16[1,512]{1,0:T(2,128)(2,1)}, u32[]{:S(2)}) copy-start(bf16[1,512]{1,0:T(2,128)(2,1)} %param.37) | copy-start | bytes 3076
  0.8 10.2 %copy-start.7 = (bf16[1,2048]{1,0:T(2,128)(2,1)S(1)}, bf16[1,2048]{1,0:T(2,128)(2,1)}, u32[]{:S(2)}) copy-start(bf16[1,2048]{1,0:T(2,128)(2,1)} %param.33) | copy-start | bytes 12292
  3.3 205.8 %all-to-all-start = ((bf16[32,16,1024]{2,1,0:T(8,128)(2,1)}), bf16[32,16,1024]{2,1,0:T(8,128)(2,1)S(1)}, u32[]{:S(2)}, u32[]{:S(2)}) async-start(bf16[32,16,1024]{2,1,0:T(8,128)(2,1)} %bitcast), calls=%async_computation | async-start | bytes 2097152 | tf_op jit(solution)/shard_map/all_to_all | solution.py:1071
  12.9 0.6 copy-start.6
  13.5 146.7 %copy-start.16 = (s32[32]{0:T(128)S(1)}, s32[32]{0:T(128)}, u32[]{:S(2)}) copy-start(s32[32]{0:T(128)} %refs_13_.1) | copy-start | bytes 388
  13.5 154.6 %copy-start.17 = (s32[32]{0:T(128)S(1)}, s32[32]{0:T(128)}, u32[]{:S(2)}) copy-start(s32[32]{0:T(128)} %param.21) | copy-start | bytes 388
  210.9 54.5 %all-to-all-start.1 = ((bf16[32,16,1024]{2,1,0:T(8,128)(2,1)}), bf16[32,16,1024]{2,1,0:T(8,128)(2,1)S(1)}, u32[]{:S(2)}, u32[]{:S(2)}) async-start(bf16[32,16,1024]{2,1,0:T(8,128)(2,1)} %broadcast_select_fusion), calls=%async_computation.1 | async-start | bytes 2097152 | tf_op jit(solution)/shard_map/all_to_all | solution.py:1078
  265.4 1.0 copy-start.3
  360.5 31.0 %copy-start.5 = (f32[1,4096]{1,0:T(1,128)S(1)}, f32[1,4096]{1,0:T(1,128)}, u32[]{:S(2)}) copy-start(f32[1,4096]{1,0:T(1,128)} %get-tuple-element.119) | copy-start | bytes 49156
  360.6 31.7 %copy-start.4 = (f32[6,1024]{1,0:T(8,128)S(1)}, f32[6,1024]{1,0:T(8,128)}, u32[]{:S(2)}) copy-start(f32[6,1024]{1,0:T(8,128)} %get-tuple-element.118) | copy-start | bytes 73732
  821.8 4.6 copy-start.2
  823.2 4.6 copy-start.1

commit v4 on v1

v4 whole, which is shorter than its diff:
```python
import jax
import jax.numpy as jnp
from jax import lax
from jax.experimental import pallas as pl
from jax.experimental.pallas import tpu as pltpu

ALL = ("section", "shard", "replica")
GROUP = ("shard", "replica")
UNITS = 12
HALF = 256
VMEM_LIMIT = 64000000


def my_bits(count):
    replica = lax.axis_index("replica")
    return tuple((lax.rem(replica // (1 << (count - 1 - p)), 2) for p in range(count)))


def across(p, count, bits):
    replica = lax.axis_index("replica")
    weight = 1 << (count - 1 - p)
    return {"replica": replica + weight * (1 - 2 * bits[p])}


def place(device, replicas):
    groups = 2 * replicas
    return {
        "section": device // groups,
        "shard": lax.rem(device, groups) // replicas,
        "replica": lax.rem(device, replicas),
    }


def greet_all(me, devices, replicas):
    barrier = pltpu.get_barrier_semaphore()

    def hello(step, carry):
        pl.semaphore_signal(
            barrier, inc=1, device_id=place(lax.rem(me + step, devices), replicas),
            device_id_type=pl.DeviceIdType.MESH,
        )
        return carry

    lax.fori_loop(1, devices, hello, 0)
    pl.semaphore_wait(barrier, devices - 1)


def remote(src, dst, send_sem, recv_sem, partner):
    return pltpu.make_async_remote_copy(
        src_ref=src,
        dst_ref=dst,
        send_sem=send_sem,
        recv_sem=recv_sem,
        device_id=partner,
        device_id_type=pl.DeviceIdType.MESH,
    )


HEAD_DIM = 64
EPSILON = 1e-12
MASKED = -1000000000.0
HIDDEN_BLOCK = 512
WIDE = 256
BF = jnp.bfloat16
F32 = jnp.float32


def mm(a, b):
    return lax.dot_general(a, b, (((1,), (0,)), ((), ())), preferred_element_type=F32)


def mm_right(a, b):
    return lax.dot_general(a, b, (((1,), (1,)), ((), ())), preferred_element_type=F32)


def mm_left(a, b):
    return lax.dot_general(a, b, (((0,), (0,)), ((), ())), preferred_element_type=F32)


def normalized(values):
    average = jnp.mean(values, axis=-1, keepdims=True)
    centred = values - average
    variance = jnp.mean(centred * centred, axis=-1, keepdims=True)
    scale = lax.rsqrt(variance + EPSILON)
    return centred * scale, scale


def normalize_back(grad, unit, scale, gain):
    gs = grad * gain
    mean_gs = jnp.mean(gs, axis=-1, keepdims=True)
    mean_gn = jnp.mean(gs * unit, axis=-1, keepdims=True)
    return (gs - mean_gs - unit * mean_gn) * scale


def head_lanes(head):
    lane = lax.broadcasted_iota(jnp.int32, (1, WIDE), 1)
    return lane // HEAD_DIM == head


def row_sum(values):
    return jnp.sum(values, axis=0, keepdims=True)


def attend_body(
    step, steps, length, x, vectors, layer, wq, wk, wv, wo, q_out, k_out, v_out, log_out,
    context_out, unit_out, scale_out, total,
):
    slots = x.shape[0]
    rows = x[...]
    lanes_of = pl.ds(pl.multiple_of(step * WIDE, WIDE), WIDE)
    q = (mm(rows, wq[...]) + vectors[layer, 0:1, lanes_of]).astype(BF)
    k = mm(rows, wk[...]).astype(BF)
    v = (mm(rows, wv[...]) + vectors[layer, 1:2, lanes_of]).astype(BF)
    q_out[...] = q
    k_out[...] = k
    v_out[...] = v
    live = lax.broadcasted_iota(jnp.int32, (1, slots), 1) < length[0]
    scaled = (q.astype(F32) * 0.125).astype(BF)
    zero = jnp.zeros_like(scaled)
    context = jnp.zeros((slots, WIDE), F32)
    logs = jnp.zeros((slots, 128), F32)
    column = lax.broadcasted_iota(jnp.int32, (1, 128), 1)
    for head in range(WIDE // HEAD_DIM):
        lanes = head_lanes(head)
        scores = mm_right(jnp.where(lanes, scaled, zero), k)
        scores = jnp.where(live, scores, MASKED)
        highest = jnp.max(scores, axis=-1, keepdims=True)
        exponent = jnp.exp(scores - highest)
        totals = jnp.sum(exponent, axis=-1, keepdims=True)
        probs = (exponent * (1.0 / totals)).astype(BF)
        context = jnp.where(lanes, mm(probs, v), context)
        logs = jnp.where(column == head, highest + jnp.log(totals), logs)
    log_out[...] = jnp.transpose(logs)[:8]
    low = context.astype(BF)
    context_out[...] = low

    @pl.when(step == 0)
    def _():
        total[...] = rows.astype(F32) + vectors[layer, 2:3]

    total[...] += mm(low, wo[...])

    @pl.when(step == steps - 1)
    def _():
        unit, scale = normalized(total[...])
        unit_out[...] = unit
        scale_out[...] = jnp.broadcast_to(scale, scale_out.shape)


def feed_body(
    step, steps, length, vectors, halves, layer, unit1, w1, w2, act_out, slope_out, unit_out,
    scale_out, result_out, low, total,
):
    @pl.when(step == 0)
    def _():
        middle = unit1[...] * vectors[layer, 3:4] + vectors[layer, 4:5]
        low[...] = middle.astype(BF)
        total[...] = middle + vectors[layer, 9:10]

    per = steps // 2
    bias = halves[layer, step // per, pl.ds(5 + lax.rem(step, per), 1)]
    inner = mm(low[...], w1[...]) + bias
    cdf = 0.5 * (1.0 + lax.erf(inner * 0.7071067811865476))
    act = (inner * cdf).astype(BF)
    act_out[...] = act
    slope_out[...] = (cdf + inner * (jnp.exp(-0.5 * inner * inner) * 0.3989422804014327)).astype(BF)
    total[...] += mm(act, w2[...])

    @pl.when(step == steps - 1)
    def _():
        unit, scale = normalized(total[...])
        unit_out[...] = unit
        scale_out[...] = jnp.broadcast_to(scale, scale_out.shape)
        live = lax.broadcasted_iota(jnp.int32, (unit.shape[0], 1), 0) < length[0]
        result = unit * vectors[layer, 10:11] + vectors[layer, 11:12]
        result_out[...] = jnp.where(live, result, 0.0).astype(BF)


def feed_back_body(
    step, steps, length, grad, unit2, scale2, g2, unit1, scale1, g1, b1, act, slope, w1, w2,
    d1_out, d2_out, first_out, vectors_out, inner_rows, second, outer, low, total,
):
    @pl.when(step == 0)
    def _():
        live = lax.broadcasted_iota(jnp.int32, (grad.shape[0], 1), 0) < length[0]
        g = jnp.where(live, grad[...].astype(F32), 0.0)
        unit = unit2[...]
        d_second = normalize_back(g, unit, scale2[:, :1], g2[...])
        second[...] = d_second
        d_outer = d_second.astype(BF)
        outer[...] = d_outer
        vectors_out[0:1] = row_sum(d_outer.astype(F32))
        vectors_out[1:2] = row_sum(g * unit)
        vectors_out[2:3] = row_sum(g)
        low[...] = (unit1[...] * g1[...] + b1[...]).astype(BF)
        total[...] = jnp.zeros_like(total)

    d_outer = outer[...]
    d_inner = (mm_right(d_outer, w2[...]) * slope[...].astype(F32)).astype(BF)
    inner_rows[step, 0:1] = row_sum(d_inner.astype(F32))
    total[...] += mm_right(d_inner, w1[...])
    d2_out[...] = mm_left(act[...], d_outer).astype(BF).reshape(d2_out.shape)
    d1 = mm_left(low[...], d_inner).astype(BF)
    half = d1.shape[0] // 2
    d1_out[0, 0] = d1[:half]
    d1_out[1, 0] = d1[half:]

    @pl.when(step == steps - 1)
    def _():
        d_middle = second[...] + total[...]
        unit = unit1[...]
        d_first = normalize_back(d_middle, unit, scale1[:, :1], g1[...])
        first_out[...] = d_first
        vectors_out[3:4] = row_sum(d_middle * unit)
        vectors_out[4:5] = row_sum(d_middle)
        vectors_out[5:6] = row_sum(d_first.astype(BF).astype(F32))


def attend_back_body(
    step, steps, length, first, x, q, k, v, log, context, wq, wk, wv, wo, dqkv_out, do_out, x_out,
    sums_out, attended, total,
):
    slots = x.shape[0]

    @pl.when(step == 0)
    def _():
        attended[...] = first[...].astype(BF)
        total[...] = first[...]

    d_att = attended[...]
    d_context = mm_right(d_att, wo[...]).astype(BF)
    queries = q[...]
    keys = k[...]
    values = v[...]
    scaled = (queries.astype(F32) * 0.125).astype(BF)
    zero = jnp.zeros_like(scaled)
    live = lax.broadcasted_iota(jnp.int32, (slots, 1), 0) < length[0]
    d_q = jnp.zeros((slots, WIDE), F32)
    d_k = jnp.zeros((slots, WIDE), F32)
    d_v = jnp.zeros((slots, WIDE), F32)
    for head in range(WIDE // HEAD_DIM):
        lanes = head_lanes(head)
        scores = mm_right(keys, jnp.where(lanes, scaled, zero))
        scores = jnp.where(live, scores, MASKED)
        probs = jnp.exp(scores - log[head : head + 1])
        d_v = jnp.where(lanes, mm(probs.astype(BF), d_context), d_v)
        d_probs = mm_right(values, jnp.where(lanes, d_context, zero))
        dots = row_sum(probs * d_probs)
        d_scores = (probs * (d_probs - dots)).astype(BF)
        d_k = jnp.where(lanes, mm(d_scores, queries), d_k)
        d_q = jnp.where(lanes, mm_left(d_scores, keys), d_q)
    d_q = (d_q * 0.125).astype(BF)
    d_k = (d_k * 0.125).astype(BF)
    d_v = d_v.astype(BF)
    sums_out[step, 0:1] = row_sum(d_q.astype(F32))
    sums_out[step, 1:2] = row_sum(d_v.astype(F32))
    total[...] += mm_right(d_q, wq[...]) + mm_right(d_k, wk[...]) + mm_right(d_v, wv[...])
    rows = x[...]
    for at, value in enumerate((d_q, d_k, d_v)):
        weight = mm_left(rows, value).astype(BF)
        half = weight.shape[0] // 2
        dqkv_out[0, at] = weight[:half]
        dqkv_out[1, at] = weight[half:]
    do_out[...] = mm_left(context[...], d_att).astype(BF).reshape(do_out.shape)

    @pl.when(step == steps - 1)
    def _():
        x_out[...] = total[...].astype(BF)


def struct(shape, dtype):
    return jax.ShapeDtypeStruct(shape, dtype)


UNIT_ORDER = (0, 1, 2, 3, 4, 8, 9, 5, 10, 11, 6, 7)
DIRECT_SETS = ((0, 1, 6, 7), (0, 1, 6, 7))
HOPS = (0.0, 4.0, 8.0, 15.0, 18.0, 21.0, 24.0)
PACE = 5.6
CROSS = 11.3


class Plan:
    def __init__(self):
        self.entries = []
        self.done = set()

    def add(self, when, key, action):
        self.entries.append((when, len(self.entries), key, action))

    def sort(self):
        self.entries.sort(key=lambda entry: entry[:2])

    def run_first(self):
        _, _, key, action = self.entries.pop(0)
        action()
        self.done.add(key)

    def until(self, when):
        while self.entries and self.entries[0][0] <= when:
            self.run_first()

    def pending(self, when):
        return bool(self.entries) and self.entries[0][0] <= when

    def missing(self, keys):
        return any(key not in self.done for key in keys)

    def require(self, keys):
        while self.missing(keys):
            self.run_first()


def front_kernel(count, length, permutation, small, shards, inputs, outs, scratch):
    full, (rows_out, dealt), stored = outs[:6], outs[6:8], (outs[8:20], outs[20:32])
    (stage, spread, ordered, halves, rows, xs, unit1, scale1, unit2, scale2, low, total,
     send_sem, recv_sem, load_sem, store_sem, deal_send, deal_recv, home_send, home_recv,
     small_send, small_recv, keep_sem) = scratch
    core = lax.axis_index("section")
    side = lax.axis_index("shard")
    bits = my_bits(count)
    sibling = {"section": 1 - core}
    facing = {"shard": 1 - side}
    corner = {"section": 1 - core, "shard": 1 - side}
    replicas = 1 << count
    groups = 2 * replicas
    devices = 2 * groups
    group = side * replicas + lax.axis_index("replica")
    me = core * groups + group
    chunk, columns = spread.shape[1:]
    strip = HALF // replicas
    position = sum(bits[p] * (1 << p) for p in range(count))
    greet_all(me, devices, replicas)

    def chip(index):
        return {"shard": index // replicas, "replica": lax.rem(index, replicas)}

    def piece(index):
        where = pl.ds(pl.multiple_of(index * chunk, chunk), chunk)
        return inputs.at[:, where, pl.ds(pl.multiple_of(core * columns, columns), columns)]

    def spread_copy(target):
        return remote(
            piece(target), spread.at[pl.ds(2 * group, 2)], deal_send.at[target],
            deal_recv.at[group], chip(target),
        )

    spread_own = pltpu.make_async_copy(
        piece(group), spread.at[pl.ds(2 * group, 2)], deal_recv.at[group]
    )

    def spread_start(step, carry):
        spread_copy(lax.rem(group + step, groups)).start()
        return carry

    def spread_wait(step, carry):
        source = lax.rem(group + step, groups)
        landed = spread.at[pl.ds(2 * source, 2)]
        remote(
            landed, landed, deal_send.at[source], deal_recv.at[source], chip(source)
        ).wait_recv()
        return carry

    def spot(device):
        where = pl.ds(pl.multiple_of(lax.rem(device, groups) * chunk, chunk), chunk)
        start = pl.multiple_of((device // groups) * columns, columns)
        return xs.at[where, pl.ds(start, columns)]

    def slot_of(device):
        return 2 * lax.rem(device, groups) + device // groups

    def home_copy(target):
        return remote(
            ordered.at[slot_of(target)], spot(me), home_send.at[target], home_recv.at[me],
            place(target, replicas),
        )

    home_own = pltpu.make_async_copy(ordered.at[slot_of(me)], spot(me), home_recv.at[me])

    def home_start(step, carry):
        home_copy(lax.rem(me + step, devices)).start()
        return carry

    def home_wait(step, carry):
        source = lax.rem(me + step, devices)
        remote(
            spot(source), spot(source), home_send.at[source], home_recv.at[source],
            place(source, replicas),
        ).wait_recv()
        return carry

    def spread_done(step, carry):
        spread_copy(lax.rem(group + step, groups)).wait_send()
        return carry

    def home_done(step, carry):
        home_copy(lax.rem(me + step, devices)).wait_send()
        return carry

    def reorder(slot, carry):
        ordered[slot] = spread[permutation[slot]]
        return carry

    def deal_second():
        spread_own.wait()
        lax.fori_loop(1, groups, spread_wait, 0)
        lax.fori_loop(0, devices, reorder, 0)
        home_own.start()
        lax.fori_loop(1, devices, home_start, 0)

    def deal_last():
        home_own.wait()
        lax.fori_loop(1, devices, home_wait, 0)

    def small_copy(index, partner):
        return remote(
            small, halves.at[core, side], small_send.at[index], small_recv.at[index], partner
        )

    small_own = pltpu.make_async_copy(small, halves.at[core, side], small_send.at[3])

    def vectors_here():
        small_own.wait()
        for index, layer, half, partner in (
            (0, 1 - core, side, sibling), (1, core, 1 - side, facing),
            (2, 1 - core, 1 - side, corner),
        ):
            landed = halves.at[layer, half]
            remote(
                landed, landed, small_send.at[index], small_recv.at[index], partner
            ).wait_recv()
        for layer in range(2):
            for half in range(2):
                rows[layer, :, pl.ds(512 * half, 512)] = halves[layer, half]

    def shard_at(unit, start, size):
        where = pl.ds(start, size)
        if unit < 4:
            return shards[unit].at[where]
        if unit < 8:
            return shards[4].at[where, pl.ds(1024 * (unit - 4), 1024)]
        return shards[5].at[pl.ds(512 * (unit - 8) + start, size)]

    def out_at(layer, unit, half, start, size):
        base = 512 * half + start if unit < 8 else 2048 * half + 512 * (unit - 8) + start
        where = pl.ds(pl.multiple_of(base, strip), size)
        if unit < 4:
            return full[unit].at[layer, where]
        if unit < 8:
            return full[4].at[layer, where, pl.ds(1024 * (unit - 4), 1024)]
        return full[5].at[layer, where]

    mine = HALF * core

    def wire(layer, unit, hop, src, dst, partner):
        index = UNITS * layer + unit
        return remote(src, dst, send_sem.at[index, hop], recv_sem.at[index, hop], partner)

    def arrive(layer, unit, hop, landed, partner):
        wire(layer, unit, hop, landed, landed, partner).wait_recv()

    def cross_rows(layer, unit):
        if unit in DIRECT_SETS[layer]:
            return mine, HALF
        return pl.multiple_of(mine + position * strip, strip), strip

    def cross(layer, unit):
        start, size = cross_rows(layer, unit)
        target = out_at(layer, unit, side, start, size)

        @pl.when(core == layer)
        def _():
            wire(layer, unit, 0, shard_at(unit, start, size), target, facing).start()

        @pl.when(core != layer)
        def _():
            arrive(layer, unit, count + 2, out_at(layer, unit, side, 0, 512), sibling)
            wire(layer, unit, 0, target, target, facing).start()

    def block(k):
        return pl.multiple_of(mine + ((position >> k) << k) * strip, strip), strip << k

    def other_block(k):
        start = ((position >> k) ^ 1) << k
        return pl.multiple_of(mine + start * strip, strip), strip << k

    def hop(layer, unit, k):
        there = 1 - side
        if k == 0:
            arrive(layer, unit, 0, out_at(layer, unit, there, *cross_rows(layer, unit)), facing)
        else:
            arrive(
                layer, unit, k, out_at(layer, unit, there, *other_block(k - 1)),
                across(k - 1, count, bits),
            )
        if k < count and unit not in DIRECT_SETS[layer]:
            held = out_at(layer, unit, there, *block(k))
            wire(layer, unit, k + 1, held, held, across(k, count, bits)).start()
        else:
            held = out_at(layer, unit, there, mine, HALF)
            wire(layer, unit, count + 1, held, held, sibling).start()

    def passed(layer, unit):
        landed = out_at(layer, unit, 1 - side, HALF * (1 - core), HALF)
        arrive(layer, unit, count + 1, landed, sibling)

        @pl.when(core == layer)
        def _():
            store(layer, unit).wait()

    def store(layer, unit):
        return pltpu.make_async_copy(
            stage.at[unit], out_at(layer, unit, side, 0, 512), store_sem.at[unit]
        )

    def load(unit):
        return pltpu.make_async_copy(shard_at(unit, 0, 512), stage.at[unit], load_sem.at[unit])

    def own_start(layer):
        for unit in UNIT_ORDER:
            source = shard_at(unit, 0, 512)
            wire(
                layer, unit, count + 2, source, out_at(layer, unit, side, 0, 512), sibling
            ).start()
            load(unit).start()

    def own_store(layer):
        for unit in UNIT_ORDER:
            load(unit).wait()
            store(layer, unit).start()

    plan = Plan()
    number = [0, 0]
    for layer in range(2):
        for unit in UNIT_ORDER:
            key = (layer, unit)
            if unit in DIRECT_SETS[layer]:
                landing = 14.0 + CROSS * (number[0] + 1)
                number[0] += 1
                plan.add(landing - 2.5 * CROSS, ("cross",) + key, lambda l=layer, u=unit: cross(l, u))
                plan.add(landing, ("hop",) + key, lambda l=layer, u=unit: hop(l, u, 0))
                plan.add(landing + 3.0, ("unit",) + key, lambda l=layer, u=unit: passed(l, u))
            else:
                begin = 6.0 + PACE * number[1]
                number[1] += 1
                plan.add(begin - 16.0, ("cross",) + key, lambda l=layer, u=unit: cross(l, u))
                for k in range(count + 1):
                    plan.add(
                        begin + HOPS[k], ("hop", k) + key, lambda l=layer, u=unit, k=k: hop(l, u, k)
                    )
                plan.add(
                    begin + HOPS[count] + 3.0, ("unit",) + key,
                    lambda l=layer, u=unit: passed(l, u),
                )
    plan.add(20.0, "deal", deal_second)
    plan.add(40.0, "inputs", deal_last)
    plan.add(10.0, "vectors", vectors_here)
    plan.sort()

    spread_own.start()
    lax.fori_loop(1, groups, spread_start, 0)
    for index, partner in enumerate((sibling, facing, corner)):
        small_copy(index, partner).start()
    small_own.start()
    for layer in range(2):
        @pl.when(core == layer)
        def _():
            own_start(layer)
    plan.until(1.0)
    for layer in range(2):
        @pl.when(core == layer)
        def _():
            own_store(layer)

    slots, width = xs.shape
    attention_steps = width // WIDE
    hidden = full[4].shape[-1]
    hidden_steps = hidden // HIDDEN_BLOCK
    band = pl.BlockSpec((slots, WIDE), lambda j: (0, j))
    wide = pl.BlockSpec((width, WIDE), lambda j: (0, j))
    hidden_band = pl.BlockSpec((slots, HIDDEN_BLOCK), lambda j: (0, j))

    def during(step, steps, begin, each, needs):
        for at in range(steps):
            when = begin + each * at
            wanted = needs(at)
            if plan.pending(when) or plan.missing(wanted):
                @pl.when(step == at)
                def _():
                    plan.require(wanted)
                    plan.until(when)

    def attend_stage(layer, begin):
        (q, k, v, log, context) = stored[layer][:5]

        def body(*refs):
            step = pl.program_id(0)
            attend_body(step, attention_steps, length, xs, rows, layer, *refs, unit1, scale1, total)
            during(step, attention_steps, begin, 5.0, lambda at: [])

        pltpu.emit_pipeline(
            body,
            grid=(attention_steps,),
            in_specs=[wide, wide, wide, pl.BlockSpec((WIDE, width), lambda j: (j, 0))],
            out_specs=[
                band, band, band, pl.BlockSpec((None, 8, slots), lambda j: (j, 0, 0)), band
            ],
        )(*(full[i].at[layer] for i in range(4)), q, k, v, log, context)

    def feed_needs(layer, step):
        return [
            ("unit", layer, unit)
            for at in range(min(step + 1, hidden_steps))
            for unit in (4 + at * HIDDEN_BLOCK // 1024, 8 + at % 4)
        ]

    def feed_stage(layer, begin):
        act, slope = stored[layer][7:9]

        def body(*refs):
            step = pl.program_id(0)
            feed_body(
                step, hidden_steps, length, rows, halves, layer, unit1, *refs, unit2, scale2, xs,
                low, total,
            )
            during(step, hidden_steps, begin, 2.5, lambda at: feed_needs(layer, at + 2))

        pltpu.emit_pipeline(
            body,
            grid=(hidden_steps,),
            in_specs=[
                pl.BlockSpec((width, HIDDEN_BLOCK), lambda j: (0, j)),
                pl.BlockSpec((HIDDEN_BLOCK, width), lambda j: (j, 0)),
            ],
            out_specs=[hidden_band, hidden_band],
        )(full[4].at[layer], full[5].at[layer], act, slope)

    def keep(source, target, at):
        copy = pltpu.make_async_copy(source, target, keep_sem.at[at])
        copy.start()
        return copy

    begin = (45.0, 95.0)
    keeping = []
    for layer in range(2):
        plan.require(["vectors", "inputs"] + [("unit", layer, unit) for unit in range(4)])
        if layer == 0:
            keeping += [keep(xs, dealt, 0), keep(rows, rows_out, 1)]
        attend_stage(layer, begin[layer])
        for copy in keeping:
            copy.wait()
        keeping = [keep(unit1, stored[layer][5], 2), keep(scale1, stored[layer][6], 3)]
        plan.require(feed_needs(layer, 1))
        feed_stage(layer, begin[layer] + 22.0)
        for copy in keeping:
            copy.wait()
        keeping = [
            keep(unit2, stored[layer][9], 4), keep(scale2, stored[layer][10], 5),
            keep(xs, stored[layer][11], 6),
        ]
    plan.until(1000000.0)
    for copy in keeping:
        copy.wait()
    lax.fori_loop(1, groups, spread_done, 0)
    lax.fori_loop(1, devices, home_done, 0)
    for index, partner in enumerate((sibling, facing, corner)):
        small_copy(index, partner).wait_send()
    for layer in range(2):
        for unit in range(UNITS):
            start, size = cross_rows(layer, unit)
            crossed = out_at(layer, unit, side, start, size)
            wire(layer, unit, 0, crossed, crossed, facing).wait_send()
            if unit not in DIRECT_SETS[layer]:
                for k in range(count):
                    held = out_at(layer, unit, 1 - side, *block(k))
                    wire(layer, unit, k + 1, held, held, across(k, count, bits)).wait_send()
            held = out_at(layer, unit, 1 - side, mine, HALF)
            wire(layer, unit, count + 1, held, held, sibling).wait_send()

        @pl.when(core == layer)
        def _():
            for unit in range(UNITS):
                own = out_at(layer, unit, side, 0, 512)
                wire(layer, unit, count + 2, own, own, sibling).wait_send()


def forward(length, permutation, small, shards, inputs, count):
    groups = 2 << count
    slots, width = inputs.shape[1:]
    hidden = shards[4].shape[-1]
    part = (2 * groups, slots // groups, width // 2)
    dma = pltpu.SemaphoreType.DMA
    square = (slots, width)
    steps = width // WIDE
    layer = [
        struct(square, BF), struct(square, BF), struct(square, BF), struct((steps, 8, slots), F32),
        struct(square, BF), struct(square, F32), struct((slots, 128), F32),
        struct((slots, hidden), BF), struct((slots, hidden), BF), struct(square, F32),
        struct((slots, 128), F32), struct(square, BF),
    ]
    out_shape = (
        [struct((2, width, width), BF)] * 4
        + [struct((2, width, hidden), BF), struct((2, hidden, width), BF)]
        + [struct((2,) + small.shape[:1] + (width,), F32), struct(square, BF)]
        + layer + layer
    )
    smem = pl.BlockSpec(memory_space=pltpu.SMEM)
    anywhere = pl.BlockSpec(memory_space=pl.ANY)

    def kernel(*refs):
        front_kernel(
            count, *refs[:3], refs[3:9], refs[9], refs[10 : 10 + len(out_shape)],
            refs[10 + len(out_shape) :],
        )

    return pl.pallas_call(
        kernel,
        out_shape=out_shape,
        in_specs=[smem, smem] + [anywhere] * 8,
        out_specs=[anywhere] * len(out_shape),
        scratch_shapes=[
            pltpu.VMEM((UNITS, 512, 1024), BF), pltpu.VMEM(part, BF), pltpu.VMEM(part, BF),
            pltpu.VMEM((2, 2) + small.shape, F32),
            pltpu.VMEM((2,) + small.shape[:1] + (width,), F32),
            pltpu.VMEM(square, BF), pltpu.VMEM(square, F32), pltpu.VMEM((slots, 128), F32),
            pltpu.VMEM(square, F32), pltpu.VMEM((slots, 128), F32),
            pltpu.VMEM(square, BF), pltpu.VMEM(square, F32),
            dma((2 * UNITS, count + 3)), dma((2 * UNITS, count + 3)), dma((UNITS,)), dma((UNITS,)),
            dma((groups,)), dma((groups,)), dma((2 * groups,)), dma((2 * groups,)),
            dma((4,)), dma((3,)), dma((7,)),
        ],
        compiler_params=pltpu.CompilerParams(
            collective_id=0, has_side_effects=True, vmem_limit_bytes=VMEM_LIMIT
        ),
        name="forward",
    )(length, permutation, small, *shards, inputs)


SENT_RING = 4
LAND_RING = 5
PIECES = 2 * UNITS
DEAL_STEP = 5
EARLY = ((0, 1, 2, 3), (1, 3, 5, 7), (0, 1, 2, 3))
AHEAD = sum(len(steps) for steps in EARLY)


def device_of(number, groups):
    return lax.rem(number, 2) * groups + number // 2


def back_kernel(count, length, inverse, gains, lower, upper, weights, results, outs, scratch):
    (total, small_total, landing, dealt, acts, d1_low, d2_low, dqkv_low, do_low, up_d1, up_d2,
     dqkv_up, do_up, grad_low, grad_up) = outs
    (xs, first, gradient, unit1, unit2, scale1, scale2, second, outer, middle, running, attended,
     vectors, inner_rows, sums) = scratch[:15]
    (own, came, across_half, kept, from_x), rest = scratch[15:20], scratch[20:]
    halves, rest = rest[:count], rest[count:]
    (spread, ordered, smalls, small_own, small_recv, send0, recv0, send_x, recv_x, send_rs, recv_rs,
     send_ag, recv_ag, load_sem, came_sem, piece_sem, small_send, small_arrive, deal_send,
     deal_recv, home_send, home_recv, act_sem, total_sem, fetch_sem, done_send, done_recv) = rest
    wq, wk, wv, wo, w1, w2 = weights
    (up_unit2, up_scale2, up_unit1, up_scale1, up_act, up_slope, up_x, up_q, up_k, up_v, up_log,
     up_context, cotangent) = upper
    (low_unit2, low_scale2, low_unit1, low_scale1, low_act, low_slope, low_x, low_q, low_k, low_v,
     low_log, low_context) = lower
    core = lax.axis_index("section")
    side = lax.axis_index("shard")
    replica = lax.axis_index("replica")
    bits = my_bits(count)
    sibling = {"section": 1 - core}
    facing = {"shard": 1 - side}
    everything = (slice(None),) * count
    rows = kept.shape[-2]
    keep_ring = kept.shape[0]
    replicas = 1 << count
    groups = 2 * replicas
    group = side * replicas + replica
    me = core * groups + group
    chunk = spread.shape[1]
    greet_all(me, 2 * groups, replicas)

    layers = ((up_d1, up_d2, dqkv_up, do_up), (d1_low, d2_low, dqkv_low, do_low))
    ranges, at = [], 0
    for order in range(2):
        for index in range(4):
            depth = layers[order][index].shape[1]
            ranges.append((order, index, at, at + depth))
            at += depth

    def part_of(order, index, unit, half):
        where = pl.ds(pl.multiple_of(HALF * half, HALF), HALF)
        return layers[order][index].at[:, unit, where]

    def core_copy(unit, source=None):
        source = landing.at[unit] if source is None else source
        return remote(source, landing.at[unit], send0.at[unit], recv0.at[unit], sibling)

    def send_core(order, which):
        for at_order, index, low, high in ranges:
            if at_order == order and index in which:
                for unit in range(low, high):
                    core_copy(unit, part_of(order, index, unit - low, 1 - core)).start()

    def own_load(source, slot):
        return pltpu.make_async_copy(source, own.at[slot], load_sem.at[slot])

    def came_load(unit):
        slot = lax.rem(unit, 2)
        return pltpu.make_async_copy(landing.at[unit], came.at[slot], came_sem.at[slot])

    def start_load(unit):
        for order, index, low, high in ranges:
            @pl.when(jnp.logical_and(unit >= low, unit < high))
            def _():
                own_load(part_of(order, index, unit - low, core), lax.rem(unit, 2)).start()

    def x_copy(unit):
        return remote(
            across_half.at[lax.rem(unit, SENT_RING)], from_x.at[lax.rem(unit, LAND_RING)],
            send_x.at[unit], recv_x.at[unit], facing,
        )

    def rs_copy(unit, p):
        slot = lax.rem(unit, keep_ring)
        return remote(
            kept.at[(slot,) + everything[:p] + (1 - bits[p],) + bits[p + 1 :]],
            halves[p].at[lax.rem(unit, LAND_RING)],
            send_rs.at[p, unit],
            recv_rs.at[p, unit],
            across(p, count, bits),
        )

    def ag_copy(unit, p):
        where = (unit,) + everything[:p] + bits[p:]
        source = kept.at[(lax.rem(unit, keep_ring),) + bits] if p == 0 else total.at[where]
        return remote(
            source, total.at[where], send_ag.at[p, unit], recv_ag.at[p, unit],
            across(p, count, bits),
        )

    def ag_arrive(unit, p):
        where = total.at[(unit,) + everything[:p] + (1 - bits[p],) + bits[p + 1 :]]
        remote(
            where, where, send_ag.at[p, unit], recv_ag.at[p, unit], across(p, count, bits)
        ).wait_recv()

    def piece_copy(unit):
        return pltpu.make_async_copy(
            kept.at[(lax.rem(unit, keep_ring),) + bits], total.at[(unit,) + bits],
            piece_sem.at[unit],
        )

    def done_copy(unit):
        index = lax.rem(unit, UNITS)
        return remote(
            total.at[unit], total.at[PIECES + index], done_send.at[index], done_recv.at[index],
            sibling,
        )

    def small_copy(step):
        partner = [sibling, facing] + [across(p, count, bits) for p in range(count)]
        source = smalls.at[1 - core] if step == 0 else small_own.at[step - 1]
        return remote(
            source, small_recv.at[step], small_send.at[step], small_arrive.at[step], partner[step]
        )

    def chunk_of(layer, target):
        return results[layer].at[pl.ds(pl.multiple_of(target * chunk, chunk), chunk)]

    def spread_copy(layer, target):
        return remote(
            chunk_of(layer, lax.rem(target, groups)), spread.at[me], deal_send.at[target],
            deal_recv.at[me], place(target, replicas),
        )

    def spread_own(layer):
        return pltpu.make_async_copy(chunk_of(layer, group), spread.at[me], deal_recv.at[me])

    def spread_start(step, carry):
        target = lax.rem(me + step, 2 * groups)
        for layer in range(2):
            @pl.when(target // groups == layer)
            def _():
                spread_copy(layer, target).start()
        return carry

    def spread_wait(step, carry):
        source = lax.rem(me + step, 2 * groups)
        remote(
            spread.at[source], spread.at[source], deal_send.at[source], deal_recv.at[source],
            place(source, replicas),
        ).wait_recv()
        return carry

    def chip(index):
        return {"shard": index // replicas, "replica": lax.rem(index, replicas)}

    def home_copy(target):
        return remote(
            ordered.at[pl.ds(2 * target, 2)], dealt.at[:, group], home_send.at[target],
            home_recv.at[group], chip(target),
        )

    def home_own():
        return pltpu.make_async_copy(
            ordered.at[pl.ds(2 * group, 2)], dealt.at[:, group], home_recv.at[group]
        )

    def home_start(step, carry):
        home_copy(lax.rem(group + step, groups)).start()
        return carry

    def home_wait(step, carry):
        source = lax.rem(group + step, groups)
        remote(
            dealt.at[:, source], dealt.at[:, source], home_send.at[source], home_recv.at[source],
            chip(source),
        ).wait_recv()
        return carry

    def reorder(slot, carry):
        ordered[slot] = spread[device_of(inverse[slot], groups)]
        return carry

    def places_of(index, dims):
        return tuple((lax.rem(index // (1 << (dims - 1 - q)), 2) for q in range(dims)))

    def tick(now):
        @pl.when(jnp.logical_and(now >= SENT_RING, now < PIECES + SENT_RING))
        def _():
            x_copy(now - SENT_RING).wait_send()

        @pl.when(jnp.logical_and(now >= keep_ring, now < PIECES + keep_ring))
        def _():
            for p in range(count):
                rs_copy(now - keep_ring, p).wait_send()
            ag_copy(now - keep_ring, 0).wait_send()

        @pl.when(now < PIECES)
        def _():
            unit = now
            slot = lax.rem(unit, 2)

            @pl.when(unit == 0)
            def _():
                start_load(0)
                core_copy(0).wait_recv()
                came_load(0).start()

            own_load(landing.at[unit], slot).wait()
            came_load(unit).wait()

            @pl.when(unit + 1 < PIECES)
            def _():
                start_load(unit + 1)
                core_copy(unit + 1).wait_recv()
                came_load(unit + 1).start()

            out_slot = lax.rem(unit, SENT_RING)
            kept_slot = lax.rem(unit, keep_ring)

            def add(block, c):
                where = pl.ds(pl.multiple_of(block * 32, 32), 32)
                across_half[out_slot, where] = (
                    own[slot, 1 - side, where] + came[slot, 1 - side, where]
                )
                return c

            lax.fori_loop(0, HALF // 32, add, 0)
            x_copy(unit).start()

            def add_kept(index, c):
                where = pl.ds(pl.multiple_of(index * rows, rows), rows)
                mine = (kept_slot,) + places_of(index, count)
                kept[mine] = own[slot, side, where] + came[slot, side, where]
                return c

            lax.fori_loop(0, 1 << count, add_kept, 0)

        @pl.when(jnp.logical_and(now >= 1, now < PIECES + 1))
        def _():
            unit = now - 1
            slot = lax.rem(unit, keep_ring)
            land = lax.rem(unit, LAND_RING)
            x_copy(unit).wait_recv()

            def add(index, c):
                where = pl.ds(pl.multiple_of(index * rows, rows), rows)
                mine = (slot,) + places_of(index, count)
                kept[mine] = kept[mine] + from_x[land, where]
                return c

            lax.fori_loop(0, 1 << count, add, 0)
            rs_copy(unit, count - 1).start()

        for step in range(count):
            p = count - 1 - step

            @pl.when(jnp.logical_and(now >= 2 + step, now < PIECES + 2 + step))
            def _():
                unit = now - (2 + step)
                slot = lax.rem(unit, keep_ring)
                land = lax.rem(unit, LAND_RING)
                rs_copy(unit, p).wait_recv()

                def add(index, c):
                    mine = (slot,) + places_of(index, p) + bits[p:]
                    kept[mine] = kept[mine] + halves[p][(land,) + places_of(index, p)]
                    return c

                if p == 0:
                    add(0, 0)
                    piece_copy(unit).start()
                    ag_copy(unit, 0).start()
                else:
                    lax.fori_loop(0, 1 << p, add, 0)
                    rs_copy(unit, p - 1).start()

        for p in range(count):
            lag = 2 + count + p

            @pl.when(jnp.logical_and(now >= lag, now < PIECES + lag))
            def _():
                unit = now - lag
                ag_arrive(unit, p)
                if p == 0:
                    piece_copy(unit).wait()
                if p + 1 < count:
                    ag_copy(unit, p + 1).start()
                else:
                    @pl.when((unit < UNITS) == (core == 0))
                    def _():
                        done_copy(unit).start()

    def early(step, phase):
        before = sum(len(steps) for steps in EARLY[:phase])
        now = -1
        for at, when in enumerate(EARLY[phase]):
            now = jnp.where(step == when, before + at, now)

        @pl.when(now >= 0)
        def _():
            tick(now)

    def fetch(source, target, at):
        copy = pltpu.make_async_copy(source, target, fetch_sem.at[at])
        copy.start()
        return copy

    waits = [
        fetch(cotangent, gradient, 0), fetch(up_unit1, unit1, 2), fetch(up_unit2, unit2, 3),
        fetch(up_scale1, scale1, 4), fetch(up_scale2, scale2, 5),
    ]
    up_rows = fetch(up_x, xs, 1)
    for layer in range(2):
        @pl.when(core == layer)
        def _():
            spread_own(layer).start()
    lax.fori_loop(1, 2 * groups, spread_start, 0)
    for copy in waits:
        copy.wait()

    slots, width = xs.shape
    attention_steps = width // WIDE
    hidden_steps = w1.shape[-1] // HIDDEN_BLOCK
    per = 512 // WIDE
    wide_per = 1024 // HIDDEN_BLOCK
    pairs = HIDDEN_BLOCK // 512
    band = pl.BlockSpec((slots, WIDE), lambda j: (0, j))
    columns = pl.BlockSpec((width, WIDE), lambda j: (0, j))

    def attention(layer, phase, q, k, v, log, context, dqkv, do):
        def body(*refs):
            step = pl.program_id(0)
            attend_back_body(
                step, attention_steps, length, first, xs, *refs, gradient, sums, attended, running
            )
            early(step, phase)

        pltpu.emit_pipeline(
            body,
            grid=(attention_steps,),
            in_specs=[
                band, band, band, pl.BlockSpec((None, 8, slots), lambda j: (j, 0, 0)), band,
                columns, columns, columns, pl.BlockSpec((WIDE, width), lambda j: (j, 0)),
            ],
            out_specs=[
                pl.BlockSpec((2, 3, 512, WIDE), lambda j: (0, 0, 0, j)),
                pl.BlockSpec((1, 1, WIDE, width), lambda j: (j // per, 0, j % per, 0)),
            ],
        )(q, k, v, log, context, wq.at[layer], wk.at[layer], wv.at[layer], wo.at[layer], dqkv, do)
        for at in range(attention_steps):
            lanes = pl.ds(WIDE * at, WIDE)
            smalls[layer, 0:1, lanes] = sums[at, 0:1]
            smalls[layer, 1:2, lanes] = sums[at, 1:2]

    hidden_band = pl.BlockSpec((slots, HIDDEN_BLOCK), lambda j: (0, j))

    def deal_second():
        spread_own(0).wait()
        lax.fori_loop(1, 2 * groups, spread_wait, 0)
        lax.fori_loop(0, 2 * groups, reorder, 0)
        home_own().start()
        lax.fori_loop(1, groups, home_start, 0)

    def feed_stage(layer, act, slope, d1, d2):
        def body(*refs):
            step = pl.program_id(0)
            feed_back_body(
                step, hidden_steps, length, gradient, unit2, scale2, gains.at[layer, 10:11],
                unit1, scale1, gains.at[layer, 3:4], gains.at[layer, 4:5], *refs, first,
                vectors, inner_rows, second, outer, middle, running,
            )
            if layer == 0:
                early(step, 1)
            else:
                pl.when(step == DEAL_STEP)(deal_second)

        pltpu.emit_pipeline(
            body,
            grid=(hidden_steps,),
            in_specs=[
                hidden_band, hidden_band,
                pl.BlockSpec((width, HIDDEN_BLOCK), lambda j: (0, j)),
                pl.BlockSpec((HIDDEN_BLOCK, width), lambda j: (j, 0)),
            ],
            out_specs=[
                pl.BlockSpec(
                    (2, 1, 512, HIDDEN_BLOCK), lambda j: (0, j // wide_per, 0, j % wide_per)
                ),
                pl.BlockSpec(
                    (1, pairs, 512, width),
                    lambda j: (j // (hidden_steps // 2), j % (hidden_steps // 2), 0, 0),
                ),
            ],
        )(act, slope, w1.at[layer], w2.at[layer], d1, d2)
        for at, source in ((2, 5), (3, 3), (4, 4), (9, 0), (10, 1), (11, 2)):
            smalls[layer, at : at + 1] = vectors[source : source + 1]
        for at in range(hidden_steps):
            line = 5 + at // wide_per
            lanes = pl.ds(HIDDEN_BLOCK * (at % wide_per), HIDDEN_BLOCK)
            smalls[layer, line : line + 1, lanes] = inner_rows[at, 0:1]

    feed_stage(1, up_act, up_slope, up_d1, up_d2)
    send_core(0, (0, 1))
    later = [
        fetch(low_unit1, unit1, 2), fetch(low_unit2, unit2, 3), fetch(low_scale1, scale1, 4),
        fetch(low_scale2, scale2, 5),
    ]
    up_rows.wait()
    attention(1, 0, up_q, up_k, up_v, up_log, up_context, dqkv_up, do_up)
    send_core(0, (2, 3))
    waits = [fetch(gradient, grad_up, 0), fetch(low_x, xs, 1)]
    for copy in later:
        copy.wait()
    feed_stage(0, low_act, low_slope, d1_low, d2_low)
    send_core(1, (0, 1))
    for copy in waits:
        copy.wait()
    attention(0, 2, low_q, low_k, low_v, low_log, low_context, dqkv_low, do_low)
    send_core(1, (2, 3))
    small_copy(0).start()
    held = fetch(gradient, grad_low, 0)
    held.wait()
    small_steps = count + 2
    both = (grad_low, grad_up)

    def exchange(layer):
        return remote(both[1 - layer], acts.at[layer], act_sem.at[0], act_sem.at[1], sibling)

    for layer in range(2):
        @pl.when(core == layer)
        def _():
            exchange(layer).start()
    grad_back = fetch(grad_up, xs, 1)
    grad_back.wait()

    @pl.when(core == 0)
    def _():
        pltpu.make_async_copy(gradient, acts.at[0], act_sem.at[2]).start()

    @pl.when(core == 1)
    def _():
        pltpu.make_async_copy(xs, acts.at[1], act_sem.at[2]).start()

    def late(now, carry):
        for step in range(small_steps):
            @pl.when(now == step + 1)
            def _():
                small_copy(step).wait_recv()
                before = smalls[core] if step == 0 else small_own[step - 1]
                small_own[step] = before + small_recv[step]
                if step + 1 < small_steps:
                    small_copy(step + 1).start()

        tick(now + AHEAD)
        return carry

    lax.fori_loop(0, PIECES + max(keep_ring, 2 + 2 * count) - AHEAD, late, 0)
    out = pltpu.make_async_copy(small_own.at[small_steps - 1], small_total, total_sem)
    out.start()

    def last(unit, carry):
        core_copy(unit).wait_send()
        for p in range(1, count):
            ag_copy(unit, p).wait_send()
        return carry

    lax.fori_loop(0, PIECES, last, 0)

    def swapped(index, carry):
        done_copy(index).wait_send()
        done_copy(index).wait_recv()
        return carry

    lax.fori_loop(0, UNITS, swapped, 0)
    for step in range(small_steps):
        small_copy(step).wait_send()

    def spread_done(step, carry):
        spread_copy(0, lax.rem(me + step, 2 * groups)).wait_send()
        return carry

    def home_done(step, carry):
        home_copy(lax.rem(group + step, groups)).wait_send()
        return carry

    lax.fori_loop(1, 2 * groups, spread_done, 0)
    home_own().wait()
    lax.fori_loop(1, groups, home_wait, 0)
    lax.fori_loop(1, groups, home_done, 0)
    back = remote(both[0], acts.at[1 - core], act_sem.at[0], act_sem.at[1], sibling)
    back.wait_send()
    back.wait_recv()
    pltpu.make_async_copy(xs, acts.at[core], act_sem.at[2]).wait()
    out.wait()


def backward(length, inverse, gains, lower, upper, weights, results, count):
    cut = (2,) * count
    rows = HALF // (1 << count)
    narrow = cut + (rows, 1024)
    dma = pltpu.SemaphoreType.DMA
    groups = 2 << count
    slots, width = results[0].shape
    chunk = slots // groups
    keep_ring = count + 5
    hidden = weights[4].shape[-1]
    sizes = [len(lower), len(upper), len(weights), len(results)]

    def kernel(*refs):
        start, groups_of = 3, []
        for size in sizes:
            groups_of.append(refs[start : start + size])
            start += size
        back_kernel(count, *refs[:3], *groups_of, refs[start : start + 15], refs[start + 15 :])

    anywhere = pl.BlockSpec(memory_space=pl.ANY)
    vmem = pl.BlockSpec(memory_space=pltpu.VMEM)
    smem = pl.BlockSpec(memory_space=pltpu.SMEM)
    vectors = (UNITS, width)
    square = (slots, width)
    feed_shape, head_shape = (2, 4, 512, 1024), (2, 3, 512, 1024)
    out_shape = [
        struct((PIECES + UNITS,) + narrow, BF),
        struct(vectors, F32),
        struct((PIECES, 2, HALF, 1024), BF),
        struct((2, groups, chunk, width), BF),
        struct((2,) + square, BF),
        struct(feed_shape, BF), struct(feed_shape, BF),
        struct(head_shape, BF), struct((2, 1, 512, 1024), BF),
        struct(feed_shape, BF), struct(feed_shape, BF),
        struct(head_shape, BF), struct((2, 1, 512, 1024), BF),
        struct(square, BF), struct(square, BF),
    ]
    result = pl.pallas_call(
        kernel,
        out_shape=out_shape,
        in_specs=[smem, smem, vmem] + [anywhere] * sum(sizes),
        out_specs=[anywhere] * len(out_shape),
        scratch_shapes=[
            pltpu.VMEM(square, BF), pltpu.VMEM(square, F32), pltpu.VMEM(square, BF),
            pltpu.VMEM(square, F32), pltpu.VMEM(square, F32),
            pltpu.VMEM((slots, 128), F32), pltpu.VMEM((slots, 128), F32),
            pltpu.VMEM(square, F32), pltpu.VMEM(square, BF), pltpu.VMEM(square, BF),
            pltpu.VMEM(square, F32), pltpu.VMEM(square, BF),
            pltpu.VMEM((8, width), F32),
            pltpu.VMEM((hidden // HIDDEN_BLOCK, 8, HIDDEN_BLOCK), F32),
            pltpu.VMEM((width // WIDE, 8, WIDE), F32),
            pltpu.VMEM((2, 2, HALF, 1024), BF),
            pltpu.VMEM((2, 2, HALF, 1024), BF),
            pltpu.VMEM((SENT_RING, HALF, 1024), BF),
            pltpu.VMEM((keep_ring,) + narrow, BF),
            pltpu.VMEM((LAND_RING, HALF, 1024), BF),
        ]
        + [pltpu.VMEM((LAND_RING,) + (2,) * p + (rows, 1024), BF) for p in range(count)]
        + [
            pltpu.VMEM((2 * groups, chunk, width), BF),
            pltpu.VMEM((2 * groups, chunk, width), BF),
            pltpu.VMEM((2,) + vectors, F32),
            pltpu.VMEM((count + 2,) + vectors, F32),
            pltpu.VMEM((count + 2,) + vectors, F32),
            dma((PIECES,)), dma((PIECES,)), dma((PIECES,)), dma((PIECES,)),
            dma((count, PIECES)), dma((count, PIECES)), dma((count, PIECES)), dma((count, PIECES)),
            dma((2,)), dma((2,)), dma((PIECES,)), dma((count + 2,)), dma((count + 2,)),
            dma((2 * groups,)), dma((2 * groups,)), dma((groups,)), dma((groups,)),
            dma((3,)), dma, dma((6,)), dma((UNITS,)), dma((UNITS,)),
        ],
        compiler_params=pltpu.CompilerParams(
            collective_id=1, has_side_effects=True, vmem_limit_bytes=VMEM_LIMIT
        ),
        name="backward",
    )(length, inverse, gains, *lower, *upper, *weights, *results)
    total, small_total, _, dealt, acts = result[:5]
    return total.reshape(3, UNITS, HALF, 1024), small_total, dealt.reshape(2, slots, width), acts


from jax.sharding import PartitionSpec as P

VECTORS = (1, 1, 1, 1, 1, 4, 1, 1, 1)


def unpack_kernel(core, narrow, first, second, *outs):
    for at in range(4):
        outs[at][0] = narrow[0, at].astype(F32)
        outs[4][0, :, pl.ds(1024 * at, 1024)] = first[0, at].astype(F32)
        outs[5][0, at] = second[0, at].astype(F32)


def unpack(core, total):
    def band(kind):
        return pl.BlockSpec(
            (1, 4, 128, 1024),
            lambda h, b, core: (jnp.where(h == core[0], 1 - core[0], 2), kind, b, 0),
        )

    square = pl.BlockSpec((1, 128, 1024), lambda h, b, core: (0, 2 * h + b, 0))
    result = pl.pallas_call(
        unpack_kernel,
        grid_spec=pltpu.PrefetchScalarGridSpec(
            num_scalar_prefetch=1,
            grid=(2, 2),
            in_specs=[band(2), band(0), band(1)],
            out_specs=[square] * 4
            + [
                pl.BlockSpec((1, 128, 4096), lambda h, b, core: (0, 2 * h + b, 0)),
                pl.BlockSpec((1, 4, 128, 1024), lambda h, b, core: (0, 0, 2 * h + b, 0)),
            ],
        ),
        out_shape=[struct((1, 512, 1024), F32)] * 4
        + [struct((1, 512, 4096), F32), struct((1, 4, 512, 1024), F32)],
        compiler_params=pltpu.CompilerParams(vmem_limit_bytes=VMEM_LIMIT),
        name="unpack",
    )(core.reshape(1), total, total, total)
    return (*result[:5], result[5].reshape(1, 2048, 1024))


def on_device(
    inputs, cotangent, lengths, permutation, query_weight, query_bias, key_weight, value_weight,
    value_bias, output_weight, output_bias, first_gain, first_bias, inner_weight, inner_bias,
    outer_weight, outer_bias, second_gain, second_bias,
):
    core = lax.axis_index("section")
    group = lax.axis_index(GROUP)
    count = lax.axis_size("replica").bit_length() - 1
    shards = [
        w[0] for w in (query_weight, key_weight, value_weight, output_weight, inner_weight, outer_weight)
    ]
    vectors = [
        v[0] for v in (query_bias, value_bias, output_bias, first_gain, first_bias, inner_bias,
                       outer_bias, second_gain, second_bias)
    ]
    everyone = jnp.arange(permutation.shape[0], dtype=jnp.int32)
    own = lax.dynamic_slice_in_dim(permutation, 2 * group + core, 1)
    length = jnp.sum(jnp.where(everyone == own, lengths, 0), keepdims=True)
    inverse = jnp.sum(
        jnp.where(permutation[None, :] == everyone[:, None], everyone[None, :], 0), axis=1
    )
    short = jnp.concatenate(vectors).astype(F32).reshape(UNITS, -1)
    short = jnp.pad(short, ((0, 16 - UNITS), (0, 0)))
    result = forward(length, permutation, short, shards, inputs, count)
    weights, gains, x, low, up = result[:6], result[6], result[7], result[8:20], result[20:32]
    grad = lax.dynamic_index_in_dim(cotangent, core, 0, keepdims=False)
    lower, upper = low[11], up[11]

    def kept(stored, rows):
        q, k, v, log, context, unit1, scale1, act, slope, unit2, scale2 = stored[:11]
        return (unit2, scale2, unit1, scale1, act, slope, rows, q, k, v, log, context)

    total, small, activations, input_grads = backward(
        length, inverse, gains, kept(low, x), kept(up, lower) + (grad,), weights, (lower, upper),
        count,
    )
    side = lax.axis_index("shard")
    pieces, at = [], 0
    for width in VECTORS:
        whole_vector = small[at : at + width].reshape(2, -1)
        pieces.append(lax.dynamic_slice_in_dim(whole_vector, side, 1, axis=0))
        at += width
    dq, dk, dv, do, d1, d2 = unpack(core, total)
    return (
        activations[None], input_grads[None], dq, pieces[0], dk, dv, pieces[1], do, pieces[2],
        pieces[3], pieces[4], d1, pieces[5], d2, pieces[6], pieces[7], pieces[8],
    )


def solution(mesh):
    matrix, vector = P("section", "shard", None), P("section", "shard")
    rows = P(("shard", "replica"), None, None)
    in_specs = (
        rows, rows, P(), P(), matrix, vector, matrix, matrix, vector, matrix, vector, vector,
        vector, matrix, vector, matrix, vector, vector, vector,
    )
    both = P("section", ("shard", "replica"), None, None)
    out_specs = (
        both, both, matrix, vector, matrix, matrix, vector, matrix, vector, vector, vector,
        matrix, vector, matrix, vector, vector, vector,
    )
    return jax.shard_map(
        on_device, mesh=mesh, in_specs=in_specs, out_specs=out_specs, check_vma=False
    )
```

time: 1120 us -> 654 us (0.58)
  matrix products: 242 us -> 0 us
  local copies, waits for them, and re-layouts: 200 us -> 13.9 us
  Pallas kernels: 521 us -> 625 us
  other arithmetic: 106 us -> 10.2 us
  starting transfers between devices: 26.1 us -> 0 us
  waiting for transfers between devices: 16.4 us -> 0 us
    dot_general x48 -> x0, matrix products: 242 us -> none  [the longest x12 55.8 us: dense_left(): jnp.einsum('ra,rb->ab', left_side, right_side, preferred_element_type=jnp...]
    pallas_call x2 -> x3, Pallas kernels: 521 us -> 625 us  [the longest x1 407 us: backward(): pl.pallas_call(kernel, out_shape=out_shape, in_specs=[smem, smem, vmem] +...]
    slice x8 -> x2, local copies, waits for them, and re-layouts: 53.1 us -> 1.88 us  [on_device(): whole_vector = small[at:at + width].reshape(2, -1)]
    unnamed x281 -> x16, local copies, waits for them, and re-layouts: 55.2 us -> 6.33 us
    reshape x22 -> x9, local copies, waits for them, and re-layouts: 41.3 us -> 0.09 us  [on_device(): whole_vector = small[at:at + width].reshape(2, -1)]
    another operation x4 -> x0, other arithmetic: 39 us -> none  [the longest x1 33.7 us: on_device(): jnp.stack([lower_packed, upper_packed])]
    reduce_sum x13 -> x2, other arithmetic: 29.2 us -> 3.22 us  [the longest x1 1.94 us: on_device(): length = jnp.sum(jnp.where(everyone == own, lengths, 0), keepdims=True)]
    all_to_all x4 -> x0, starting transfers between devices: 25.9 us -> none  [the longest x1 8.51 us: own_cotangent(): return lax.all_to_all(ordered, ALL, 0, 0, tiled=True).reshape(shape)]
  transfers between devices with their start and end apart: 5 -> 0, of which waited for: 2 -> 0; matrix products, arithmetic and copies ran while one was open for 30% -> 0% of each run, Pallas kernels for 47% -> 0%
where the time goes in v4:
time: 654 us; the launch traced here: 650 us
  Pallas kernels  625 us (96%)
  local copies, waits for them, and re-layouts  13.9 us (2%)
  other arithmetic  10.2 us (2%)
    pallas_call x1, Pallas kernels, backward(): pl.pallas_call(kernel, out_shape=out_shape, in_specs=[smem, smem, vmem] +...  407 us
    pallas_call x1, Pallas kernels, forward(): pl.pallas_call(kernel, out_shape=out_shape, in_specs=[smem, smem] + [anyw...  205 us

profile of v4, /device:TPU:0, one launch (start us, length us, event | category | flops | bytes accessed | tf_op | source)
XLA Modules:
  0.0 649.7 jit_solution(9362940601416373050)
XLA Ops:
  0.7 1.4 dynamic_slice.34
  2.1 1.9 fusion
  4.0 1.3 select_reduce_fusion.refs_1_
  5.3 0.7 reduce
  6.0 0.7 reduce.1
  6.7 0.7 reduce.2
  7.4 0.7 reduce.3
  8.1 0.7 reduce.4
  8.8 0.7 reduce.6
  9.5 0.7 reduce.7
  10.2 0.7 reduce.8
  10.9 0.7 reduce.5
  11.6 0.3 dynamic-update-slice
  11.9 0.2 dynamic-update-slice.1
  12.1 0.2 dynamic-update-slice.2
  12.3 0.2 dynamic-update-slice.3
  12.7 0.3 dynamic-update-slice.5
  13.0 0.2 dynamic-update-slice.6
  13.6 0.6 pad_convert_fusion.refs_2_
  14.2 1.0 dynamic-slice_bitcast_fusion.refs_27_
  15.3 205.1 %forward.1 = (bf16[2,1024,1024]{2,1,0:T(8,128)(2,1)}, bf16[2,1024,1024]{2,1,0:T(8,128)(2,1)}, bf16[2,1024,1024]{2,1,0:T(8,128)(2,1)}, bf16[2,1024,1024]{2,1,0:T(...) custom-call(s32[1]{0:T(128)} %bitcast.1.refs_0_, ...), custom_call_target="tpu_custom_call" | custom-call | tf_op jit(solution)/shard_map/forward/pallas_call | solution.py:715
  220.4 407.0 %backward.1 = (bf16[36,2,2,2,32,1024]{5,4,3,2,1,0:T(8,128)(2,1)}, f32[12,1024]{1,0:T(8,128)}, bf16[24,2,256,1024]{3,2,1,0:T(8,128)(2,1)}, bf16[2,16,32,1024]{3,2...) custom-call(s32[1]{0:T(128)} %bitcast.1.refs_0_, ...), custom_call_target="tpu_custom_call" | custom-call | tf_op jit(solution)/shard_map/backward/pallas_call | solution.py:1275
  627.5 0.8 slice.32
  628.3 1.0 slice_reduce_fusion
  629.4 0.6 constant_dynamic-slice_fusion.2
  630.0 0.6 constant_dynamic-slice_fusion
  630.6 0.6 constant_dynamic-slice_fusion.3
  631.2 0.6 constant_dynamic-slice_fusion.5
  631.8 0.6 constant_dynamic-slice_fusion.7
  632.4 12.5 %unpack.1 = (f32[1,512,1024]{2,1,0:T(8,128)}, f32[1,512,1024]{2,1,0:T(8,128)}, f32[1,512,1024]{2,1,0:T(8,128)}, f32[1,512,1024]{2,1,0:T(8,128)}, f32[1,512,4096]{2,1,0:T(8,128)}, /*index=5*/f32[1,4,512,1024]{3,2,1,0:T(8,128)}) custom-call(s32[1]{0:T(128)} %bitcast.11.core, bf16[3,12,256,1024]{3,2,1,0:T(8,128)(2,1)} %bitcast.15, ...), custom_call_target="tpu_custom_call" | custom-call | tf_op jit(solution)/shard_map/unpack/pallas_call | solution.py:1337
  644.9 3.2 copy.47
  648.1 1.3 copy.48
  (20 shorter events, 0.7 us)
Async XLA Ops:
  0.7 13.6 %copy-start = (bf16[2,512,1024]{2,1,0:T(8,128)(2,1)S(1)}, bf16[2,512,1024]{2,1,0:T(8,128)(2,1)}, u32[]{:S(2)}) copy-start(bf16[2,512,1024]{2,1,0:T(8,128)(2,1)} %param.20) | copy-start | bytes 6291460
  644.9 3.2 copy-start.2
  644.9 4.6 copy-start.1

commit v5 on v4

--- a/solution.py
+++ b/solution.py
@@ -54,6 +54,131 @@
         device_id=partner,
         device_id_type=pl.DeviceIdType.MESH,
     )
+
+
+def device_of(number, groups):
+    return lax.rem(number, 2) * groups + number // 2
+
+
+class Deal:
+    def __init__(self, layer, source, target, inverse, buffers):
+        (self.spread, self.ordered, self.send1, self.recv1, self.send2, self.recv2) = buffers
+        self.layer, self.source, self.target, self.inverse = layer, source, target, inverse
+        self.groups = self.spread.shape[0] // 2
+        self.replicas = self.groups // 2
+        self.chunk = self.spread.shape[1]
+        self.core = lax.axis_index("section")
+        self.group = lax.axis_index("shard") * self.replicas + lax.axis_index("replica")
+        self.me = self.core * self.groups + self.group
+
+    def chip(self, index):
+        return {
+            "section": self.layer, "shard": index // self.replicas,
+            "replica": lax.rem(index, self.replicas),
+        }
+
+    def rows_of(self, index):
+        return self.source.at[pl.ds(pl.multiple_of(index * self.chunk, self.chunk), self.chunk)]
+
+    def first(self, index):
+        return remote(
+            self.rows_of(index), self.spread.at[self.me], self.send1.at[index],
+            self.recv1.at[self.me], self.chip(index),
+        )
+
+    def first_own(self):
+        return pltpu.make_async_copy(
+            self.rows_of(self.group), self.spread.at[self.me], self.recv1.at[self.me]
+        )
+
+    def home(self, index):
+        return remote(
+            self.ordered.at[pl.ds(2 * index, 2)], self.target.at[:, self.group],
+            self.send2.at[index], self.recv2.at[self.group], self.chip(index),
+        )
+
+    def home_own(self):
+        return pltpu.make_async_copy(
+            self.ordered.at[pl.ds(2 * self.group, 2)], self.target.at[:, self.group],
+            self.recv2.at[self.group],
+        )
+
+    def each_first(self, act):
+        def body(step, carry):
+            @pl.when(jnp.logical_or(step > 0, self.core != self.layer))
+            def _():
+                act(self.first(lax.rem(self.group + step, self.groups)))
+            return carry
+
+        lax.fori_loop(0, self.groups, body, 0)
+
+    def start(self):
+        @pl.when(self.core == self.layer)
+        def _():
+            self.first_own().start()
+
+        self.each_first(lambda copy: copy.start())
+
+    def second(self):
+        @pl.when(self.core == self.layer)
+        def _():
+            self.first_own().wait()
+
+            def landed(step, carry):
+                source = lax.rem(self.me + step, 2 * self.groups)
+                here = self.spread.at[source]
+                remote(
+                    here, here, self.send1.at[lax.rem(source, self.groups)],
+                    self.recv1.at[source], place(source, self.replicas),
+                ).wait_recv()
+                return carry
+
+            lax.fori_loop(1, 2 * self.groups, landed, 0)
+
+            def reorder(slot, carry):
+                self.ordered[slot] = self.spread[device_of(self.inverse[slot], self.groups)]
+                return carry
+
+            lax.fori_loop(0, 2 * self.groups, reorder, 0)
+            self.home_own().start()
+
+            def send(step, carry):
+                self.home(lax.rem(self.group + step, self.groups)).start()
+                return carry
+
+            lax.fori_loop(1, self.groups, send, 0)
+
+    def last(self):
+        self.each_first(lambda copy: copy.wait_send())
+
+        @pl.when(self.core == self.layer)
+        def _():
+            self.home_own().wait()
+
+            def landed(step, carry):
+                source = lax.rem(self.group + step, self.groups)
+                here = self.target.at[:, source]
+                remote(
+                    here, here, self.send2.at[source], self.recv2.at[source], self.chip(source)
+                ).wait_recv()
+                return carry
+
+            lax.fori_loop(1, self.groups, landed, 0)
+
+            def sent(step, carry):
+                self.home(lax.rem(self.group + step, self.groups)).wait_send()
+                return carry
+
+            lax.fori_loop(1, self.groups, sent, 0)
+
+
+def deal_buffers(groups, chunk, width):
+    dma = pltpu.SemaphoreType.DMA
+    return [
+        pltpu.VMEM((2 * groups, chunk, width), jnp.bfloat16),
+        pltpu.VMEM((2 * groups, chunk, width), jnp.bfloat16),
+        dma((groups,)), dma((2 * groups,)), dma((groups,)), dma((groups,)),
+    ]
 
 
 HEAD_DIM = 64
@@ -274,9 +399,10 @@
 
 UNIT_ORDER = (0, 1, 2, 3, 4, 8, 9, 5, 10, 11, 6, 7)
 DIRECT_SETS = ((0, 1, 6, 7), (0, 1, 6, 7))
-HOPS = (0.0, 4.0, 8.0, 15.0, 18.0, 21.0, 24.0)
-PACE = 5.6
-CROSS = 11.3
+HOPS = (0.0, 10.0, 20.0, 34.0, 36.0, 40.0, 44.0)
+PACE = 7.0
+CROSS = 17.0
+OUT_STEP = 1
 
 
 class Plan:
@@ -310,8 +436,10 @@
             self.run_first()
 
 
-def front_kernel(count, length, permutation, small, shards, inputs, outs, scratch):
+def front_kernel(count, length, permutation, inverse, small, shards, inputs, outs, scratch):
     full, (rows_out, dealt), stored = outs[:6], outs[6:8], (outs[8:20], outs[20:32])
+    deal = Deal(0, outs[19], outs[32], inverse, scratch[:6])
+    scratch = scratch[6:]
     (stage, spread, ordered, halves, rows, xs, unit1, scale1, unit2, scale2, low, total,
      send_sem, recv_sem, load_sem, store_sem, deal_send, deal_recv, home_send, home_recv,
      small_send, small_recv, keep_sem) = scratch
@@ -536,13 +664,13 @@
             if unit in DIRECT_SETS[layer]:
                 landing = 14.0 + CROSS * (number[0] + 1)
                 number[0] += 1
-                plan.add(landing - 2.5 * CROSS, ("cross",) + key, lambda l=layer, u=unit: cross(l, u))
+                plan.add(landing - 1.7 * CROSS, ("cross",) + key, lambda l=layer, u=unit: cross(l, u))
                 plan.add(landing, ("hop",) + key, lambda l=layer, u=unit: hop(l, u, 0))
                 plan.add(landing + 3.0, ("unit",) + key, lambda l=layer, u=unit: passed(l, u))
             else:
                 begin = 6.0 + PACE * number[1]
                 number[1] += 1
-                plan.add(begin - 16.0, ("cross",) + key, lambda l=layer, u=unit: cross(l, u))
+                plan.add(begin - 60.0, ("cross",) + key, lambda l=layer, u=unit: cross(l, u))
                 for k in range(count + 1):
                     plan.add(
                         begin + HOPS[k], ("hop", k) + key, lambda l=layer, u=unit, k=k: hop(l, u, k)
@@ -551,8 +679,8 @@
                     begin + HOPS[count] + 3.0, ("unit",) + key,
                     lambda l=layer, u=unit: passed(l, u),
                 )
-    plan.add(20.0, "deal", deal_second)
-    plan.add(40.0, "inputs", deal_last)
+    plan.add(30.0, "deal", deal_second)
+    plan.add(50.0, "inputs", deal_last)
     plan.add(10.0, "vectors", vectors_here)
     plan.sort()
 
@@ -623,6 +751,8 @@
                 low, total,
             )
             during(step, hidden_steps, begin, 2.5, lambda at: feed_needs(layer, at + 2))
+            if layer == 1:
+                pl.when(step == OUT_STEP)(deal.second)
 
         pltpu.emit_pipeline(
             body,
@@ -639,7 +769,7 @@
         copy.start()
         return copy
 
-    begin = (45.0, 95.0)
+    begin = (75.0, 125.0)
     keeping = []
     for layer in range(2):
         plan.require(["vectors", "inputs"] + [("unit", layer, unit) for unit in range(4)])
@@ -657,9 +787,13 @@
             keep(unit2, stored[layer][9], 4), keep(scale2, stored[layer][10], 5),
             keep(xs, stored[layer][11], 6),
         ]
+        if layer == 0:
+            keeping.pop().wait()
+            deal.start()
     plan.until(1000000.0)
     for copy in keeping:
         copy.wait()
+    deal.last()
     lax.fori_loop(1, groups, spread_done, 0)
     lax.fori_loop(1, devices, home_done, 0)
     for index, partner in enumerate((sibling, facing, corner)):
@@ -683,7 +817,7 @@
                 wire(layer, unit, count + 2, own, own, sibling).wait_send()
 
 
-def forward(length, permutation, small, shards, inputs, count):
+def forward(length, permutation, inverse, small, shards, inputs, count):
     groups = 2 << count
     slots, width = inputs.shape[1:]
     hidden = shards[4].shape[-1]
@@ -701,23 +835,24 @@
         [struct((2, width, width), BF)] * 4
         + [struct((2, width, hidden), BF), struct((2, hidden, width), BF)]
         + [struct((2,) + small.shape[:1] + (width,), F32), struct(square, BF)]
-        + layer + layer
+        + layer + layer + [struct((2, groups, slots // groups, width), BF)]
     )
     smem = pl.BlockSpec(memory_space=pltpu.SMEM)
     anywhere = pl.BlockSpec(memory_space=pl.ANY)
 
     def kernel(*refs):
         front_kernel(
-            count, *refs[:3], refs[3:9], refs[9], refs[10 : 10 + len(out_shape)],
-            refs[10 + len(out_shape) :],
+            count, *refs[:4], refs[4:10], refs[10], refs[11 : 11 + len(out_shape)],
+            refs[11 + len(out_shape) :],
         )
 
     return pl.pallas_call(
         kernel,
         out_shape=out_shape,
-        in_specs=[smem, smem] + [anywhere] * 8,
+        in_specs=[smem] * 3 + [anywhere] * 8,
         out_specs=[anywhere] * len(out_shape),
-        scratch_shapes=[
+        scratch_shapes=deal_buffers(groups, slots // groups, width)
+        + [
             pltpu.VMEM((UNITS, 512, 1024), BF), pltpu.VMEM(part, BF), pltpu.VMEM(part, BF),
             pltpu.VMEM((2, 2) + small.shape, F32),
             pltpu.VMEM((2,) + small.shape[:1] + (width,), F32),
@@ -732,31 +867,28 @@
             collective_id=0, has_side_effects=True, vmem_limit_bytes=VMEM_LIMIT
         ),
         name="forward",
-    )(length, permutation, small, *shards, inputs)
+    )(length, permutation, inverse, small, *shards, inputs)
 
 
 SENT_RING = 4
 LAND_RING = 5
 PIECES = 2 * UNITS
 DEAL_STEP = 5
-EARLY = ((0, 1, 2, 3), (1, 3, 5, 7), (0, 1, 2, 3))
+EARLY = ((0, 1, 2, 3), (1, 3, 5, 7), (0, 1, 2, 3), (6,))
 AHEAD = sum(len(steps) for steps in EARLY)
 
 
-def device_of(number, groups):
-    return lax.rem(number, 2) * groups + number // 2
-
-
-def back_kernel(count, length, inverse, gains, lower, upper, weights, results, outs, scratch):
-    (total, small_total, landing, dealt, acts, d1_low, d2_low, dqkv_low, do_low, up_d1, up_d2,
+def back_kernel(count, length, inverse, gains, lower, upper, weights, result, outs, scratch):
+    (total, small_total, landing, _, acts, d1_low, d2_low, dqkv_low, do_low, up_d1, up_d2,
      dqkv_up, do_up, grad_low, grad_up) = outs
     (xs, first, gradient, unit1, unit2, scale1, scale2, second, outer, middle, running, attended,
      vectors, inner_rows, sums) = scratch[:15]
     (own, came, across_half, kept, from_x), rest = scratch[15:20], scratch[20:]
     halves, rest = rest[:count], rest[count:]
-    (spread, ordered, smalls, small_own, small_recv, send0, recv0, send_x, recv_x, send_rs, recv_rs,
-     send_ag, recv_ag, load_sem, came_sem, piece_sem, small_send, small_arrive, deal_send,
-     deal_recv, home_send, home_recv, act_sem, total_sem, fetch_sem, done_send, done_recv) = rest
+    deal = Deal(1, result, outs[3], inverse, rest[:6])
+    (smalls, small_own, small_recv, send0, recv0, send_x, recv_x, send_rs, recv_rs,
+     send_ag, recv_ag, load_sem, came_sem, piece_sem, small_send, small_arrive,
+     act_sem, total_sem, fetch_sem, done_send, done_recv) = rest[6:]
     wq, wk, wv, wo, w1, w2 = weights
     (up_unit2, up_scale2, up_unit1, up_scale1, up_act, up_slope, up_x, up_q, up_k, up_v, up_log,
      up_context, cotangent) = upper
@@ -775,7 +907,6 @@
     groups = 2 * replicas
     group = side * replicas + replica
     me = core * groups + group
-    chunk = spread.shape[1]
     greet_all(me, 2 * groups, replicas)
 
     layers = ((up_d1, up_d2, dqkv_up, do_up), (d1_low, d2_low, dqkv_low, do_low))
@@ -794,10 +925,10 @@
         source = landing.at[unit] if source is None else source
         return remote(source, landing.at[unit], send0.at[unit], recv0.at[unit], sibling)
 
-    def send_core(order, which):
+    def send_core(order, which, only=range(PIECES)):
         for at_order, index, low, high in ranges:
             if at_order == order and index in which:
-                for unit in range(low, high):
+                for unit in [u for u in range(low, high) if u in only]:
                     core_copy(unit, part_of(order, index, unit - low, 1 - core)).start()
 
     def own_load(source, slot):
@@ -862,64 +993,6 @@
         return remote(
             source, small_recv.at[step], small_send.at[step], small_arrive.at[step], partner[step]
         )
-
-    def chunk_of(layer, target):
-        return results[layer].at[pl.ds(pl.multiple_of(target * chunk, chunk), chunk)]
-
-    def spread_copy(layer, target):
-        return remote(
-            chunk_of(layer, lax.rem(target, groups)), spread.at[me], deal_send.at[target],
-            deal_recv.at[me], place(target, replicas),
-        )
-
-    def spread_own(layer):
-        return pltpu.make_async_copy(chunk_of(layer, group), spread.at[me], deal_recv.at[me])
-
-    def spread_start(step, carry):
-        target = lax.rem(me + step, 2 * groups)
-        for layer in range(2):
-            @pl.when(target // groups == layer)
-            def _():
-                spread_copy(layer, target).start()
-        return carry
-
-    def spread_wait(step, carry):
-        source = lax.rem(me + step, 2 * groups)
-        remote(
-            spread.at[source], spread.at[source], deal_send.at[source], deal_recv.at[source],
-            place(source, replicas),
-        ).wait_recv()
-        return carry
-
-    def chip(index):
-        return {"shard": index // replicas, "replica": lax.rem(index, replicas)}
-
-    def home_copy(target):
-        return remote(
-            ordered.at[pl.ds(2 * target, 2)], dealt.at[:, group], home_send.at[target],
-            home_recv.at[group], chip(target),
-        )
-
-    def home_own():
-        return pltpu.make_async_copy(
-            ordered.at[pl.ds(2 * group, 2)], dealt.at[:, group], home_recv.at[group]
-        )
-
-    def home_start(step, carry):
-        home_copy(lax.rem(group + step, groups)).start()
-        return carry
-
-    def home_wait(step, carry):
-        source = lax.rem(group + step, groups)
-        remote(
-            dealt.at[:, source], dealt.at[:, source], home_send.at[source], home_recv.at[source],
-            chip(source),
-        ).wait_recv()
-        return carry
-
-    def reorder(slot, carry):
-        ordered[slot] = spread[device_of(inverse[slot], groups)]
-        return carry
 
     def places_of(index, dims):
         return tuple((lax.rem(index // (1 << (dims - 1 - q)), 2) for q in range(dims)))
@@ -1032,7 +1105,7 @@
                         done_copy(unit).start()
 
     def early(step, phase):
-        before = sum(len(steps) for steps in EARLY[:phase])
+        before = 0 if phase == 3 else len(EARLY[3]) + sum(len(steps) for steps in EARLY[:phase])
         now = -1
         for at, when in enumerate(EARLY[phase]):
             now = jnp.where(step == when, before + at, now)
@@ -1051,11 +1124,7 @@
         fetch(up_scale1, scale1, 4), fetch(up_scale2, scale2, 5),
     ]
     up_rows = fetch(up_x, xs, 1)
-    for layer in range(2):
-        @pl.when(core == layer)
-        def _():
-            spread_own(layer).start()
-    lax.fori_loop(1, 2 * groups, spread_start, 0)
+    deal.start()
     for copy in waits:
         copy.wait()
 
@@ -1093,18 +1162,9 @@
             smalls[layer, 0:1, lanes] = sums[at, 0:1]
             smalls[layer, 1:2, lanes] = sums[at, 1:2]
 
-    hidden_band = pl.BlockSpec((slots, HIDDEN_BLOCK), lambda j: (0, j))
-
-    def deal_second():
-        spread_own(0).wait()
-        lax.fori_loop(1, 2 * groups, spread_wait, 0)
-        lax.fori_loop(0, 2 * groups, reorder, 0)
-        home_own().start()
-        lax.fori_loop(1, groups, home_start, 0)
-
-    def feed_stage(layer, act, slope, d1, d2):
+    def feed_stage(layer, act, slope, d1, d2, begin, steps):
         def body(*refs):
-            step = pl.program_id(0)
+            step = pl.program_id(0) + begin
             feed_back_body(
                 step, hidden_steps, length, gradient, unit2, scale2, gains.at[layer, 10:11],
                 unit1, scale1, gains.at[layer, 3:4], gains.at[layer, 4:5], *refs, first,
@@ -1112,27 +1172,33 @@
             )
             if layer == 0:
                 early(step, 1)
-            else:
-                pl.when(step == DEAL_STEP)(deal_second)
-
+            elif begin > 0:
+                pl.when(step == DEAL_STEP)(deal.second)
+                early(step, 3)
+
+        half = hidden_steps // 2
+        hidden_band = pl.BlockSpec((slots, HIDDEN_BLOCK), lambda j: (0, j + begin))
         pltpu.emit_pipeline(
             body,
-            grid=(hidden_steps,),
+            grid=(steps,),
             in_specs=[
                 hidden_band, hidden_band,
-                pl.BlockSpec((width, HIDDEN_BLOCK), lambda j: (0, j)),
-                pl.BlockSpec((HIDDEN_BLOCK, width), lambda j: (j, 0)),
+                pl.BlockSpec((width, HIDDEN_BLOCK), lambda j: (0, j + begin)),
+                pl.BlockSpec((HIDDEN_BLOCK, width), lambda j: (j + begin, 0)),
             ],
             out_specs=[
                 pl.BlockSpec(
-                    (2, 1, 512, HIDDEN_BLOCK), lambda j: (0, j // wide_per, 0, j % wide_per)
+                    (2, 1, 512, HIDDEN_BLOCK),
+                    lambda j: (0, (j + begin) // wide_per, 0, (j + begin) % wide_per),
                 ),
                 pl.BlockSpec(
                     (1, pairs, 512, width),
-                    lambda j: (j // (hidden_steps // 2), j % (hidden_steps // 2), 0, 0),
+                    lambda j: ((j + begin) // half, (j + begin) % half, 0, 0),
                 ),
             ],
         )(act, slope, w1.at[layer], w2.at[layer], d1, d2)
+
+    def feed_sums(layer):
         for at, source in ((2, 5), (3, 3), (4, 4), (9, 0), (10, 1), (11, 2)):
             smalls[layer, at : at + 1] = vectors[source : source + 1]
         for at in range(hidden_steps):
@@ -1140,8 +1206,12 @@
             lanes = pl.ds(HIDDEN_BLOCK * (at % wide_per), HIDDEN_BLOCK)
             smalls[layer, line : line + 1, lanes] = inner_rows[at, 0:1]
 
-    feed_stage(1, up_act, up_slope, up_d1, up_d2)
-    send_core(0, (0, 1))
+    start_units = UNITS // 6
+    feed_stage(1, up_act, up_slope, up_d1, up_d2, 0, hidden_steps // 2)
+    send_core(0, (0, 1), range(start_units))
+    feed_stage(1, up_act, up_slope, up_d1, up_d2, hidden_steps // 2, hidden_steps // 2)
+    feed_sums(1)
+    send_core(0, (0, 1), range(start_units, 2 * UNITS))
     later = [
         fetch(low_unit1, unit1, 2), fetch(low_unit2, unit2, 3), fetch(low_scale1, scale1, 4),
         fetch(low_scale2, scale2, 5),
@@ -1152,7 +1222,8 @@
     waits = [fetch(gradient, grad_up, 0), fetch(low_x, xs, 1)]
     for copy in later:
         copy.wait()
-    feed_stage(0, low_act, low_slope, d1_low, d2_low)
+    feed_stage(0, low_act, low_slope, d1_low, d2_low, 0, hidden_steps)
+    feed_sums(0)
     send_core(1, (0, 1))
     for copy in waits:
         copy.wait()
@@ -1216,18 +1287,7 @@
     for step in range(small_steps):
         small_copy(step).wait_send()
 
-    def spread_done(step, carry):
-        spread_copy(0, lax.rem(me + step, 2 * groups)).wait_send()
-        return carry
-
-    def home_done(step, carry):
-        home_copy(lax.rem(group + step, groups)).wait_send()
-        return carry
-
-    lax.fori_loop(1, 2 * groups, spread_done, 0)
-    home_own().wait()
-    lax.fori_loop(1, groups, home_wait, 0)
-    lax.fori_loop(1, groups, home_done, 0)
+    deal.last()
     back = remote(both[0], acts.at[1 - core], act_sem.at[0], act_sem.at[1], sibling)
     back.wait_send()
     back.wait_recv()
@@ -1235,24 +1295,27 @@
     out.wait()
 
 
-def backward(length, inverse, gains, lower, upper, weights, results, count):
+def backward(length, inverse, gains, lower, upper, weights, result, count):
     cut = (2,) * count
     rows = HALF // (1 << count)
     narrow = cut + (rows, 1024)
     dma = pltpu.SemaphoreType.DMA
     groups = 2 << count
-    slots, width = results[0].shape
+    slots, width = result.shape
     chunk = slots // groups
     keep_ring = count + 5
     hidden = weights[4].shape[-1]
-    sizes = [len(lower), len(upper), len(weights), len(results)]
+    sizes = [len(lower), len(upper), len(weights)]
 
     def kernel(*refs):
         start, groups_of = 3, []
         for size in sizes:
             groups_of.append(refs[start : start + size])
             start += size
-        back_kernel(count, *refs[:3], *groups_of, refs[start : start + 15], refs[start + 15 :])
+        back_kernel(
+            count, *refs[:3], *groups_of, refs[start], refs[start + 1 : start + 16],
+            refs[start + 16 :],
+        )
 
     anywhere = pl.BlockSpec(memory_space=pl.ANY)
     vmem = pl.BlockSpec(memory_space=pltpu.VMEM)
@@ -1275,7 +1338,7 @@
     result = pl.pallas_call(
         kernel,
         out_shape=out_shape,
-        in_specs=[smem, smem, vmem] + [anywhere] * sum(sizes),
+        in_specs=[smem, smem, vmem] + [anywhere] * (sum(sizes) + 1),
         out_specs=[anywhere] * len(out_shape),
         scratch_shapes=[
             pltpu.VMEM(square, BF), pltpu.VMEM(square, F32), pltpu.VMEM(square, BF),
@@ -1293,23 +1356,21 @@
             pltpu.VMEM((LAND_RING, HALF, 1024), BF),
         ]
         + [pltpu.VMEM((LAND_RING,) + (2,) * p + (rows, 1024), BF) for p in range(count)]
+        + deal_buffers(groups, chunk, width)
         + [
-            pltpu.VMEM((2 * groups, chunk, width), BF),
-            pltpu.VMEM((2 * groups, chunk, width), BF),
             pltpu.VMEM((2,) + vectors, F32),
             pltpu.VMEM((count + 2,) + vectors, F32),
             pltpu.VMEM((count + 2,) + vectors, F32),
             dma((PIECES,)), dma((PIECES,)), dma((PIECES,)), dma((PIECES,)),
             dma((count, PIECES)), dma((count, PIECES)), dma((count, PIECES)), dma((count, PIECES)),
             dma((2,)), dma((2,)), dma((PIECES,)), dma((count + 2,)), dma((count + 2,)),
-            dma((2 * groups,)), dma((2 * groups,)), dma((groups,)), dma((groups,)),
             dma((3,)), dma, dma((6,)), dma((UNITS,)), dma((UNITS,)),
         ],
         compiler_params=pltpu.CompilerParams(
             collective_id=1, has_side_effects=True, vmem_limit_bytes=VMEM_LIMIT
         ),
         name="backward",
-    )(length, inverse, gains, *lower, *upper, *weights, *results)
+    )(length, inverse, gains, *lower, *upper, *weights, result)
     total, small_total, _, dealt, acts = result[:5]
     return total.reshape(3, UNITS, HALF, 1024), small_total, dealt.reshape(2, slots, width), acts
 
@@ -1377,19 +1438,21 @@
     )
     short = jnp.concatenate(vectors).astype(F32).reshape(UNITS, -1)
     short = jnp.pad(short, ((0, 16 - UNITS), (0, 0)))
-    result = forward(length, permutation, short, shards, inputs, count)
+    result = forward(length, permutation, inverse, short, shards, inputs, count)
     weights, gains, x, low, up = result[:6], result[6], result[7], result[8:20], result[20:32]
     grad = lax.dynamic_index_in_dim(cotangent, core, 0, keepdims=False)
     lower, upper = low[11], up[11]
+    lower_home = result[32].reshape(2, *lower.shape)
 
     def kept(stored, rows):
         q, k, v, log, context, unit1, scale1, act, slope, unit2, scale2 = stored[:11]
         return (unit2, scale2, unit1, scale1, act, slope, rows, q, k, v, log, context)
 
-    total, small, activations, input_grads = backward(
-        length, inverse, gains, kept(low, x), kept(up, lower) + (grad,), weights, (lower, upper),
+    total, small, upper_home, input_grads = backward(
+        length, inverse, gains, kept(low, x), kept(up, lower) + (grad,), weights, upper,
         count,
     )
+    activations = jnp.where(core == 0, lower_home, upper_home)
     side = lax.axis_index("shard")
     pieces, at = [], 0
     for width in VECTORS:

time: 654 us -> 613 us (0.937)
  Pallas kernels: 625 us -> 581 us
    pallas_call x1, Pallas kernels: 407 us -> 373 us  [backward(): pl.pallas_call(kernel, out_shape=out_shape, in_specs=[smem, smem, vmem] +...]
    pallas_call x1, Pallas kernels: 205 us -> 195 us  [forward(): pl.pallas_call(kernel, out_shape=out_shape, in_specs=[smem] * 3 + [anywhe...]
where the time goes in v5:
time: 613 us; the launch traced here: 605 us
  Pallas kernels  581 us (95%)
  other arithmetic  11.7 us (2%)
  local copies, waits for them, and re-layouts  10.9 us (2%)
    pallas_call x1, Pallas kernels, backward(): pl.pallas_call(kernel, out_shape=out_shape, in_specs=[smem, smem, vmem] +...  373 us
    pallas_call x1, Pallas kernels, forward(): pl.pallas_call(kernel, out_shape=out_shape, in_specs=[smem] * 3 + [anywhe...  195 us
    pallas_call x1, Pallas kernels, unpack(): pl.pallas_call(unpack_kernel, grid_spec=pltpu.PrefetchScalarGridSpec(num_...  13.4 us

profile of v5, /device:TPU:0, one launch (start us, length us, event | category | flops | bytes accessed | tf_op | source)
XLA Modules:
  0.0 604.5 jit_solution(3503667300841388223)
XLA Ops:
  0.7 1.4 dynamic_slice.34
  2.1 1.9 fusion
  4.0 1.3 select_reduce_fusion.refs_2_.refs_1_
  5.3 0.7 reduce
  6.0 0.2 dynamic-update-slice
  6.2 0.7 reduce.1
  6.9 0.2 dynamic-update-slice.1
  7.2 0.7 reduce.2
  7.9 0.2 dynamic-update-slice.2
  8.1 0.7 reduce.3
  8.8 0.2 dynamic-update-slice.3
  9.1 0.7 reduce.4
  9.8 0.2 dynamic-update-slice.4
  10.0 0.7 reduce.5
  10.8 0.3 dynamic-update-slice.5
  11.0 0.7 reduce.6
  11.8 0.2 dynamic-update-slice.6
  12.0 0.7 reduce.7
  12.7 0.2 dynamic-update-slice.7
  12.9 0.7 reduce.8
  13.9 0.6 pad_convert_fusion.refs_3_
  14.5 194.9 %forward.1 = (bf16[2,1024,1024]{2,1,0:T(8,128)(2,1)}, bf16[2,1024,1024]{2,1,0:T(8,128)(2,1)}, bf16[2,1024,1024]{2,1,0:T(8,128)(2,1)}, bf16[2,1024,1024]{2,1,0:T(...) custom-call(s32[1]{0:T(128)} %bitcast.1.refs_0_, ...), custom_call_target="tpu_custom_call" | custom-call | tf_op jit(solution)/shard_map/forward/pallas_call | solution.py:849
  209.5 1.0 dynamic-slice_bitcast_fusion.refs_27_
  210.5 372.6 %backward.1 = (bf16[36,2,2,2,32,1024]{5,4,3,2,1,0:T(8,128)(2,1)}, f32[12,1024]{1,0:T(8,128)}, bf16[24,2,256,1024]{3,2,1,0:T(8,128)(2,1)}, bf16[2,16,32,1024]{3,2...) custom-call(s32[1]{0:T(128)} %bitcast.1.refs_0_, ...), custom_call_target="tpu_custom_call" | custom-call | tf_op jit(solution)/shard_map/backward/pallas_call | solution.py:1338
  583.1 1.5 broadcast_select_fusion
  584.7 13.4 %unpack.1 = (f32[1,512,1024]{2,1,0:T(8,128)}, f32[1,512,1024]{2,1,0:T(8,128)}, f32[1,512,1024]{2,1,0:T(8,128)}, f32[1,512,1024]{2,1,0:T(8,128)}, f32[1,512,4096]{2,1,0:T(8,128)}, /*index=5*/f32[1,4,512,1024]{3,2,1,0:T(8,128)}) custom-call(s32[1]{0:T(128)} %bitcast.11.core, bf16[3,12,256,1024]{3,2,1,0:T(8,128)(2,1)} %bitcast.15, ...), custom_call_target="tpu_custom_call" | custom-call | tf_op jit(solution)/shard_map/unpack/pallas_call | solution.py:1398
  598.2 0.6 constant_dynamic-slice_fusion.7
  598.8 0.6 constant_dynamic-slice_fusion.5
  599.4 0.6 constant_dynamic-slice_fusion.3
  600.0 0.6 constant_dynamic-slice_fusion.2
  600.7 0.6 constant_dynamic-slice_fusion
  601.2 3.1 copy.46
  (22 shorter events, 0.5 us)
Async XLA Ops:
  0.7 208.8 %copy-start = (bf16[2,512,1024]{2,1,0:T(8,128)(2,1)S(1)}, bf16[2,512,1024]{2,1,0:T(8,128)(2,1)}, u32[]{:S(2)}) copy-start(bf16[2,512,1024]{2,1,0:T(8,128)(2,1)} %param.20) | copy-start | bytes 6291460
  210.5 372.6 %copy-start.2 = (bf16[2,16,32,1024]{3,2,1,0:T(8,128)(2,1)S(1)}, bf16[2,16,32,1024]{3,2,1,0:T(8,128)(2,1)}, u32[]{:S(2)}) copy-start(bf16[2,16,32,1024]{3,2,1,0:T(8,128)(2,1)} %get-tuple-element.60) | copy-start | bytes 6291460
  584.7 13.4 %copy-start.3 = (f32[12,1024]{1,0:T(8,128)S(1)}, f32[12,1024]{1,0:T(8,128)}, u32[]{:S(2)}) copy-start(f32[12,1024]{1,0:T(8,128)} %get-tuple-element.97) | copy-start | bytes 147460
  584.7 19.6 %copy-start.1 = (bf16[2,512,1024]{2,1,0:T(8,128)(2,1)S(1)}, bf16[2,512,1024]{2,1,0:T(8,128)(2,1)}, u32[]{:S(2)}) copy-start(bf16[2,512,1024]{2,1,0:T(8,128)(2,1)} %param.20) | copy-start | bytes 6291460

commit v6 on v5

--- a/solution.py
+++ b/solution.py
@@ -402,7 +402,7 @@
 HOPS = (0.0, 10.0, 20.0, 34.0, 36.0, 40.0, 44.0)
 PACE = 7.0
 CROSS = 17.0
-OUT_STEP = 1
+OUT_STEP = 3
 
 
 class Plan:
@@ -724,6 +724,8 @@
             step = pl.program_id(0)
             attend_body(step, attention_steps, length, xs, rows, layer, *refs, unit1, scale1, total)
             during(step, attention_steps, begin, 5.0, lambda at: [])
+            if layer == 1:
+                pl.when(step == OUT_STEP)(deal.second)
 
         pltpu.emit_pipeline(
             body,
@@ -751,8 +753,6 @@
                 low, total,
             )
             during(step, hidden_steps, begin, 2.5, lambda at: feed_needs(layer, at + 2))
-            if layer == 1:
-                pl.when(step == OUT_STEP)(deal.second)
 
         pltpu.emit_pipeline(
             body,

time: 613 us -> 605 us (0.987)
  Pallas kernels: 581 us -> 574 us
where the time goes in v6:
time: 605 us; the launch traced here: 598 us
  Pallas kernels  574 us (95%)
  other arithmetic  11.7 us (2%)
  local copies, waits for them, and re-layouts  10.9 us (2%)
    pallas_call x1, Pallas kernels, backward(): pl.pallas_call(kernel, out_shape=out_shape, in_specs=[smem, smem, vmem] +...  370 us
    pallas_call x1, Pallas kernels, forward(): pl.pallas_call(kernel, out_shape=out_shape, in_specs=[smem] * 3 + [anywhe...  190 us
    pallas_call x1, Pallas kernels, unpack(): pl.pallas_call(unpack_kernel, grid_spec=pltpu.PrefetchScalarGridSpec(num_...  13.4 us

profile of v6, /device:TPU:0, one launch (start us, length us, event | category | flops | bytes accessed | tf_op | source)
XLA Modules:
  0.0 597.6 jit_solution(16914727300478398791)
XLA Ops:
  0.7 1.4 dynamic_slice.34
  2.1 1.9 fusion
  4.0 1.3 select_reduce_fusion.refs_2_.refs_1_
  5.3 0.7 reduce
  6.0 0.2 dynamic-update-slice
  6.2 0.7 reduce.1
  6.9 0.2 dynamic-update-slice.1
  7.2 0.7 reduce.2
  7.9 0.2 dynamic-update-slice.2
  8.1 0.7 reduce.3
  8.8 0.2 dynamic-update-slice.3
  9.1 0.7 reduce.4
  9.8 0.2 dynamic-update-slice.4
  10.0 0.7 reduce.5
  10.8 0.3 dynamic-update-slice.5
  11.0 0.7 reduce.6
  11.8 0.2 dynamic-update-slice.6
  12.0 0.7 reduce.7
  12.7 0.2 dynamic-update-slice.7
  12.9 0.7 reduce.8
  13.9 0.6 pad_convert_fusion.refs_3_
  14.5 190.3 %forward.1 = (bf16[2,1024,1024]{2,1,0:T(8,128)(2,1)}, bf16[2,1024,1024]{2,1,0:T(8,128)(2,1)}, bf16[2,1024,1024]{2,1,0:T(8,128)(2,1)}, bf16[2,1024,1024]{2,1,0:T(...) custom-call(s32[1]{0:T(128)} %bitcast.1.refs_0_, ...), custom_call_target="tpu_custom_call" | custom-call | tf_op jit(solution)/shard_map/forward/pallas_call | solution.py:849
  204.9 1.0 dynamic-slice_bitcast_fusion.refs_27_
  205.9 370.3 %backward.1 = (bf16[36,2,2,2,32,1024]{5,4,3,2,1,0:T(8,128)(2,1)}, f32[12,1024]{1,0:T(8,128)}, bf16[24,2,256,1024]{3,2,1,0:T(8,128)(2,1)}, bf16[2,16,32,1024]{3,2...) custom-call(s32[1]{0:T(128)} %bitcast.1.refs_0_, ...), custom_call_target="tpu_custom_call" | custom-call | tf_op jit(solution)/shard_map/backward/pallas_call | solution.py:1338
  576.2 1.5 broadcast_select_fusion
  577.8 13.4 %unpack.1 = (f32[1,512,1024]{2,1,0:T(8,128)}, f32[1,512,1024]{2,1,0:T(8,128)}, f32[1,512,1024]{2,1,0:T(8,128)}, f32[1,512,1024]{2,1,0:T(8,128)}, f32[1,512,4096]{2,1,0:T(8,128)}, /*index=5*/f32[1,4,512,1024]{3,2,1,0:T(8,128)}) custom-call(s32[1]{0:T(128)} %bitcast.11.core, bf16[3,12,256,1024]{3,2,1,0:T(8,128)(2,1)} %bitcast.15, ...), custom_call_target="tpu_custom_call" | custom-call | tf_op jit(solution)/shard_map/unpack/pallas_call | solution.py:1398
  591.3 0.6 constant_dynamic-slice_fusion.7
  591.9 0.6 constant_dynamic-slice_fusion.5
  592.5 0.6 constant_dynamic-slice_fusion.3
  593.1 0.6 constant_dynamic-slice_fusion.2
  593.7 0.6 constant_dynamic-slice_fusion
  594.3 3.1 copy.46
  (22 shorter events, 0.5 us)
Async XLA Ops:
  0.7 204.2 %copy-start = (bf16[2,512,1024]{2,1,0:T(8,128)(2,1)S(1)}, bf16[2,512,1024]{2,1,0:T(8,128)(2,1)}, u32[]{:S(2)}) copy-start(bf16[2,512,1024]{2,1,0:T(8,128)(2,1)} %param.20) | copy-start | bytes 6291460
  205.9 370.3 %copy-start.2 = (bf16[2,16,32,1024]{3,2,1,0:T(8,128)(2,1)S(1)}, bf16[2,16,32,1024]{3,2,1,0:T(8,128)(2,1)}, u32[]{:S(2)}) copy-start(bf16[2,16,32,1024]{3,2,1,0:T(8,128)(2,1)} %get-tuple-element.60) | copy-start | bytes 6291460
  577.8 13.4 %copy-start.3 = (f32[12,1024]{1,0:T(8,128)S(1)}, f32[12,1024]{1,0:T(8,128)}, u32[]{:S(2)}) copy-start(f32[12,1024]{1,0:T(8,128)} %get-tuple-element.97) | copy-start | bytes 147460
  577.8 19.6 %copy-start.1 = (bf16[2,512,1024]{2,1,0:T(8,128)(2,1)S(1)}, bf16[2,512,1024]{2,1,0:T(8,128)(2,1)}, u32[]{:S(2)}) copy-start(bf16[2,512,1024]{2,1,0:T(8,128)(2,1)} %param.20) | copy-start | bytes 6291460
